TPU v7x, 128 devices: a whole 4x4x4 slice. The times are simulated.
128 devices in a mesh: slot: 32 (over x, z, y_hi), dp: 4 (over y_lo, core).
Axes of the slice: x: 4, y: 4 (y_hi: 2, y_lo: 2; y = y_hi * 2 + y_lo), z: 4, core: 2. Of those that a mesh axis runs over, the one named last changes fastest.
Arguments:
- tokens: bfloat16 [12, 4096, 1024], P('dp', 'slot'), may hold values from -6 to 6
- slot_keys: bfloat16 [1024, 1024], P(None, 'slot'), may hold values from -1.5 to 1.5
- expert_in: bfloat16 [128, 1024, 4096], P('slot', None, 'dp'), may hold values from -0.5 to 0.5
- expert_out: bfloat16 [128, 4096, 1024], P('slot', 'dp'), may hold values from -0.1875 to 0.1875
Outputs:
- combined: bfloat16 [12, 4096, 1024], P('dp', 'slot')
All inputs are finite; a program needn't handle non-finite values.
Results may differ from a plain program's by a relative error of at most 0.0085.
Values may be sent and summed in bfloat16 or wider, within the bound.
No kernel may reach another device: no remote copies, remote signals or barrier semaphores. Data moves between devices by JAX's collectives and lax.ppermute only.
A program may use at most 128 MiB of HBM per device.

v0:
```python
import functools

import jax
import jax.numpy as jnp
from jax import lax
from jax.experimental import pallas as pl
from jax.experimental.pallas import tpu as pltpu
from jax.sharding import Mesh
from jax.sharding import PartitionSpec as P


X, Z, Y = "slot_0", "slot_1", "slot_2"
SLOT = (X, Z, Y)
OWNERS = (Z, Y)
LANES = 128
ROOM = 16 * 1024 * 1024
VMEM = pl.BlockSpec(memory_space=pltpu.VMEM)


def ahead(array, axis, step):
    size = lax.axis_size(axis)
    return lax.ppermute(array, axis, [((i + step) % size, i) for i in range(size)])


def all_to_all(array, axis):
    return lax.all_to_all(array, axis, split_axis=0, concat_axis=0, tiled=True)


def to_everyone(array, axis):
    copies = jnp.broadcast_to(array, (lax.axis_size(axis), *array.shape))
    return all_to_all(copies, axis)


def dispatch_kernel(keys, *refs):
    *blocks, message, logits, row_stats = refs
    owners, own_slots, features = keys.shape
    slots = owners * own_slots
    positions = blocks[0].shape[0]
    columns = keys[...].reshape(slots, features)
    for r, block in enumerate(blocks):
        logits[:, r * positions : (r + 1) * positions] = lax.dot_general(
            columns, block[...], (((1,), (1,)), ((), ())), preferred_element_type=jnp.float32
        )
    values = logits[...]
    row_top = jnp.max(values, axis=0, keepdims=True)
    row_stats[0:1] = row_top
    row_stats[1:2] = jnp.sum(jnp.exp(values - row_top), axis=0, keepdims=True)
    top = jnp.max(values, axis=1, keepdims=True).astype(jnp.bfloat16).astype(jnp.float32)
    raised = jnp.exp(values - top)
    rest = jnp.sum(raised, axis=1, keepdims=True)
    lane = lax.broadcasted_iota(jnp.int32, (slots, LANES), 1)
    stats = jnp.where(lane == 0, top, 0.0)
    for k in (1, 2, 3):
        piece = rest.astype(jnp.bfloat16).astype(jnp.float32)
        stats = jnp.where(lane == k, piece, stats)
        rest = rest - piece
    message[:, :, features:] = stats.astype(jnp.bfloat16).reshape(owners, own_slots, LANES)
    weights = raised.astype(jnp.bfloat16)
    sums = None
    for r, block in enumerate(blocks):
        part = jnp.dot(
            weights[:, r * positions : (r + 1) * positions],
            block[...],
            preferred_element_type=jnp.float32,
        )
        sums = part if sums is None else sums + part
    message[:, :, :features] = sums.astype(jnp.bfloat16).reshape(owners, own_slots, features)


def dispatch(keys, blocks):
    owners, own_slots, features = keys.shape
    slots, positions = owners * own_slots, len(blocks) * blocks[0].shape[0]
    return pl.pallas_call(
        dispatch_kernel,
        out_shape=(
            jax.ShapeDtypeStruct((owners, own_slots, features + LANES), jnp.bfloat16),
            jax.ShapeDtypeStruct((slots, positions), jnp.float32),
            jax.ShapeDtypeStruct((2, positions), jnp.float32),
        ),
        in_specs=[VMEM] * (1 + len(blocks)),
        out_specs=(VMEM,) * 3,
        cost_estimate=pl.CostEstimate(
            flops=4 * slots * positions * features,
            bytes_accessed=4 * slots * features,
            transcendentals=2 * slots * positions,
        ),
        compiler_params=pltpu.CompilerParams(vmem_limit_bytes=ROOM),
        name="dispatch",
    )(keys, *blocks)


def merge_kernel(*refs):
    *arrived, inputs = refs
    features = inputs.shape[2]
    for b, pieces in enumerate(arrived):
        owners = pieces.shape[0]
        tops, totals = [], []
        for k in range(owners):
            stats = pieces[k, :, features:].astype(jnp.float32)
            tops.append(stats[:, 0:1])
            totals.append(stats[:, 1:2] + stats[:, 2:3] + stats[:, 3:4])
        peak = functools.reduce(jnp.maximum, tops)
        scales = [jnp.exp(top - peak) for top in tops]
        whole = sum(scale * total for scale, total in zip(scales, totals))
        summed = sum(
            (scales[k] / whole) * pieces[k, :, :features].astype(jnp.float32)
            for k in range(owners)
        )
        inputs[b] = summed.astype(jnp.bfloat16)


def merge(arrived):
    _, own_slots, width = arrived[0].shape
    shape = (len(arrived), own_slots, width - LANES)
    return pl.pallas_call(
        merge_kernel,
        out_shape=jax.ShapeDtypeStruct(shape, jnp.bfloat16),
        in_specs=[VMEM] * len(arrived),
        out_specs=VMEM,
        cost_estimate=pl.CostEstimate(
            flops=1000000, bytes_accessed=2 * len(arrived) * arrived[0].size, transcendentals=0
        ),
        compiler_params=pltpu.CompilerParams(vmem_limit_bytes=ROOM),
        name="merge",
    )(*arrived)


def combine_kernel(logits, own_stats, first, second, third, everyone, own, right, far, left):
    positions = own.shape[0]
    owners, own_slots, features = everyone.shape
    stats = [own_stats[...], first[...], second[...], third[...]]
    for k in (1, 2, 3):
        cut = 4 * positions - k * positions
        stats[k] = jnp.concatenate([stats[k][:, cut:], stats[k][:, :cut]], axis=1)
    highest = functools.reduce(jnp.maximum, [s[0:1] for s in stats])
    whole = sum(s[1:2] * jnp.exp(s[0:1] - highest) for s in stats)
    mix = (jnp.exp(logits[...] - highest) / whole).astype(jnp.bfloat16)
    outputs = everyone[...].reshape(owners * own_slots, features)
    for r, out in enumerate((own, right, far, left)):
        out[...] = lax.dot_general(
            mix[:, r * positions : (r + 1) * positions],
            outputs,
            (((0,), (0,)), ((), ())),
            preferred_element_type=jnp.float32,
        ).astype(out.dtype)


def combine(logits, own_stats, other_stats, everyone):
    slots, width = logits.shape
    features = everyone.shape[2]
    shape = (width // 4, features)
    return pl.pallas_call(
        combine_kernel,
        out_shape=(
            jax.ShapeDtypeStruct(shape, jnp.float32),
            jax.ShapeDtypeStruct(shape, jnp.float32),
            jax.ShapeDtypeStruct(shape, jnp.bfloat16),
            jax.ShapeDtypeStruct(shape, jnp.float32),
        ),
        in_specs=[VMEM] * 6,
        out_specs=(VMEM,) * 4,
        cost_estimate=pl.CostEstimate(
            flops=2 * slots * width * features,
            bytes_accessed=4 * slots * width,
            transcendentals=slots * width,
        ),
        compiler_params=pltpu.CompilerParams(vmem_limit_bytes=ROOM),
        name="combine",
    )(logits, own_stats, *other_stats, everyone)


def shards(tokens, slot_keys, expert_in, expert_out):
    images, positions, features = tokens.shape
    own_slots = slot_keys.shape[1]
    experts = expert_in.shape[0]
    per_expert = own_slots // experts
    ranks = lax.axis_size("dp")
    mid = positions // 2

    keys = to_everyone(slot_keys.T, OWNERS)
    arrived, logits, row_stats = [], [], []
    for b in range(images):
        own = tokens[b]
        right = ahead(own, X, 1)
        left = ahead(own, X, 3)
        if b % 3 == 0:
            far = [ahead(right, X, 1)]
        elif b % 3 == 1:
            far = [ahead(left, X, 3)]
        else:
            far = [ahead(right[:mid], X, 1), ahead(left[mid:], X, 3)]
            far = [jnp.concatenate(far, axis=0)]
        message, values, stats = dispatch(keys, [own, right, *far, left])
        arrived.append(all_to_all(message, OWNERS))
        logits.append(values)
        row_stats.append(stats)
    joint = jnp.stack(row_stats)
    other_stats = [ahead(joint, X, k) for k in (1, 2, 3)]
    slot_inputs = merge(arrived)

    rows = lax.all_gather(slot_inputs, "dp", axis=0, tiled=True)
    rows = rows.reshape(ranks * images, experts, per_expert, features)
    rows = rows.transpose(1, 0, 2, 3).reshape(experts, -1, features)
    hidden = jnp.einsum("erd,edf->erf", rows, expert_in, preferred_element_type=jnp.float32)
    hidden = jax.nn.gelu(hidden, approximate=True).astype(jnp.bfloat16)
    result = jnp.einsum("erf,efd->erd", hidden, expert_out, preferred_element_type=jnp.float32)
    result = result.astype(jnp.bfloat16).reshape(experts, ranks, images, per_expert, features)
    result = result.transpose(1, 2, 0, 3, 4).reshape(ranks, images * own_slots, features)
    result = all_to_all(result, "dp")
    outputs = jnp.sum(result.astype(jnp.float32), axis=0).astype(jnp.bfloat16)
    outputs = outputs.reshape(images, own_slots, features)

    finished = []
    for b in range(images):
        everyone = to_everyone(outputs[b], OWNERS)
        own, right, far, left = combine(
            logits[b], row_stats[b], [o[b] for o in other_stats], everyone
        )
        if b % 3 == 0:
            right = right + ahead(far, X, 3).astype(jnp.float32)
        elif b % 3 == 1:
            left = left + ahead(far, X, 1).astype(jnp.float32)
        else:
            low = ahead(far[:mid], X, 3).astype(jnp.float32)
            high = ahead(far[mid:], X, 1).astype(jnp.float32)
            right = right + jnp.pad(low, ((0, mid), (0, 0)))
            left = left + jnp.pad(high, ((mid, 0), (0, 0)))
        right = ahead(right.astype(jnp.bfloat16), X, 3).astype(jnp.float32)
        left = ahead(left.astype(jnp.bfloat16), X, 1).astype(jnp.float32)
        finished.append((own + right + left).astype(jnp.bfloat16))
    return jnp.stack(finished)


def solution(mesh):
    split = Mesh(mesh.devices.reshape(4, 4, 2, mesh.shape["dp"]), (X, Z, Y, "dp"))
    return jax.shard_map(
        shards,
        mesh=split,
        in_specs=(P("dp", SLOT, None), P(None, SLOT), P(SLOT, None, "dp"), P(SLOT, "dp", None)),
        out_specs=P("dp", SLOT, None),
        check_vma=False,
    )
```

profile of v0, /device:TPU:0, one launch (start us, length us, event | category | flops | bytes accessed | tf_op | source)
XLA Modules:
  0.0 184.6 jit_solution(2995948417820131728)
XLA Ops:
  0.0 1.2 slice_bitcast_fusion.2
  1.2 2.9 %collective-permute-start.6 = (bf16[128,1024]{1,0:T(8,128)(2,1)S(1)}, bf16[128,1024]{1,0:T(8,128)(2,1)S(1)}, u32[]{:S(2)}, u32[]{:S(2)}) collective-permute-start(bf16[128,1024]{1,0:T(8,128)(2,1)S(1)} %get-tuple-element.48.refs_0_), channel_id=1, source_target_pairs={{32,0},{64,32},{96,64},{0,96},{33,1},{65,33},{97,65},{1,97},{34,2}... | collective-permute-start | bytes 786440 | tf_op jit(solution)/shard_map/ppermute | solution.py:22
  4.1 0.9 broadcast_in_dim.12
  5.0 7.9 %all-to-all-start = ((bf16[8,32,1024]{2,1,0:T(8,128)(2,1)}), bf16[8,32,1024]{2,1,0:T(8,128)(2,1)S(1)}, u32[]{:S(2)}, u32[]{:S(2)}) async-start(bf16[8,32,1024]{2,1,0:T(8,128)(2,1)} %broadcast_in_dim.12), calls=%async_computation | async-start | bytes 1048576 | tf_op jit(solution)/shard_map/all_to_all | solution.py:26
  13.0 3.3 %collective-permute-start.7 = (bf16[64,1024]{1,0:T(8,128)(2,1)S(1)}, bf16[64,1024]{1,0:T(8,128)(2,1)S(1)}, u32[]{:S(2)}, u32[]{:S(2)}) collective-permute-start(bf16[64,1024]{1,0:T(8,128)(2,1)S(1)} %slice.79), channel_id=1, source_target_pairs={{32,0},{64,32},{96,64},{0,96},{33,1},{65,33},{97,65},{1,97},{34,2}... | collective-permute-start | bytes 393224 | tf_op jit(solution)/shard_map/ppermute | solution.py:22
  16.4 3.2 %collective-permute-start = (bf16[128,1024]{1,0:T(8,128)(2,1)S(1)}, bf16[128,1024]{1,0:T(8,128)(2,1)S(1)}, u32[]{:S(2)}, u32[]{:S(2)}) collective-permute-start(bf16[128,1024]{1,0:T(8,128)(2,1)S(1)} %get-tuple-element.47.refs_0_), channel_id=1, source_target_pairs={{32,0},{64,32},{96,64},{0,96},{33,1},{65,33},{97,65},{1,97},{34,2}... | collective-permute-start | bytes 786440 | tf_op jit(solution)/shard_map/ppermute | solution.py:22
  19.6 2.9 %collective-permute-done.9 = bf16[64,1024]{1,0:T(8,128)(2,1)S(1)} collective-permute-done((bf16[64,1024]{1,0:T(8,128)(2,1)S(1)}, bf16[64,1024]{1,0:T(8,128)(2,1)S(1)}, u32[]{:S(2)}, u32[]{:S(2)}) %collective-permute-start.9) | collective-permute-done | bytes 131104 | tf_op jit(solution)/shard_map/ppermute | solution.py:22
  22.6 1.7 all-to-all-done.keys
  24.2 2.3 %dispatch.5 = (bf16[8,32,1152]{2,1,0:T(8,128)(2,1)}, f32[256,512]{1,0:T(8,128)S(1)}, f32[2,512]{1,0:T(2,128)S(1)}) custom-call(bf16[8,32,1024]{2,1,0:T(8,128)(2,1)S(1)} %all-to-all-done.keys, bf16[128,1024]{1,0:T(8,128)(2,1)S(1)} %get-tuple-element.48.refs_0_, bf16[128,1024]{1,0:T(8,128)(2,1)S(1)} %collective-permute-done.6.refs_1_, ...), custom_call_target="tpu_custom_call" | custom-call | flops 536870912 | bytes 1048576 | tf_op jit(solution)/shard_map/dispatch/pallas_call | solution.py:73
  26.5 5.5 %all-to-all-start.3 = ((bf16[8,32,1152]{2,1,0:T(8,128)(2,1)}), bf16[8,32,1152]{2,1,0:T(8,128)(2,1)S(1)}, u32[]{:S(2)}, u32[]{:S(2)}) async-start(bf16[8,32,1152]{2,1,0:T(8,128)(2,1)} %get-tuple-element.32), calls=%async_computation.3 | async-start | bytes 1179648 | tf_op jit(solution)/shard_map/all_to_all | solution.py:26
  32.1 3.2 %collective-permute-start.1 = (bf16[128,1024]{1,0:T(8,128)(2,1)S(1)}, bf16[128,1024]{1,0:T(8,128)(2,1)S(1)}, u32[]{:S(2)}, u32[]{:S(2)}) collective-permute-start(bf16[128,1024]{1,0:T(8,128)(2,1)S(1)} %collective-permute-done.refs_1_), channel_id=1, source_target_pairs={{32,0},{64,32},{96,64},{0,96},{33,1},{65,33},{97,65},{1,97},{34,2}... | collective-permute-start | bytes 786440 | tf_op jit(solution)/shard_map/ppermute | solution.py:22
  35.3 6.0 %collective-permute-done.2.refs_3_ = bf16[128,1024]{1,0:T(8,128)(2,1)S(1)} collective-permute-done((bf16[128,1024]{1,0:T(8,128)(2,1)S(1)}, bf16[128,1024]{1,0:T(8,128)(2,1)S(1)}, u32[]{:S(2)}, u32[]{:S(2)}) %collective-permute-start.2) | collective-permute-done | bytes 262176 | tf_op jit(solution)/shard_map/ppermute | solution.py:22
  41.3 2.3 %dispatch.3 = (bf16[8,32,1152]{2,1,0:T(8,128)(2,1)}, f32[256,512]{1,0:T(8,128)S(1)}, f32[2,512]{1,0:T(2,128)S(1)}) custom-call(bf16[8,32,1024]{2,1,0:T(8,128)(2,1)S(1)} %all-to-all-done.keys, bf16[128,1024]{1,0:T(8,128)(2,1)S(1)} %get-tuple-element.47.refs_0_, bf16[128,1024]{1,0:T(8,128)(2,1)S(1)} %collective-permute-done.refs_1_, ...), custom_call_target="tpu_custom_call" | custom-call | flops 536870912 | bytes 1048576 | tf_op jit(solution)/shard_map/dispatch/pallas_call | solution.py:73
  44.4 6.9 %all-to-all-start.1 = ((bf16[8,32,1152]{2,1,0:T(8,128)(2,1)}), bf16[8,32,1152]{2,1,0:T(8,128)(2,1)S(1)}, u32[]{:S(2)}, u32[]{:S(2)}) async-start(bf16[8,32,1152]{2,1,0:T(8,128)(2,1)} %get-tuple-element.30), calls=%async_computation.1 | async-start | bytes 1179648 | tf_op jit(solution)/shard_map/all_to_all | solution.py:26
  51.3 1.9 %collective-permute-start.3 = (bf16[128,1024]{1,0:T(8,128)(2,1)S(1)}, bf16[128,1024]{1,0:T(8,128)(2,1)S(1)}, u32[]{:S(2)}, u32[]{:S(2)}) collective-permute-start(bf16[128,1024]{1,0:T(8,128)(2,1)S(1)} %get-tuple-element.49.refs_0_), channel_id=1, source_target_pairs={{32,0},{64,32},{96,64},{0,96},{33,1},{65,33},{97,65},{1,97},{34,2}... | collective-permute-start | bytes 786440 | tf_op jit(solution)/shard_map/ppermute | solution.py:22
  53.4 4.3 %collective-permute-done.3.refs_1_ = bf16[128,1024]{1,0:T(8,128)(2,1)S(1)} collective-permute-done((bf16[128,1024]{1,0:T(8,128)(2,1)S(1)}, bf16[128,1024]{1,0:T(8,128)(2,1)S(1)}, u32[]{:S(2)}, u32[]{:S(2)}) %collective-permute-start.3) | collective-permute-done | bytes 262176 | tf_op jit(solution)/shard_map/ppermute | solution.py:22
  57.7 3.1 %collective-permute-done.5.refs_2_ = bf16[128,1024]{1,0:T(8,128)(2,1)S(1)} collective-permute-done((bf16[128,1024]{1,0:T(8,128)(2,1)S(1)}, bf16[128,1024]{1,0:T(8,128)(2,1)S(1)}, u32[]{:S(2)}, u32[]{:S(2)}) %collective-permute-start.5) | collective-permute-done | bytes 262176 | tf_op jit(solution)/shard_map/ppermute | solution.py:22
  60.8 1.0 copy-done.7
  61.8 1.5 dispatch.4
  63.3 17.7 %all_to_all.40.refs_1_ = bf16[8,32,1152]{2,1,0:T(8,128)(2,1)S(1)} all-to-all(bf16[8,32,1152]{2,1,0:T(8,128)(2,1)S(1)} %get-tuple-element.31), channel_id=1, replica_groups=mesh['slot_0'=4,'slot_1'=4,'slot_2'=2,'dp'=4] {'slot_1','slot_2'}, dimensions={0} | all-to-all | bytes 1179648 | tf_op jit(solution)/shard_map/all_to_all | solution.py:26
  81.8 7.8 %all_gather.3 = bf16[12,32,1024]{2,1,0:T(8,128)(2,1)S(1)} all-gather(bf16[3,32,1024]{2,1,0:T(8,128)(2,1)S(1)} %merge.1), channel_id=1, replica_groups=mesh['slot_0'=4,'slot_1'=4,'slot_2'=2,'dp'=4] {'dp'}, dimensions={0}, use_global_device_ids=true | all-gather | bytes 983040 | tf_op jit(solution)/shard_map/all_gather | solution.py:201
  89.6 8.6 %convolution_convert_fusion = bf16[4,96,1024]{2,1,0:T(8,128)(2,1)S(1)} fusion(bf16[4,1024,1024]{2,1,0:T(8,128)(2,1)} %param.7, bf16[4,1024,1024]{2,1,0:T(8,128)(2,1)} %param.6, bf16[12,32,1024]{2,1,0:T(8,128)(2,1)S(1)} %all_gather.3), kind=kOutput, calls=%fused_computation.9 | convolution fusion | flops 1614544896 | bytes 18350080 | tf_op jit(solution)/shard_map/erf,efd->erd/dot_general | solution.py:206
  98.3 14.0 %all_to_all.41 = bf16[4,96,1024]{2,1,0:T(8,128)(2,1)S(1)} all-to-all(bf16[4,96,1024]{2,1,0:T(8,128)(2,1)S(1)} %bitcast.57), channel_id=1, replica_groups=mesh['slot_0'=4,'slot_1'=4,'slot_2'=2,'dp'=4] {'dp'}, dimensions={0} | all-to-all | bytes 1572864 | tf_op jit(solution)/shard_map/all_to_all | solution.py:26
  112.5 0.9 broadcast_in_dim.13
  113.4 3.7 %all-to-all-start.5 = ((bf16[8,32,1024]{2,1,0:T(8,128)(2,1)}), bf16[8,32,1024]{2,1,0:T(8,128)(2,1)S(1)}, u32[]{:S(2)}, u32[]{:S(2)}) async-start(bf16[8,32,1024]{2,1,0:T(8,128)(2,1)} %broadcast_in_dim.13), calls=%async_computation.5 | async-start | bytes 1048576 | tf_op jit(solution)/shard_map/all_to_all | solution.py:26
  117.2 11.2 %all-to-all-done.5.everyone = bf16[8,32,1024]{2,1,0:T(8,128)(2,1)S(1)} async-done(((bf16[8,32,1024]{2,1,0:T(8,128)(2,1)}), bf16[8,32,1024]{2,1,0:T(8,128)(2,1)S(1)}, u32[]{:S(2)}, u32[]{:S(2)}) %all-to-all-start.5) | async-done | bytes 524320 | tf_op jit(solution)/shard_map/all_to_all | solution.py:26
  128.3 0.9 broadcast_in_dim.15
  129.2 3.5 %all-to-all-start.7 = ((bf16[8,32,1024]{2,1,0:T(8,128)(2,1)}), bf16[8,32,1024]{2,1,0:T(8,128)(2,1)S(1)}, u32[]{:S(2)}, u32[]{:S(2)}) async-start(bf16[8,32,1024]{2,1,0:T(8,128)(2,1)} %broadcast_in_dim.15), calls=%async_computation.7 | async-start | bytes 1048576 | tf_op jit(solution)/shard_map/all_to_all | solution.py:26
  132.8 1.6 collective-permute-start.10
  134.4 3.6 %collective-permute-done.11 = f32[3,2,512]{2,1,0:T(2,128)S(1)} collective-permute-done((f32[3,2,512]{2,1,0:T(2,128)S(1)}, f32[3,2,512]{2,1,0:T(2,128)S(1)}, u32[]{:S(2)}, u32[]{:S(2)}) %collective-permute-start.11) | collective-permute-done | bytes 12320 | tf_op jit(solution)/shard_map/ppermute | solution.py:22
  137.9 5.3 %all-to-all-done.7.everyone = bf16[8,32,1024]{2,1,0:T(8,128)(2,1)S(1)} async-done(((bf16[8,32,1024]{2,1,0:T(8,128)(2,1)}), bf16[8,32,1024]{2,1,0:T(8,128)(2,1)S(1)}, u32[]{:S(2)}, u32[]{:S(2)}) %all-to-all-start.7) | async-done | bytes 524320 | tf_op jit(solution)/shard_map/all_to_all | solution.py:26
  143.2 0.9 broadcast_in_dim.14
  144.1 3.5 %all-to-all-start.6 = ((bf16[8,32,1024]{2,1,0:T(8,128)(2,1)}), bf16[8,32,1024]{2,1,0:T(8,128)(2,1)S(1)}, u32[]{:S(2)}, u32[]{:S(2)}) async-start(bf16[8,32,1024]{2,1,0:T(8,128)(2,1)} %broadcast_in_dim.14), calls=%async_computation.6 | async-start | bytes 1048576 | tf_op jit(solution)/shard_map/all_to_all | solution.py:26
  149.0 1.0 copy-done.1
  151.4 3.1 %collective-permute-start.15 = (bf16[128,1024]{1,0:T(8,128)(2,1)S(1)}, bf16[128,1024]{1,0:T(8,128)(2,1)S(1)}, u32[]{:S(2)}, u32[]{:S(2)}) collective-permute-start(bf16[128,1024]{1,0:T(8,128)(2,1)S(1)} %convert_element_type.70), channel_id=1, source_target_pairs={{32,0},{64,32},{96,64},{0,96},{33,1},{65,33},{97,65},{1,97},{34,2}... | collective-permute-start | bytes 786440 | tf_op jit(solution)/shard_map/ppermute | solution.py:22
  154.5 3.2 %all-to-all-done.6.everyone = bf16[8,32,1024]{2,1,0:T(8,128)(2,1)S(1)} async-done(((bf16[8,32,1024]{2,1,0:T(8,128)(2,1)}), bf16[8,32,1024]{2,1,0:T(8,128)(2,1)S(1)}, u32[]{:S(2)}, u32[]{:S(2)}) %all-to-all-start.6) | async-done | bytes 524320 | tf_op jit(solution)/shard_map/all_to_all | solution.py:26
  158.4 2.1 %collective-permute-start.16 = (bf16[128,1024]{1,0:T(8,128)(2,1)S(1)}, bf16[128,1024]{1,0:T(8,128)(2,1)S(1)}, u32[]{:S(2)}, u32[]{:S(2)}) collective-permute-start(bf16[128,1024]{1,0:T(8,128)(2,1)S(1)} %convert_element_type.73), channel_id=1, source_target_pairs={{96,0},{0,32},{32,64},{64,96},{97,1},{1,33},{33,65},{65,97},{98,2}... | collective-permute-start | bytes 786440 | tf_op jit(solution)/shard_map/ppermute | solution.py:22
  160.5 1.2 collective-permute-start.21
  161.7 0.9 add_convert_fusion.2
  162.7 3.8 %collective-permute-done.21 = bf16[64,1024]{1,0:T(8,128)(2,1)S(1)} collective-permute-done((bf16[64,1024]{1,0:T(8,128)(2,1)}, bf16[64,1024]{1,0:T(8,128)(2,1)S(1)}, u32[]{:S(2)}, u32[]{:S(2)}) %collective-permute-start.21) | collective-permute-done | bytes 131104 | tf_op jit(solution)/shard_map/ppermute | solution.py:22
  166.5 1.0 collective-permute-start.20
  167.6 2.6 %collective-permute-start.22 = (bf16[128,1024]{1,0:T(8,128)(2,1)S(1)}, bf16[128,1024]{1,0:T(8,128)(2,1)S(1)}, u32[]{:S(2)}, u32[]{:S(2)}) collective-permute-start(bf16[128,1024]{1,0:T(8,128)(2,1)S(1)} %add_convert_fusion.1), channel_id=1, source_target_pairs={{32,0},{64,32},{96,64},{0,96},{33,1},{65,33},{97,65},{1,97},{34,2}... | collective-permute-start | bytes 786440 | tf_op jit(solution)/shard_map/ppermute | solution.py:22
  170.2 1.0 add_convert_fusion.6
  171.4 5.8 %collective-permute-done.20 = bf16[128,1024]{1,0:T(8,128)(2,1)S(1)} collective-permute-done((bf16[128,1024]{1,0:T(8,128)(2,1)S(1)}, bf16[128,1024]{1,0:T(8,128)(2,1)S(1)}, u32[]{:S(2)}, u32[]{:S(2)}) %collective-permute-start.20) | collective-permute-done | bytes 262176 | tf_op jit(solution)/shard_map/ppermute | solution.py:22
  177.1 0.8 collective-permute-start.18
  178.1 1.9 %collective-permute-done.14 = bf16[128,1024]{1,0:T(8,128)(2,1)S(1)} collective-permute-done((bf16[128,1024]{1,0:T(8,128)(2,1)S(1)}, bf16[128,1024]{1,0:T(8,128)(2,1)S(1)}, u32[]{:S(2)}, u32[]{:S(2)}) %collective-permute-start.14) | collective-permute-done | bytes 262176 | tf_op jit(solution)/shard_map/ppermute | solution.py:22
  180.2 3.4 %collective-permute-done.18 = bf16[128,1024]{1,0:T(8,128)(2,1)S(1)} collective-permute-done((bf16[128,1024]{1,0:T(8,128)(2,1)S(1)}, bf16[128,1024]{1,0:T(8,128)(2,1)S(1)}, u32[]{:S(2)}, u32[]{:S(2)}) %collective-permute-start.18) | collective-permute-done | bytes 262176 | tf_op jit(solution)/shard_map/ppermute | solution.py:22
  183.6 1.0 pad_maximum_fusion
  (69 shorter events, 6.1 us)
Async XLA Ops:
  0.0 4.1 %copy-start.10 = (bf16[1024,32]{0,1:T(8,128)(2,1)S(1)}, bf16[1024,32]{0,1:T(8,128)(2,1)}, u32[]{:S(2)}) copy-start(bf16[1024,32]{0,1:T(8,128)(2,1)} %param.5) | copy-start | bytes 196612
  1.2 11.7 %collective-permute-start.6 = (bf16[128,1024]{1,0:T(8,128)(2,1)S(1)}, bf16[128,1024]{1,0:T(8,128)(2,1)S(1)}, u32[]{:S(2)}, u32[]{:S(2)}) collective-permute-start(bf16[128,1024]{1,0:T(8,128)(2,1)S(1)} %get-tuple-element.48.refs_0_), channel_id=1, source_target_pairs={{32,0},{64,32},{96,64},{0,96},{33,1},{65,33},{97,65},{1,97},{34,2}... | collective-permute-start | bytes 786440 | tf_op jit(solution)/shard_map/ppermute | solution.py:22
  4.1 12.1 %collective-permute-start.8 = (bf16[128,1024]{1,0:T(8,128)(2,1)S(1)}, bf16[128,1024]{1,0:T(8,128)(2,1)S(1)}, u32[]{:S(2)}, u32[]{:S(2)}) collective-permute-start(bf16[128,1024]{1,0:T(8,128)(2,1)S(1)} %get-tuple-element.48.refs_0_), channel_id=1, source_target_pairs={{96,0},{0,32},{32,64},{64,96},{97,1},{1,33},{33,65},{65,97},{98,2}... | collective-permute-start | bytes 786440 | tf_op jit(solution)/shard_map/ppermute | solution.py:22
  5.0 19.2 %all-to-all-start = ((bf16[8,32,1024]{2,1,0:T(8,128)(2,1)}), bf16[8,32,1024]{2,1,0:T(8,128)(2,1)S(1)}, u32[]{:S(2)}, u32[]{:S(2)}) async-start(bf16[8,32,1024]{2,1,0:T(8,128)(2,1)} %broadcast_in_dim.12), calls=%async_computation | async-start | bytes 1048576 | tf_op jit(solution)/shard_map/all_to_all | solution.py:26
  13.0 6.6 %collective-permute-start.7 = (bf16[64,1024]{1,0:T(8,128)(2,1)S(1)}, bf16[64,1024]{1,0:T(8,128)(2,1)S(1)}, u32[]{:S(2)}, u32[]{:S(2)}) collective-permute-start(bf16[64,1024]{1,0:T(8,128)(2,1)S(1)} %slice.79), channel_id=1, source_target_pairs={{32,0},{64,32},{96,64},{0,96},{33,1},{65,33},{97,65},{1,97},{34,2}... | collective-permute-start | bytes 393224 | tf_op jit(solution)/shard_map/ppermute | solution.py:22
  16.3 6.2 %collective-permute-start.9 = (bf16[64,1024]{1,0:T(8,128)(2,1)S(1)}, bf16[64,1024]{1,0:T(8,128)(2,1)S(1)}, u32[]{:S(2)}, u32[]{:S(2)}) collective-permute-start(bf16[64,1024]{1,0:T(8,128)(2,1)S(1)} %slice.80), channel_id=1, source_target_pairs={{96,0},{0,32},{32,64},{64,96},{97,1},{1,33},{33,65},{65,97},{98,2}... | collective-permute-start | bytes 393224 | tf_op jit(solution)/shard_map/ppermute | solution.py:22
  16.4 15.7 %collective-permute-start = (bf16[128,1024]{1,0:T(8,128)(2,1)S(1)}, bf16[128,1024]{1,0:T(8,128)(2,1)S(1)}, u32[]{:S(2)}, u32[]{:S(2)}) collective-permute-start(bf16[128,1024]{1,0:T(8,128)(2,1)S(1)} %get-tuple-element.47.refs_0_), channel_id=1, source_target_pairs={{32,0},{64,32},{96,64},{0,96},{33,1},{65,33},{97,65},{1,97},{34,2}... | collective-permute-start | bytes 786440 | tf_op jit(solution)/shard_map/ppermute | solution.py:22
  24.2 17.1 %copy-start.6 = (bf16[8,32,1024]{2,1,0:T(8,128)(2,1)}, bf16[8,32,1024]{2,1,0:T(8,128)(2,1)S(1)}, u32[]{:S(2)}) copy-start(bf16[8,32,1024]{2,1,0:T(8,128)(2,1)S(1)} %all-to-all-done.keys) | copy-start | bytes 1572868
  26.5 17.9 %all-to-all-start.3 = ((bf16[8,32,1152]{2,1,0:T(8,128)(2,1)}), bf16[8,32,1152]{2,1,0:T(8,128)(2,1)S(1)}, u32[]{:S(2)}, u32[]{:S(2)}) async-start(bf16[8,32,1152]{2,1,0:T(8,128)(2,1)} %get-tuple-element.32), calls=%async_computation.3 | async-start | bytes 1179648 | tf_op jit(solution)/shard_map/all_to_all | solution.py:26
  32.1 9.2 %collective-permute-start.2 = (bf16[128,1024]{1,0:T(8,128)(2,1)S(1)}, bf16[128,1024]{1,0:T(8,128)(2,1)S(1)}, u32[]{:S(2)}, u32[]{:S(2)}) collective-permute-start(bf16[128,1024]{1,0:T(8,128)(2,1)S(1)} %get-tuple-element.47.refs_0_), channel_id=1, source_target_pairs={{96,0},{0,32},{32,64},{64,96},{97,1},{1,33},{33,65},{65,97},{98,2}... | collective-permute-start | bytes 786440 | tf_op jit(solution)/shard_map/ppermute | solution.py:22
  32.1 9.2 %collective-permute-start.1 = (bf16[128,1024]{1,0:T(8,128)(2,1)S(1)}, bf16[128,1024]{1,0:T(8,128)(2,1)S(1)}, u32[]{:S(2)}, u32[]{:S(2)}) collective-permute-start(bf16[128,1024]{1,0:T(8,128)(2,1)S(1)} %collective-permute-done.refs_1_), channel_id=1, source_target_pairs={{32,0},{64,32},{96,64},{0,96},{33,1},{65,33},{97,65},{1,97},{34,2}... | collective-permute-start | bytes 786440 | tf_op jit(solution)/shard_map/ppermute | solution.py:22
  35.3 17.9 %collective-permute-start.4 = (bf16[128,1024]{1,0:T(8,128)(2,1)S(1)}, bf16[128,1024]{1,0:T(8,128)(2,1)S(1)}, u32[]{:S(2)}, u32[]{:S(2)}) collective-permute-start(bf16[128,1024]{1,0:T(8,128)(2,1)S(1)} %get-tuple-element.49.refs_0_), channel_id=1, source_target_pairs={{96,0},{0,32},{32,64},{64,96},{97,1},{1,33},{33,65},{65,97},{98,2}... | collective-permute-start | bytes 786440 | tf_op jit(solution)/shard_map/ppermute | solution.py:22
  43.6 0.8 copy-start
  44.4 18.9 %all-to-all-start.1 = ((bf16[8,32,1152]{2,1,0:T(8,128)(2,1)}), bf16[8,32,1152]{2,1,0:T(8,128)(2,1)S(1)}, u32[]{:S(2)}, u32[]{:S(2)}) async-start(bf16[8,32,1152]{2,1,0:T(8,128)(2,1)} %get-tuple-element.30), calls=%async_computation.1 | async-start | bytes 1179648 | tf_op jit(solution)/shard_map/all_to_all | solution.py:26
  51.3 6.4 %collective-permute-start.3 = (bf16[128,1024]{1,0:T(8,128)(2,1)S(1)}, bf16[128,1024]{1,0:T(8,128)(2,1)S(1)}, u32[]{:S(2)}, u32[]{:S(2)}) collective-permute-start(bf16[128,1024]{1,0:T(8,128)(2,1)S(1)} %get-tuple-element.49.refs_0_), channel_id=1, source_target_pairs={{32,0},{64,32},{96,64},{0,96},{33,1},{65,33},{97,65},{1,97},{34,2}... | collective-permute-start | bytes 786440 | tf_op jit(solution)/shard_map/ppermute | solution.py:22
  53.2 7.6 %collective-permute-start.5 = (bf16[128,1024]{1,0:T(8,128)(2,1)S(1)}, bf16[128,1024]{1,0:T(8,128)(2,1)S(1)}, u32[]{:S(2)}, u32[]{:S(2)}) collective-permute-start(bf16[128,1024]{1,0:T(8,128)(2,1)S(1)} %collective-permute-done.4.refs_3_), channel_id=1, source_target_pairs={{96,0},{0,32},{32,64},{64,96},{97,1},{1,33},{33,65},{65,97},{98,2}... | collective-permute-start | bytes 786440 | tf_op jit(solution)/shard_map/ppermute | solution.py:22
  60.8 1.0 copy-start.7
  63.3 18.5 %copy-start.2 = (f32[256,512]{1,0:T(8,128)}, f32[256,512]{1,0:T(8,128)S(1)}, u32[]{:S(2)}) copy-start(f32[256,512]{1,0:T(8,128)S(1)} %get-tuple-element.37.logits) | copy-start | bytes 1572868
  113.4 14.9 %all-to-all-start.5 = ((bf16[8,32,1024]{2,1,0:T(8,128)(2,1)}), bf16[8,32,1024]{2,1,0:T(8,128)(2,1)S(1)}, u32[]{:S(2)}, u32[]{:S(2)}) async-start(bf16[8,32,1024]{2,1,0:T(8,128)(2,1)} %broadcast_in_dim.13), calls=%async_computation.5 | async-start | bytes 1048576 | tf_op jit(solution)/shard_map/all_to_all | solution.py:26
  117.1 17.3 %collective-permute-start.12 = (f32[3,2,512]{2,1,0:T(2,128)S(1)}, f32[3,2,512]{2,1,0:T(2,128)S(1)}, u32[]{:S(2)}, u32[]{:S(2)}) collective-permute-start(f32[3,2,512]{2,1,0:T(2,128)S(1)} %pad_maximum_fusion.2), channel_id=1, source_target_pairs={{96,0},{0,32},{32,64},{64,96},{97,1},{1,33},{33,65},{65,97},{98,2}... | collective-permute-start | bytes 36872 | tf_op jit(solution)/shard_map/ppermute | solution.py:22
  129.2 14.1 %all-to-all-start.7 = ((bf16[8,32,1024]{2,1,0:T(8,128)(2,1)}), bf16[8,32,1024]{2,1,0:T(8,128)(2,1)S(1)}, u32[]{:S(2)}, u32[]{:S(2)}) async-start(bf16[8,32,1024]{2,1,0:T(8,128)(2,1)} %broadcast_in_dim.15), calls=%async_computation.7 | async-start | bytes 1048576 | tf_op jit(solution)/shard_map/all_to_all | solution.py:26
  132.7 5.3 %collective-permute-start.11 = (f32[3,2,512]{2,1,0:T(2,128)S(1)}, f32[3,2,512]{2,1,0:T(2,128)S(1)}, u32[]{:S(2)}, u32[]{:S(2)}) collective-permute-start(f32[3,2,512]{2,1,0:T(2,128)S(1)} %pad_maximum_fusion.2), channel_id=1, source_target_pairs={{64,0},{96,32},{0,64},{32,96},{65,1},{97,33},{1,65},{33,97},{66,2}... | collective-permute-start | bytes 36872 | tf_op jit(solution)/shard_map/ppermute | solution.py:22
  132.8 14.8 %collective-permute-start.10 = (f32[3,2,512]{2,1,0:T(2,128)S(1)}, f32[3,2,512]{2,1,0:T(2,128)S(1)}, u32[]{:S(2)}, u32[]{:S(2)}) collective-permute-start(f32[3,2,512]{2,1,0:T(2,128)S(1)} %pad_maximum_fusion.2), channel_id=1, source_target_pairs={{32,0},{64,32},{96,64},{0,96},{33,1},{65,33},{97,65},{1,97},{34,2}... | collective-permute-start | bytes 36872 | tf_op jit(solution)/shard_map/ppermute | solution.py:22
  144.1 13.6 %all-to-all-start.6 = ((bf16[8,32,1024]{2,1,0:T(8,128)(2,1)}), bf16[8,32,1024]{2,1,0:T(8,128)(2,1)S(1)}, u32[]{:S(2)}, u32[]{:S(2)}) async-start(bf16[8,32,1024]{2,1,0:T(8,128)(2,1)} %broadcast_in_dim.14), calls=%async_computation.6 | async-start | bytes 1048576 | tf_op jit(solution)/shard_map/all_to_all | solution.py:26
  148.1 0.9 copy-start.4
  148.2 9.6 %copy-start.3 = (f32[256,512]{1,0:T(8,128)S(1)}, f32[256,512]{1,0:T(8,128)}, u32[]{:S(2)}) copy-start(f32[256,512]{1,0:T(8,128)} %copy-done.2) | copy-start | bytes 1572868
  148.9 11.6 %collective-permute-start.19 = (bf16[64,1024]{1,0:T(8,128)(2,1)}, bf16[64,1024]{1,0:T(8,128)(2,1)}, u32[]{:S(2)}, u32[]{:S(2)}) collective-permute-start(bf16[64,1024]{1,0:T(8,128)(2,1)} %get-tuple-element.50), channel_id=1, source_target_pairs={{96,0},{0,32},{32,64},{64,96},{97,1},{1,33},{33,65},{65,97},{98,2}... | collective-permute-start | bytes 393224 | tf_op jit(solution)/shard_map/ppermute | solution.py:22
  149.0 1.0 copy-start.1
  150.6 0.8 copy-start.8
  150.6 17.0 %collective-permute-start.13 = (bf16[128,1024]{1,0:T(8,128)(2,1)S(1)}, bf16[128,1024]{1,0:T(8,128)(2,1)}, u32[]{:S(2)}, u32[]{:S(2)}) collective-permute-start(bf16[128,1024]{1,0:T(8,128)(2,1)S(1)} %get-tuple-element.35), channel_id=1, source_target_pairs={{96,0},{0,32},{32,64},{64,96},{97,1},{1,33},{33,65},{65,97},{98,2}... | collective-permute-start | bytes 786440 | tf_op jit(solution)/shard_map/ppermute | solution.py:22
  151.4 26.7 %collective-permute-start.15 = (bf16[128,1024]{1,0:T(8,128)(2,1)S(1)}, bf16[128,1024]{1,0:T(8,128)(2,1)S(1)}, u32[]{:S(2)}, u32[]{:S(2)}) collective-permute-start(bf16[128,1024]{1,0:T(8,128)(2,1)S(1)} %convert_element_type.70), channel_id=1, source_target_pairs={{32,0},{64,32},{96,64},{0,96},{33,1},{65,33},{97,65},{1,97},{34,2}... | collective-permute-start | bytes 786440 | tf_op jit(solution)/shard_map/ppermute | solution.py:22
  158.3 11.9 %copy-start.9 = (f32[128,1024]{1,0:T(8,128)S(1)}, f32[128,1024]{1,0:T(8,128)}, u32[]{:S(2)}) copy-start(f32[128,1024]{1,0:T(8,128)} %copy-done.8) | copy-start | bytes 1572868
  158.3 13.0 %collective-permute-start.17 = (bf16[128,1024]{1,0:T(8,128)(2,1)S(1)}, bf16[128,1024]{1,0:T(8,128)(2,1)S(1)}, u32[]{:S(2)}, u32[]{:S(2)}) collective-permute-start(bf16[128,1024]{1,0:T(8,128)(2,1)S(1)} %get-tuple-element.41), channel_id=1, source_target_pairs={{32,0},{64,32},{96,64},{0,96},{33,1},{65,33},{97,65},{1,97},{34,2}... | collective-permute-start | bytes 786440 | tf_op jit(solution)/shard_map/ppermute | solution.py:22
  158.4 21.8 %collective-permute-start.16 = (bf16[128,1024]{1,0:T(8,128)(2,1)S(1)}, bf16[128,1024]{1,0:T(8,128)(2,1)S(1)}, u32[]{:S(2)}, u32[]{:S(2)}) collective-permute-start(bf16[128,1024]{1,0:T(8,128)(2,1)S(1)} %convert_element_type.73), channel_id=1, source_target_pairs={{96,0},{0,32},{32,64},{64,96},{97,1},{1,33},{33,65},{65,97},{98,2}... | collective-permute-start | bytes 786440 | tf_op jit(solution)/shard_map/ppermute | solution.py:22
  160.5 6.0 %collective-permute-start.21 = (bf16[64,1024]{1,0:T(8,128)(2,1)}, bf16[64,1024]{1,0:T(8,128)(2,1)S(1)}, u32[]{:S(2)}, u32[]{:S(2)}) collective-permute-start(bf16[64,1024]{1,0:T(8,128)(2,1)} %get-tuple-element.51), channel_id=1, source_target_pairs={{32,0},{64,32},{96,64},{0,96},{33,1},{65,33},{97,65},{1,97},{34,2}... | collective-permute-start | bytes 393224 | tf_op jit(solution)/shard_map/ppermute | solution.py:22
  162.6 15.3 %copy-start.5 = (f32[128,1024]{1,0:T(8,128)S(1)}, f32[128,1024]{1,0:T(8,128)}, u32[]{:S(2)}) copy-start(f32[128,1024]{1,0:T(8,128)} %copy-done.4) | copy-start | bytes 1572868
  166.5 10.7 %collective-permute-start.20 = (bf16[128,1024]{1,0:T(8,128)(2,1)S(1)}, bf16[128,1024]{1,0:T(8,128)(2,1)S(1)}, u32[]{:S(2)}, u32[]{:S(2)}) collective-permute-start(bf16[128,1024]{1,0:T(8,128)(2,1)S(1)} %add_convert_fusion.2), channel_id=1, source_target_pairs={{96,0},{0,32},{32,64},{64,96},{97,1},{1,33},{33,65},{65,97},{98,2}... | collective-permute-start | bytes 786440 | tf_op jit(solution)/shard_map/ppermute | solution.py:22
  167.6 10.4 %collective-permute-start.22 = (bf16[128,1024]{1,0:T(8,128)(2,1)S(1)}, bf16[128,1024]{1,0:T(8,128)(2,1)S(1)}, u32[]{:S(2)}, u32[]{:S(2)}) collective-permute-start(bf16[128,1024]{1,0:T(8,128)(2,1)S(1)} %add_convert_fusion.1), channel_id=1, source_target_pairs={{32,0},{64,32},{96,64},{0,96},{33,1},{65,33},{97,65},{1,97},{34,2}... | collective-permute-start | bytes 786440 | tf_op jit(solution)/shard_map/ppermute | solution.py:22
  171.2 8.8 %collective-permute-start.14 = (bf16[128,1024]{1,0:T(8,128)(2,1)S(1)}, bf16[128,1024]{1,0:T(8,128)(2,1)S(1)}, u32[]{:S(2)}, u32[]{:S(2)}) collective-permute-start(bf16[128,1024]{1,0:T(8,128)(2,1)S(1)} %add_convert_fusion.6), channel_id=1, source_target_pairs={{96,0},{0,32},{32,64},{64,96},{97,1},{1,33},{33,65},{65,97},{98,2}... | collective-permute-start | bytes 786440 | tf_op jit(solution)/shard_map/ppermute | solution.py:22
  177.1 6.4 %collective-permute-start.18 = (bf16[128,1024]{1,0:T(8,128)(2,1)S(1)}, bf16[128,1024]{1,0:T(8,128)(2,1)S(1)}, u32[]{:S(2)}, u32[]{:S(2)}) collective-permute-start(bf16[128,1024]{1,0:T(8,128)(2,1)S(1)} %add_convert_fusion.4), channel_id=1, source_target_pairs={{32,0},{64,32},{96,64},{0,96},{33,1},{65,33},{97,65},{1,97},{34,2}... | collective-permute-start | bytes 786440 | tf_op jit(solution)/shard_map/ppermute | solution.py:22
where the time goes:
time: 185 us
  starting transfers between devices  58.7 us (32%)
  waiting for transfers between devices  56.3 us (30%)
  blocking collectives  39.5 us (21%)
  local copies, waits for them, and re-layouts  9.18 us (5%)
  matrix products  8.63 us (5%)
  Pallas kernels  8.38 us (5%)
  other arithmetic  3.54 us (2%)
    ppermute x23, waiting for transfers between devices, ahead(): lax.ppermute(array, axis, [((i + step) % size, i) for i in range(size)])  34.9 us
    all_to_all x2, blocking collectives, all_to_all(): return lax.all_to_all(array, axis, split_axis=0, concat_axis=0, tiled=True)  31.7 us
    all_to_all x6, starting transfers between devices, all_to_all(): return lax.all_to_all(array, axis, split_axis=0, concat_axis=0, tiled=True)  31.1 us
    ppermute x23, starting transfers between devices, ahead(): lax.ppermute(array, axis, [((i + step) % size, i) for i in range(size)])  27.7 us
    all_to_all x6, waiting for transfers between devices, all_to_all(): return lax.all_to_all(array, axis, split_axis=0, concat_axis=0, tiled=True)  21.4 us
    dot_general x1, matrix products, shards(): jnp.einsum('erf,efd->erd', hidden, expert_out, preferred_element_type=jnp...  8.63 us
    all_gather x1, blocking collectives, shards(): rows = lax.all_gather(slot_inputs, 'dp', axis=0, tiled=True)  7.78 us
    pallas_call x3, Pallas kernels, dispatch(): pl.pallas_call(dispatch_kernel, out_shape=(jax.ShapeDtypeStruct((owners,...  6.03 us
  transfers between devices with their start and end apart: 29, of which 13 were waited for; matrix products, arithmetic and copies ran while one was open for 3% of the time, Pallas kernels for 4%

commit v1 on v0

v1 whole, which is shorter than its diff:
```python
import functools

import jax
import jax.numpy as jnp
from jax import lax
from jax.experimental import pallas as pl
from jax.experimental.pallas import tpu as pltpu
from jax.sharding import Mesh
from jax.sharding import PartitionSpec as P


X, Z, Y = "slot_0", "slot_1", "slot_2"
SLOT = (X, Z, Y)
OWNERS = (Z, Y)
LANES = 128
ROOM = 24 * 1024 * 1024
VMEM = pl.BlockSpec(memory_space=pltpu.VMEM)


def ahead(array, axis, step):
    size = lax.axis_size(axis)
    return lax.ppermute(array, axis, [((i + step) % size, i) for i in range(size)])


def swapped(array, axis, mask):
    size = lax.axis_size(axis)
    return lax.ppermute(array, axis, [(i, i ^ mask) for i in range(size)])


def all_to_all(array, axis):
    return lax.all_to_all(array, axis, split_axis=0, concat_axis=0, tiled=True)


def to_everyone(array, axis):
    copies = jnp.broadcast_to(array, (lax.axis_size(axis), *array.shape))
    return all_to_all(copies, axis)


def dispatch_kernel(keys, own, r0, r1, f0, f1, l0, l1, message, logits, row_stats, field):
    owners, own_slots, features = keys.shape
    slots = owners * own_slots
    images, positions, _ = own.shape
    half = positions // 2

    def one(b, carry):
        field[:positions] = own[b]
        for k, block in enumerate((r0, r1, f0, f1, l0, l1)):
            field[positions + k * half : positions + (k + 1) * half] = block[b]
        values = lax.dot_general(
            keys[...].reshape(slots, features),
            field[...],
            (((1,), (1,)), ((), ())),
            preferred_element_type=jnp.float32,
        )
        logits[b] = values
        row_top = jnp.max(values, axis=0, keepdims=True)
        row_total = jnp.sum(jnp.exp(values - row_top), axis=0, keepdims=True)
        row_stats[b] = jnp.concatenate([row_top, row_total], axis=0)
        top = jnp.max(values, axis=1, keepdims=True).astype(jnp.bfloat16).astype(jnp.float32)
        raised = jnp.exp(values - top)
        rest = jnp.sum(raised, axis=1, keepdims=True)
        lane = lax.broadcasted_iota(jnp.int32, (slots, LANES), 1)
        stats = jnp.where(lane == 0, top, 0.0)
        for k in (1, 2, 3):
            piece = rest.astype(jnp.bfloat16).astype(jnp.float32)
            stats = jnp.where(lane == k, piece, stats)
            rest = rest - piece
        stats = stats.astype(jnp.bfloat16).reshape(owners, own_slots, LANES)
        sums = jnp.dot(
            raised.astype(jnp.bfloat16), field[...], preferred_element_type=jnp.float32
        ).astype(jnp.bfloat16)
        sums = sums.reshape(owners, own_slots, features)
        for k in range(owners):
            message[k, b, :, features:] = stats[k]
            message[k, b, :, :features] = sums[k]
        return carry

    lax.fori_loop(0, images, one, 0)


def dispatch(keys, blocks):
    owners, own_slots, features = keys.shape
    images = blocks[0].shape[0]
    slots, positions = owners * own_slots, sum(block.shape[1] for block in blocks)
    return pl.pallas_call(
        dispatch_kernel,
        out_shape=(
            jax.ShapeDtypeStruct((owners, images, own_slots, features + LANES), jnp.bfloat16),
            jax.ShapeDtypeStruct((images, slots, positions), jnp.float32),
            jax.ShapeDtypeStruct((images, 2, positions), jnp.float32),
        ),
        in_specs=[VMEM] * (1 + len(blocks)),
        out_specs=(VMEM,) * 3,
        scratch_shapes=[pltpu.VMEM((positions, features), jnp.bfloat16)],
        cost_estimate=pl.CostEstimate(
            flops=4 * images * slots * positions * features,
            bytes_accessed=4 * images * slots * features,
            transcendentals=2 * images * slots * positions,
        ),
        compiler_params=pltpu.CompilerParams(vmem_limit_bytes=ROOM),
        name="dispatch",
    )(keys, *blocks)


def merge_kernel(arrived, inputs):
    owners, images, _, _ = arrived.shape
    features = inputs.shape[2]
    for b in range(images):
        tops, totals = [], []
        for k in range(owners):
            stats = arrived[k, b, :, features:].astype(jnp.float32)
            tops.append(stats[:, 0:1])
            totals.append(stats[:, 1:2] + stats[:, 2:3] + stats[:, 3:4])
        peak = functools.reduce(jnp.maximum, tops)
        scales = [jnp.exp(top - peak) for top in tops]
        whole = sum(scale * total for scale, total in zip(scales, totals))
        summed = sum(
            (scales[k] / whole) * arrived[k, b, :, :features].astype(jnp.float32)
            for k in range(owners)
        )
        inputs[b] = summed.astype(jnp.bfloat16)


def merge(arrived):
    _, images, own_slots, width = arrived.shape
    return pl.pallas_call(
        merge_kernel,
        out_shape=jax.ShapeDtypeStruct((images, own_slots, width - LANES), jnp.bfloat16),
        in_specs=[VMEM],
        out_specs=VMEM,
        cost_estimate=pl.CostEstimate(
            flops=4 * arrived.size, bytes_accessed=2 * arrived.size, transcendentals=0
        ),
        compiler_params=pltpu.CompilerParams(vmem_limit_bytes=ROOM),
        name="merge",
    )(arrived)


def combine_kernel(logits, own_stats, first, second, third, everyone, own, *rest):
    images, positions, _ = own.shape
    half = positions // 2
    owners, _, _, _ = everyone.shape

    def one(b, carry):
        stats = [own_stats[b], first[b], second[b], third[b]]
        for k in (1, 2, 3):
            cut = 4 * positions - k * positions
            stats[k] = jnp.concatenate([stats[k][:, cut:], stats[k][:, :cut]], axis=1)
        highest = functools.reduce(jnp.maximum, [s[0:1] for s in stats])
        whole = sum(s[1:2] * jnp.exp(s[0:1] - highest) for s in stats)
        mix = (jnp.exp(logits[b] - highest) / whole).astype(jnp.bfloat16)
        outputs = jnp.concatenate([everyone[k, b] for k in range(owners)], axis=0)
        combined = lax.dot_general(
            mix, outputs, (((0,), (0,)), ((), ())), preferred_element_type=jnp.float32
        )
        own[b] = combined[:positions]
        for k, out in enumerate(rest):
            at = positions + k * half
            out[b] = combined[at : at + half].astype(out.dtype)
        return carry

    lax.fori_loop(0, images, one, 0)


def combine(logits, own_stats, other_stats, everyone):
    images, slots, width = logits.shape
    features = everyone.shape[3]
    positions = width // 4
    kinds = (jnp.float32, jnp.bfloat16, jnp.bfloat16, jnp.bfloat16, jnp.bfloat16, jnp.float32)
    return pl.pallas_call(
        combine_kernel,
        out_shape=(
            jax.ShapeDtypeStruct((images, positions, features), jnp.float32),
            *(jax.ShapeDtypeStruct((images, positions // 2, features), kind) for kind in kinds),
        ),
        in_specs=[VMEM] * 6,
        out_specs=(VMEM,) * 7,
        cost_estimate=pl.CostEstimate(
            flops=2 * images * slots * width * features,
            bytes_accessed=4 * images * slots * width,
            transcendentals=images * slots * width,
        ),
        compiler_params=pltpu.CompilerParams(vmem_limit_bytes=ROOM),
        name="combine",
    )(logits, own_stats, *other_stats, everyone)


def shards(tokens, slot_keys, expert_in, expert_out):
    images, positions, features = tokens.shape
    own_slots = slot_keys.shape[1]
    experts = expert_in.shape[0]
    per_expert = own_slots // experts
    ranks = lax.axis_size("dp")
    half = positions // 2
    low, high = tokens[:, :half], tokens[:, half:]

    r0 = ahead(low, X, 1)
    l1 = ahead(high, X, 3)
    r1 = ahead(high, X, 1)
    l0 = ahead(low, X, 3)
    keys = to_everyone(slot_keys.T, OWNERS)
    f0 = ahead(r0, X, 1)
    f1 = ahead(l1, X, 3)
    message, logits, row_stats = dispatch(keys, [tokens, r0, r1, f0, f1, l0, l1])
    arrived = all_to_all(message, OWNERS)
    other_stats = [ahead(row_stats, X, k) for k in (1, 2, 3)]
    slot_inputs = merge(arrived)

    rows = lax.all_gather(slot_inputs, "dp", axis=0, tiled=True)
    rows = rows.reshape(ranks * images, experts, per_expert, features)
    rows = rows.transpose(1, 0, 2, 3).reshape(experts, -1, features)
    hidden = jnp.einsum("erd,edf->erf", rows, expert_in, preferred_element_type=jnp.float32)
    hidden = jax.nn.gelu(hidden, approximate=True).astype(jnp.bfloat16)
    result = jnp.einsum("erf,efd->erd", hidden, expert_out, preferred_element_type=jnp.float32)
    result = result.reshape(experts, ranks, images, per_expert, features)
    result = result.transpose(1, 2, 0, 3, 4).reshape(ranks, images, own_slots, features)
    rank = lax.axis_index("dp")
    outputs = lax.dynamic_index_in_dim(result, rank, 0, keepdims=False)
    for k in (2, 3, 1):
        piece = lax.dynamic_index_in_dim(result, rank ^ k, 0, keepdims=False)
        piece = swapped(piece.astype(jnp.bfloat16), "dp", k)
        outputs = outputs + piece.astype(jnp.float32)
    everyone = to_everyone(outputs.astype(jnp.bfloat16), OWNERS)

    own, r0, r1, f0, f1, l0, l1 = combine(logits, row_stats, other_stats, everyone)
    p0 = ahead(f0, X, 3).astype(jnp.float32)
    p1 = ahead(f1, X, 1).astype(jnp.float32)
    u1 = ahead(r1, X, 3).astype(jnp.float32)
    v0 = ahead(l0, X, 1).astype(jnp.float32)
    u0 = ahead((r0 + p0).astype(jnp.bfloat16), X, 3).astype(jnp.float32)
    v1 = ahead((l1 + p1).astype(jnp.bfloat16), X, 1).astype(jnp.float32)
    low = (own[:, :half] + u0 + v0).astype(jnp.bfloat16)
    high = (own[:, half:] + u1 + v1).astype(jnp.bfloat16)
    return jnp.concatenate([low, high], axis=1)


def solution(mesh):
    split = Mesh(mesh.devices.reshape(4, 4, 2, mesh.shape["dp"]), (X, Z, Y, "dp"))
    return jax.shard_map(
        shards,
        mesh=split,
        in_specs=(P("dp", SLOT, None), P(None, SLOT), P(SLOT, None, "dp"), P(SLOT, "dp", None)),
        out_specs=P("dp", SLOT, None),
        check_vma=False,
    )
```

time: 185 us -> 169 us (0.914)
  blocking collectives: 39.5 us -> 8.28 us
  waiting for transfers between devices: 56.3 us -> 84.9 us
  starting transfers between devices: 58.7 us -> 41.3 us
  local copies, waits for them, and re-layouts: 9.18 us -> 15.6 us
  Pallas kernels: 8.38 us -> 6.51 us
    all_to_all x2 -> x0, blocking collectives: 31.7 us -> none  [all_to_all(): return lax.all_to_all(array, axis, split_axis=0, concat_axis=0, tiled=True)]
    all_to_all x6 -> x3, waiting for transfers between devices: 21.4 us -> 40.4 us  [all_to_all(): return lax.all_to_all(array, axis, split_axis=0, concat_axis=0, tiled=True)]
    all_to_all x6 -> x3, starting transfers between devices: 31.1 us -> 18.6 us  [all_to_all(): return lax.all_to_all(array, axis, split_axis=0, concat_axis=0, tiled=True)]
    ppermute x0 -> x3, waiting for transfers between devices: none -> 8.6 us  [swapped(): return lax.ppermute(array, axis, [(i, i ^ mask) for i in range(size)])]
    ppermute x23 -> x15, starting transfers between devices: 27.7 us -> 20.5 us  [ahead(): lax.ppermute(array, axis, [((i + step) % size, i) for i in range(size)])]
    unnamed x22 -> x24, local copies, waits for them, and re-layouts: 3.75 us -> 8.75 us
    ppermute x0 -> x3, starting transfers between devices: none -> 2.22 us  [swapped(): return lax.ppermute(array, axis, [(i, i ^ mask) for i in range(size)])]
    pallas_call x3 -> x1, Pallas kernels: 6.03 us -> 4.2 us  [dispatch(): pl.pallas_call(dispatch_kernel, out_shape=(jax.ShapeDtypeStruct((owners,...]
  transfers between devices with their start and end apart: 29 -> 21, of which waited for: 13 -> 14; matrix products, arithmetic and copies ran while one was open for 3% -> 1% of each run, Pallas kernels for 4% -> 0%
where the time goes in v1:
time: 169 us; the launch traced here: 168 us
  waiting for transfers between devices  84.9 us (50%)
  starting transfers between devices  41.3 us (24%)
  local copies, waits for them, and re-layouts  15.6 us (9%)
  matrix products  8.85 us (5%)
  blocking collectives  8.28 us (5%)
  Pallas kernels  6.51 us (4%)
  other arithmetic  2.58 us (2%)
    all_to_all x3, waiting for transfers between devices, all_to_all(): return lax.all_to_all(array, axis, split_axis=0, concat_axis=0, tiled=True)  40.4 us
    ppermute x15, waiting for transfers between devices, ahead(): lax.ppermute(array, axis, [((i + step) % size, i) for i in range(size)])  35.8 us
    ppermute x15, starting transfers between devices, ahead(): lax.ppermute(array, axis, [((i + step) % size, i) for i in range(size)])  20.5 us
    all_to_all x3, starting transfers between devices, all_to_all(): return lax.all_to_all(array, axis, split_axis=0, concat_axis=0, tiled=True)  18.6 us
    dot_general x1, matrix products, shards(): jnp.einsum('erf,efd->erd', hidden, expert_out, preferred_element_type=jnp...  8.85 us
    unnamed x24, local copies, waits for them, and re-layouts  8.75 us
    ppermute x3, waiting for transfers between devices, swapped(): return lax.ppermute(array, axis, [(i, i ^ mask) for i in range(size)])  8.6 us
    all_gather x1, blocking collectives, shards(): rows = lax.all_gather(slot_inputs, 'dp', axis=0, tiled=True)  8.28 us
  transfers between devices with their start and end apart: 21, of which 14 were waited for; matrix products, arithmetic and copies ran while one was open for 1% of the time, Pallas kernels for 0%

profile of v1, /device:TPU:0, one launch (start us, length us, event | category | flops | bytes accessed | tf_op | source)
XLA Modules:
  0.0 168.1 jit_solution(10360231853500347712)
XLA Ops:
  0.0 2.0 %fusion.32 = (bf16[3,64,1024]{2,1,0:T(8,128)(2,1)}, bf16[3,64,1024]{2,1,0:T(8,128)(2,1)S(1)}) fusion(bf16[3,128,1024]{2,1,0:T(8,128)(2,1)} %own.1), kind=kLoop, calls=%fused_computation.37 | loop fusion | bytes 1572864 | tf_op jit(solution)/shard_map/slice | solution.py:195
  2.0 1.6 collective-permute-start.3
  3.6 1.6 collective-permute-start
  5.3 0.9 broadcast_in_dim.6
  6.1 8.1 %all-to-all-start = ((bf16[8,32,1024]{2,1,0:T(8,128)(2,1)}), bf16[8,32,1024]{2,1,0:T(8,128)(2,1)S(1)}, u32[]{:S(2)}, u32[]{:S(2)}) async-start(bf16[8,32,1024]{2,1,0:T(8,128)(2,1)} %broadcast_in_dim.6), calls=%async_computation | async-start | bytes 1048576 | tf_op jit(solution)/shard_map/all_to_all | solution.py:31
  14.2 1.5 collective-permute-start.1
  16.5 3.0 %collective-permute-start.2 = (bf16[3,64,1024]{2,1,0:T(8,128)(2,1)S(1)}, bf16[3,64,1024]{2,1,0:T(8,128)(2,1)S(1)}, u32[]{:S(2)}, u32[]{:S(2)}) collective-permute-start(bf16[3,64,1024]{2,1,0:T(8,128)(2,1)S(1)} %collective-permute-done.r0), channel_id=1, source_target_pairs={{32,0},{64,32},{96,64},{0,96},{33,1},{65,33},{97,65},{1,97},{34,2}... | collective-permute-start | bytes 1179656 | tf_op jit(solution)/shard_map/ppermute | solution.py:22
  19.5 0.7 copy-done.1
  20.2 6.2 %collective-permute-done.1.r1 = bf16[3,64,1024]{2,1,0:T(8,128)(2,1)S(1)} collective-permute-done((bf16[3,64,1024]{2,1,0:T(8,128)(2,1)}, bf16[3,64,1024]{2,1,0:T(8,128)(2,1)S(1)}, u32[]{:S(2)}, u32[]{:S(2)}) %collective-permute-start.1) | collective-permute-done | bytes 393248 | tf_op jit(solution)/shard_map/ppermute | solution.py:22
  26.4 0.8 copy-done.3
  27.1 1.8 %collective-permute-done.5.l0 = bf16[3,64,1024]{2,1,0:T(8,128)(2,1)S(1)} collective-permute-done((bf16[3,64,1024]{2,1,0:T(8,128)(2,1)S(1)}, bf16[3,64,1024]{2,1,0:T(8,128)(2,1)S(1)}, u32[]{:S(2)}, u32[]{:S(2)}) %collective-permute-start.5) | collective-permute-done | bytes 393248 | tf_op jit(solution)/shard_map/ppermute | solution.py:22
  28.9 0.8 copy-done.5
  29.7 5.4 %collective-permute-done.4.f1 = bf16[3,64,1024]{2,1,0:T(8,128)(2,1)S(1)} collective-permute-done((bf16[3,64,1024]{2,1,0:T(8,128)(2,1)S(1)}, bf16[3,64,1024]{2,1,0:T(8,128)(2,1)S(1)}, u32[]{:S(2)}, u32[]{:S(2)}) %collective-permute-start.4) | collective-permute-done | bytes 393248 | tf_op jit(solution)/shard_map/ppermute | solution.py:22
  35.1 0.8 copy-done.7
  35.9 0.7 copy-done.9
  36.6 1.0 copy-done.2
  37.6 1.0 copy-done.4
  38.6 1.0 copy-done.6
  39.6 1.0 copy-done.8
  40.6 1.0 copy-done.10
  41.6 4.2 %dispatch.1 = (bf16[8,3,32,1152]{3,2,1,0:T(8,128)(2,1)}, f32[3,256,512]{2,1,0:T(8,128)S(1)}, f32[3,2,512]{2,1,0:T(2,128)S(1)}) custom-call(bf16[8,32,1024]{2,1,0:T(8,128)(2,1)S(1)} %all-to-all-done.keys, bf16[3,128,1024]{2,1,0:T(8,128)(2,1)S(1)} %copy-done, bf16[3,64,1024]{2,1,0:T(8,128)(2,1)S(1)} %copy-done.2, bf16[3,64,1024]{2,1,0:T(8,128)(2,1)S(1)} %copy-done.4, ...), custom_call_target="tpu_custom_call" | custom-call | flops 1610612736 | bytes 3145728 | tf_op jit(solution)/shard_map/dispatch/pallas_call | solution.py:85
  45.8 6.9 %all-to-all-start.1 = ((bf16[8,3,32,1152]{3,2,1,0:T(8,128)(2,1)}), bf16[8,3,32,1152]{3,2,1,0:T(8,128)(2,1)S(1)}, u32[]{:S(2)}, u32[]{:S(2)}) async-start(bf16[8,3,32,1152]{3,2,1,0:T(8,128)(2,1)} %get-tuple-element.17), calls=%async_computation.1 | async-start | bytes 3538944 | tf_op jit(solution)/shard_map/all_to_all | solution.py:31
  52.7 22.7 %all-to-all-done.1.arrived = bf16[8,3,32,1152]{3,2,1,0:T(8,128)(2,1)S(1)} async-done(((bf16[8,3,32,1152]{3,2,1,0:T(8,128)(2,1)}), bf16[8,3,32,1152]{3,2,1,0:T(8,128)(2,1)S(1)}, u32[]{:S(2)}, u32[]{:S(2)}) %all-to-all-start.1) | async-done | bytes 1769504 | tf_op jit(solution)/shard_map/all_to_all | solution.py:31
  75.4 0.8 merge.1
  76.2 8.3 %all_gather.3 = bf16[12,32,1024]{2,1,0:T(8,128)(2,1)} all-gather(bf16[3,32,1024]{2,1,0:T(8,128)(2,1)S(1)} %merge.1), channel_id=1, replica_groups=mesh['slot_0'=4,'slot_1'=4,'slot_2'=2,'dp'=4] {'dp'}, dimensions={0}, use_global_device_ids=true | all-gather | bytes 983040 | tf_op jit(solution)/shard_map/all_gather | solution.py:209
  84.5 8.9 %fusion.8 = f32[4,96,1024]{2,1,0:T(8,128)S(1)} fusion(bf16[4,1024,1024]{2,1,0:T(8,128)(2,1)} %param.7, bf16[4,1024,1024]{2,1,0:T(8,128)(2,1)} %param.6, bf16[12,32,1024]{2,1,0:T(8,128)(2,1)} %all_gather.3), kind=kOutput, calls=%fused_computation.10 | convolution fusion | flops 1614151680 | bytes 19136512 | tf_op jit(solution)/shard_map/erf,efd->erd/dot_general | solution.py:214
  93.3 1.3 copy.15
  94.6 1.3 fusion.25
  95.9 1.4 collective-permute-start.9
  97.4 0.8 collective-permute-start.10
  98.2 5.6 %collective-permute-done.9 = bf16[3,32,1024]{2,1,0:T(8,128)(2,1)S(1)} collective-permute-done((bf16[3,32,1024]{2,1,0:T(8,128)(2,1)S(1)}, bf16[3,32,1024]{2,1,0:T(8,128)(2,1)S(1)}, u32[]{:S(2)}, u32[]{:S(2)}) %collective-permute-start.9) | collective-permute-done | bytes 196640 | tf_op jit(solution)/shard_map/ppermute | solution.py:27
  103.8 3.0 %collective-permute-done.10 = bf16[3,32,1024]{2,1,0:T(8,128)(2,1)S(1)} collective-permute-done((bf16[3,32,1024]{2,1,0:T(8,128)(2,1)S(1)}, bf16[3,32,1024]{2,1,0:T(8,128)(2,1)S(1)}, u32[]{:S(2)}, u32[]{:S(2)}) %collective-permute-start.10) | collective-permute-done | bytes 196640 | tf_op jit(solution)/shard_map/ppermute | solution.py:27
  106.8 1.1 fusion.24
  107.9 1.4 broadcast_in_dim.7
  109.3 3.6 %all-to-all-start.2 = ((bf16[8,3,32,1024]{3,2,1,0:T(8,128)(2,1)}), bf16[8,3,32,1024]{3,2,1,0:T(8,128)(2,1)S(1)}, u32[]{:S(2)}, u32[]{:S(2)}) async-start(bf16[8,3,32,1024]{3,2,1,0:T(8,128)(2,1)} %broadcast_in_dim.7), calls=%async_computation.2 | async-start | bytes 3145728 | tf_op jit(solution)/shard_map/all_to_all | solution.py:31
  112.9 1.5 collective-permute-start.7
  114.4 1.8 %collective-permute-start.6 = (f32[3,2,512]{2,1,0:T(2,128)S(1)}, f32[3,2,512]{2,1,0:T(2,128)S(1)}, u32[]{:S(2)}, u32[]{:S(2)}) collective-permute-start(f32[3,2,512]{2,1,0:T(2,128)S(1)} %get-tuple-element.16.own_stats), channel_id=1, source_target_pairs={{32,0},{64,32},{96,64},{0,96},{33,1},{65,33},{97,65},{1,97},{34,2}... | collective-permute-start | bytes 36872 | tf_op jit(solution)/shard_map/ppermute | solution.py:22
  116.2 1.7 collective-permute-done.8.third
  118.2 0.6 collective-permute-done.6.first
  118.8 17.7 %all-to-all-done.2.everyone = bf16[8,3,32,1024]{3,2,1,0:T(8,128)(2,1)S(1)} async-done(((bf16[8,3,32,1024]{3,2,1,0:T(8,128)(2,1)}), bf16[8,3,32,1024]{3,2,1,0:T(8,128)(2,1)S(1)}, u32[]{:S(2)}, u32[]{:S(2)}) %all-to-all-start.2) | async-done | bytes 1572896 | tf_op jit(solution)/shard_map/all_to_all | solution.py:31
  136.5 1.5 combine.1
  138.1 3.2 %collective-permute-start.16 = (bf16[3,64,1024]{2,1,0:T(8,128)(2,1)S(1)}, bf16[3,64,1024]{2,1,0:T(8,128)(2,1)S(1)}, u32[]{:S(2)}, u32[]{:S(2)}) collective-permute-start(bf16[3,64,1024]{2,1,0:T(8,128)(2,1)S(1)} %get-tuple-element.24), channel_id=1, source_target_pairs={{32,0},{64,32},{96,64},{0,96},{33,1},{65,33},{97,65},{1,97},{34,2}... | collective-permute-start | bytes 1179656 | tf_op jit(solution)/shard_map/ppermute | solution.py:22
  141.4 2.0 %collective-permute-start.15 = (bf16[3,64,1024]{2,1,0:T(8,128)(2,1)S(1)}, bf16[3,64,1024]{2,1,0:T(8,128)(2,1)S(1)}, u32[]{:S(2)}, u32[]{:S(2)}) collective-permute-start(bf16[3,64,1024]{2,1,0:T(8,128)(2,1)S(1)} %get-tuple-element.22), channel_id=1, source_target_pairs={{96,0},{0,32},{32,64},{64,96},{97,1},{1,33},{33,65},{65,97},{98,2}... | collective-permute-start | bytes 1179656 | tf_op jit(solution)/shard_map/ppermute | solution.py:22
  143.4 7.9 %collective-permute-done.12 = bf16[3,64,1024]{2,1,0:T(8,128)(2,1)S(1)} collective-permute-done((bf16[3,64,1024]{2,1,0:T(8,128)(2,1)S(1)}, bf16[3,64,1024]{2,1,0:T(8,128)(2,1)S(1)}, u32[]{:S(2)}, u32[]{:S(2)}) %collective-permute-start.12) | collective-permute-done | bytes 393248 | tf_op jit(solution)/shard_map/ppermute | solution.py:22
  151.6 3.3 %collective-permute-start.17 = (bf16[3,64,1024]{2,1,0:T(8,128)(2,1)S(1)}, bf16[3,64,1024]{2,1,0:T(8,128)(2,1)S(1)}, u32[]{:S(2)}, u32[]{:S(2)}) collective-permute-start(bf16[3,64,1024]{2,1,0:T(8,128)(2,1)S(1)} %add_convert_fusion.1), channel_id=1, source_target_pairs={{32,0},{64,32},{96,64},{0,96},{33,1},{65,33},{97,65},{1,97},{34,2}... | collective-permute-start | bytes 1179656 | tf_op jit(solution)/shard_map/ppermute | solution.py:22
  154.9 4.4 %collective-permute-done.14 = bf16[3,64,1024]{2,1,0:T(8,128)(2,1)S(1)} collective-permute-done((bf16[3,64,1024]{2,1,0:T(8,128)(2,1)S(1)}, bf16[3,64,1024]{2,1,0:T(8,128)(2,1)S(1)}, u32[]{:S(2)}, u32[]{:S(2)}) %collective-permute-start.14) | collective-permute-done | bytes 393248 | tf_op jit(solution)/shard_map/ppermute | solution.py:22
  159.7 7.0 %collective-permute-done.13 = bf16[3,64,1024]{2,1,0:T(8,128)(2,1)S(1)} collective-permute-done((bf16[3,64,1024]{2,1,0:T(8,128)(2,1)S(1)}, bf16[3,64,1024]{2,1,0:T(8,128)(2,1)S(1)}, u32[]{:S(2)}, u32[]{:S(2)}) %collective-permute-start.13) | collective-permute-done | bytes 393248 | tf_op jit(solution)/shard_map/ppermute | solution.py:22
  167.1 0.9 pad_maximum_fusion
  (33 shorter events, 2.5 us)
Async XLA Ops:
  0.0 36.6 %copy-start = (bf16[3,128,1024]{2,1,0:T(8,128)(2,1)S(1)}, bf16[3,128,1024]{2,1,0:T(8,128)(2,1)}, u32[]{:S(2)}) copy-start(bf16[3,128,1024]{2,1,0:T(8,128)(2,1)} %own.1) | copy-start | bytes 2359300
  0.0 5.3 %copy-start.11 = (bf16[1024,32]{0,1:T(8,128)(2,1)S(1)}, bf16[1024,32]{0,1:T(8,128)(2,1)}, u32[]{:S(2)}) copy-start(bf16[1024,32]{0,1:T(8,128)(2,1)} %param.5) | copy-start | bytes 196612
  2.0 14.2 %collective-permute-start.3 = (bf16[3,64,1024]{2,1,0:T(8,128)(2,1)}, bf16[3,64,1024]{2,1,0:T(8,128)(2,1)S(1)}, u32[]{:S(2)}, u32[]{:S(2)}) collective-permute-start(bf16[3,64,1024]{2,1,0:T(8,128)(2,1)} %get-tuple-element.30), channel_id=1, source_target_pairs={{96,0},{0,32},{32,64},{64,96},{97,1},{1,33},{33,65},{65,97},{98,2}... | collective-permute-start | bytes 1179656 | tf_op jit(solution)/shard_map/ppermute | solution.py:22
  3.6 12.9 %collective-permute-start = (bf16[3,64,1024]{2,1,0:T(8,128)(2,1)S(1)}, bf16[3,64,1024]{2,1,0:T(8,128)(2,1)S(1)}, u32[]{:S(2)}, u32[]{:S(2)}) collective-permute-start(bf16[3,64,1024]{2,1,0:T(8,128)(2,1)S(1)} %get-tuple-element.31), channel_id=1, source_target_pairs={{32,0},{64,32},{96,64},{0,96},{33,1},{65,33},{97,65},{1,97},{34,2}... | collective-permute-start | bytes 1179656 | tf_op jit(solution)/shard_map/ppermute | solution.py:22
  6.1 23.6 %all-to-all-start = ((bf16[8,32,1024]{2,1,0:T(8,128)(2,1)}), bf16[8,32,1024]{2,1,0:T(8,128)(2,1)S(1)}, u32[]{:S(2)}, u32[]{:S(2)}) async-start(bf16[8,32,1024]{2,1,0:T(8,128)(2,1)} %broadcast_in_dim.6), calls=%async_computation | async-start | bytes 1048576 | tf_op jit(solution)/shard_map/all_to_all | solution.py:31
  14.2 12.2 %collective-permute-start.1 = (bf16[3,64,1024]{2,1,0:T(8,128)(2,1)}, bf16[3,64,1024]{2,1,0:T(8,128)(2,1)S(1)}, u32[]{:S(2)}, u32[]{:S(2)}) collective-permute-start(bf16[3,64,1024]{2,1,0:T(8,128)(2,1)} %get-tuple-element.30), channel_id=1, source_target_pairs={{32,0},{64,32},{96,64},{0,96},{33,1},{65,33},{97,65},{1,97},{34,2}... | collective-permute-start | bytes 1179656 | tf_op jit(solution)/shard_map/ppermute | solution.py:22
  15.7 13.2 %collective-permute-start.5 = (bf16[3,64,1024]{2,1,0:T(8,128)(2,1)S(1)}, bf16[3,64,1024]{2,1,0:T(8,128)(2,1)S(1)}, u32[]{:S(2)}, u32[]{:S(2)}) collective-permute-start(bf16[3,64,1024]{2,1,0:T(8,128)(2,1)S(1)} %get-tuple-element.31), channel_id=1, source_target_pairs={{96,0},{0,32},{32,64},{64,96},{97,1},{1,33},{33,65},{65,97},{98,2}... | collective-permute-start | bytes 1179656 | tf_op jit(solution)/shard_map/ppermute | solution.py:22
  16.2 18.9 %collective-permute-start.4 = (bf16[3,64,1024]{2,1,0:T(8,128)(2,1)S(1)}, bf16[3,64,1024]{2,1,0:T(8,128)(2,1)S(1)}, u32[]{:S(2)}, u32[]{:S(2)}) collective-permute-start(bf16[3,64,1024]{2,1,0:T(8,128)(2,1)S(1)} %collective-permute-done.3.l1), channel_id=1, source_target_pairs={{96,0},{0,32},{32,64},{64,96},{97,1},{1,33},{33,65},{65,97},{98,2}... | collective-permute-start | bytes 1179656 | tf_op jit(solution)/shard_map/ppermute | solution.py:22
  16.5 19.4 %collective-permute-start.2 = (bf16[3,64,1024]{2,1,0:T(8,128)(2,1)S(1)}, bf16[3,64,1024]{2,1,0:T(8,128)(2,1)S(1)}, u32[]{:S(2)}, u32[]{:S(2)}) collective-permute-start(bf16[3,64,1024]{2,1,0:T(8,128)(2,1)S(1)} %collective-permute-done.r0), channel_id=1, source_target_pairs={{32,0},{64,32},{96,64},{0,96},{33,1},{65,33},{97,65},{1,97},{34,2}... | collective-permute-start | bytes 1179656 | tf_op jit(solution)/shard_map/ppermute | solution.py:22
  19.5 0.8 copy-start.1
  26.4 0.8 copy-start.3
  28.9 0.8 copy-start.5
  35.1 0.8 copy-start.7
  35.9 0.7 copy-start.9
  36.6 1.0 copy-start.2
  37.6 1.0 copy-start.4
  38.6 1.0 copy-start.6
  39.6 1.0 copy-start.8
  40.6 1.0 copy-start.10
  45.8 29.6 %all-to-all-start.1 = ((bf16[8,3,32,1152]{3,2,1,0:T(8,128)(2,1)}), bf16[8,3,32,1152]{3,2,1,0:T(8,128)(2,1)S(1)}, u32[]{:S(2)}, u32[]{:S(2)}) async-start(bf16[8,3,32,1152]{3,2,1,0:T(8,128)(2,1)} %get-tuple-element.17), calls=%async_computation.1 | async-start | bytes 3538944 | tf_op jit(solution)/shard_map/all_to_all | solution.py:31
  95.9 7.9 %collective-permute-start.9 = (bf16[3,32,1024]{2,1,0:T(8,128)(2,1)S(1)}, bf16[3,32,1024]{2,1,0:T(8,128)(2,1)S(1)}, u32[]{:S(2)}, u32[]{:S(2)}) collective-permute-start(bf16[3,32,1024]{2,1,0:T(8,128)(2,1)S(1)} %get-tuple-element.27), channel_id=1, source_target_pairs={{0,2},{1,3},{2,0},{3,1},{4,6},{5,7},{6,4},{7,5},{8,10},{9,11},{10,... | collective-permute-start | bytes 589832 | tf_op jit(solution)/shard_map/ppermute | solution.py:27
  97.3 6.5 %collective-permute-start.11 = (bf16[3,32,1024]{2,1,0:T(8,128)(2,1)S(1)}, bf16[3,32,1024]{2,1,0:T(8,128)(2,1)S(1)}, u32[]{:S(2)}, u32[]{:S(2)}) collective-permute-start(bf16[3,32,1024]{2,1,0:T(8,128)(2,1)S(1)} %get-tuple-element.28), channel_id=1, source_target_pairs={{0,1},{1,0},{2,3},{3,2},{4,5},{5,4},{6,7},{7,6},{8,9},{9,8},{10,11... | collective-permute-start | bytes 589832 | tf_op jit(solution)/shard_map/ppermute | solution.py:27
  97.4 9.4 %collective-permute-start.10 = (bf16[3,32,1024]{2,1,0:T(8,128)(2,1)S(1)}, bf16[3,32,1024]{2,1,0:T(8,128)(2,1)S(1)}, u32[]{:S(2)}, u32[]{:S(2)}) collective-permute-start(bf16[3,32,1024]{2,1,0:T(8,128)(2,1)S(1)} %get-tuple-element.29), channel_id=1, source_target_pairs={{0,3},{1,2},{2,1},{3,0},{4,7},{5,6},{6,5},{7,4},{8,11},{9,10},{10,... | collective-permute-start | bytes 589832 | tf_op jit(solution)/shard_map/ppermute | solution.py:27
  109.3 27.3 %all-to-all-start.2 = ((bf16[8,3,32,1024]{3,2,1,0:T(8,128)(2,1)}), bf16[8,3,32,1024]{3,2,1,0:T(8,128)(2,1)S(1)}, u32[]{:S(2)}, u32[]{:S(2)}) async-start(bf16[8,3,32,1024]{3,2,1,0:T(8,128)(2,1)} %broadcast_in_dim.7), calls=%async_computation.2 | async-start | bytes 3145728 | tf_op jit(solution)/shard_map/all_to_all | solution.py:31
  112.8 5.0 %collective-permute-start.8 = (f32[3,2,512]{2,1,0:T(2,128)S(1)}, f32[3,2,512]{2,1,0:T(2,128)S(1)}, u32[]{:S(2)}, u32[]{:S(2)}) collective-permute-start(f32[3,2,512]{2,1,0:T(2,128)S(1)} %get-tuple-element.16.own_stats), channel_id=1, source_target_pairs={{96,0},{0,32},{32,64},{64,96},{97,1},{1,33},{33,65},{65,97},{98,2}... | collective-permute-start | bytes 36872 | tf_op jit(solution)/shard_map/ppermute | solution.py:22
  112.9 5.3 %collective-permute-start.7 = (f32[3,2,512]{2,1,0:T(2,128)S(1)}, f32[3,2,512]{2,1,0:T(2,128)S(1)}, u32[]{:S(2)}, u32[]{:S(2)}) collective-permute-start(f32[3,2,512]{2,1,0:T(2,128)S(1)} %get-tuple-element.16.own_stats), channel_id=1, source_target_pairs={{64,0},{96,32},{0,64},{32,96},{65,1},{97,33},{1,65},{33,97},{66,2}... | collective-permute-start | bytes 36872 | tf_op jit(solution)/shard_map/ppermute | solution.py:22
  114.4 4.4 %collective-permute-start.6 = (f32[3,2,512]{2,1,0:T(2,128)S(1)}, f32[3,2,512]{2,1,0:T(2,128)S(1)}, u32[]{:S(2)}, u32[]{:S(2)}) collective-permute-start(f32[3,2,512]{2,1,0:T(2,128)S(1)} %get-tuple-element.16.own_stats), channel_id=1, source_target_pairs={{32,0},{64,32},{96,64},{0,96},{33,1},{65,33},{97,65},{1,97},{34,2}... | collective-permute-start | bytes 36872 | tf_op jit(solution)/shard_map/ppermute | solution.py:22
  138.0 13.3 %collective-permute-start.12 = (bf16[3,64,1024]{2,1,0:T(8,128)(2,1)S(1)}, bf16[3,64,1024]{2,1,0:T(8,128)(2,1)S(1)}, u32[]{:S(2)}, u32[]{:S(2)}) collective-permute-start(bf16[3,64,1024]{2,1,0:T(8,128)(2,1)S(1)} %get-tuple-element.20), channel_id=1, source_target_pairs={{96,0},{0,32},{32,64},{64,96},{97,1},{1,33},{33,65},{65,97},{98,2}... | collective-permute-start | bytes 1179656 | tf_op jit(solution)/shard_map/ppermute | solution.py:22
  138.1 13.4 %collective-permute-start.16 = (bf16[3,64,1024]{2,1,0:T(8,128)(2,1)S(1)}, bf16[3,64,1024]{2,1,0:T(8,128)(2,1)S(1)}, u32[]{:S(2)}, u32[]{:S(2)}) collective-permute-start(bf16[3,64,1024]{2,1,0:T(8,128)(2,1)S(1)} %get-tuple-element.24), channel_id=1, source_target_pairs={{32,0},{64,32},{96,64},{0,96},{33,1},{65,33},{97,65},{1,97},{34,2}... | collective-permute-start | bytes 1179656 | tf_op jit(solution)/shard_map/ppermute | solution.py:22
  141.3 17.9 %collective-permute-start.14 = (bf16[3,64,1024]{2,1,0:T(8,128)(2,1)S(1)}, bf16[3,64,1024]{2,1,0:T(8,128)(2,1)S(1)}, u32[]{:S(2)}, u32[]{:S(2)}) collective-permute-start(bf16[3,64,1024]{2,1,0:T(8,128)(2,1)S(1)} %get-tuple-element.21), channel_id=1, source_target_pairs={{32,0},{64,32},{96,64},{0,96},{33,1},{65,33},{97,65},{1,97},{34,2}... | collective-permute-start | bytes 1179656 | tf_op jit(solution)/shard_map/ppermute | solution.py:22
  141.4 18.4 %collective-permute-start.15 = (bf16[3,64,1024]{2,1,0:T(8,128)(2,1)S(1)}, bf16[3,64,1024]{2,1,0:T(8,128)(2,1)S(1)}, u32[]{:S(2)}, u32[]{:S(2)}) collective-permute-start(bf16[3,64,1024]{2,1,0:T(8,128)(2,1)S(1)} %get-tuple-element.22), channel_id=1, source_target_pairs={{96,0},{0,32},{32,64},{64,96},{97,1},{1,33},{33,65},{65,97},{98,2}... | collective-permute-start | bytes 1179656 | tf_op jit(solution)/shard_map/ppermute | solution.py:22
  151.4 15.3 %collective-permute-start.13 = (bf16[3,64,1024]{2,1,0:T(8,128)(2,1)S(1)}, bf16[3,64,1024]{2,1,0:T(8,128)(2,1)S(1)}, u32[]{:S(2)}, u32[]{:S(2)}) collective-permute-start(bf16[3,64,1024]{2,1,0:T(8,128)(2,1)S(1)} %add_convert_fusion.3), channel_id=1, source_target_pairs={{96,0},{0,32},{32,64},{64,96},{97,1},{1,33},{33,65},{65,97},{98,2}... | collective-permute-start | bytes 1179656 | tf_op jit(solution)/shard_map/ppermute | solution.py:22
  151.6 15.2 %collective-permute-start.17 = (bf16[3,64,1024]{2,1,0:T(8,128)(2,1)S(1)}, bf16[3,64,1024]{2,1,0:T(8,128)(2,1)S(1)}, u32[]{:S(2)}, u32[]{:S(2)}) collective-permute-start(bf16[3,64,1024]{2,1,0:T(8,128)(2,1)S(1)} %add_convert_fusion.1), channel_id=1, source_target_pairs={{32,0},{64,32},{96,64},{0,96},{33,1},{65,33},{97,65},{1,97},{34,2}... | collective-permute-start | bytes 1179656 | tf_op jit(solution)/shard_map/ppermute | solution.py:22

commit v2 on v1

--- a/solution.py
+++ b/solution.py
@@ -15,6 +15,7 @@
 LANES = 128
 ROOM = 24 * 1024 * 1024
 VMEM = pl.BlockSpec(memory_space=pltpu.VMEM)
+ANY = pl.BlockSpec(memory_space=pl.ANY)
 
 
 def ahead(array, axis, step):
@@ -36,19 +37,57 @@
     return all_to_all(copies, axis)
 
 
-def dispatch_kernel(keys, own, r0, r1, f0, f1, l0, l1, message, logits, row_stats, field):
+def dispatch_kernel(
+    first,
+    second,
+    keys,
+    own,
+    r0,
+    r1,
+    f0,
+    f1,
+    l0,
+    l1,
+    message,
+    logits,
+    row_stats,
+    first_here,
+    second_here,
+    field,
+    arrivals,
+    loaded,
+):
     owners, own_slots, features = keys.shape
     slots = owners * own_slots
     images, positions, _ = own.shape
     half = positions // 2
 
+    def copies(b):
+        blocks = [(own.at[b], field.at[b, 0:positions])]
+        for k, block in enumerate((r0, r1, f0, f1, l0, l1)):
+            at = positions + k * half
+            blocks.append((block.at[b], field.at[b, at : at + half]))
+        return [
+            pltpu.make_async_copy(source, target, arrivals.at[b, k])
+            for k, (source, target) in enumerate(blocks)
+        ]
+
+    for b in range(images):
+        for copy in copies(b):
+            copy.start()
+    loads = [
+        pltpu.make_async_copy(first, first_here, loaded.at[0]),
+        pltpu.make_async_copy(second, second_here, loaded.at[1]),
+    ]
+    for load in loads:
+        load.start()
+
     def one(b, carry):
-        field[:positions] = own[b]
-        for k, block in enumerate((r0, r1, f0, f1, l0, l1)):
-            field[positions + k * half : positions + (k + 1) * half] = block[b]
+        for copy in copies(b):
+            copy.wait()
         values = lax.dot_general(
             keys[...].reshape(slots, features),
-            field[...],
+            field[b],
             (((1,), (1,)), ((), ())),
             preferred_element_type=jnp.float32,
         )
@@ -67,7 +106,7 @@
             rest = rest - piece
         stats = stats.astype(jnp.bfloat16).reshape(owners, own_slots, LANES)
         sums = jnp.dot(
-            raised.astype(jnp.bfloat16), field[...], preferred_element_type=jnp.float32
+            raised.astype(jnp.bfloat16), field[b], preferred_element_type=jnp.float32
         ).astype(jnp.bfloat16)
         sums = sums.reshape(owners, own_slots, features)
         for k in range(owners):
@@ -76,9 +115,11 @@
         return carry
 
     lax.fori_loop(0, images, one, 0)
-
-
-def dispatch(keys, blocks):
+    for load in loads:
+        load.wait()
+
+
+def dispatch(weights, keys, blocks):
     owners, own_slots, features = keys.shape
     images = blocks[0].shape[0]
     slots, positions = owners * own_slots, sum(block.shape[1] for block in blocks)
@@ -88,10 +129,15 @@
             jax.ShapeDtypeStruct((owners, images, own_slots, features + LANES), jnp.bfloat16),
             jax.ShapeDtypeStruct((images, slots, positions), jnp.float32),
             jax.ShapeDtypeStruct((images, 2, positions), jnp.float32),
-        ),
-        in_specs=[VMEM] * (1 + len(blocks)),
-        out_specs=(VMEM,) * 3,
-        scratch_shapes=[pltpu.VMEM((positions, features), jnp.bfloat16)],
+            *(jax.ShapeDtypeStruct(w.shape, w.dtype) for w in weights),
+        ),
+        in_specs=[ANY] * 2 + [VMEM] + [ANY] * len(blocks),
+        out_specs=(VMEM,) * 5,
+        scratch_shapes=[
+            pltpu.VMEM((images, positions, features), jnp.bfloat16),
+            pltpu.SemaphoreType.DMA((images, len(blocks))),
+            pltpu.SemaphoreType.DMA((2,)),
+        ],
         cost_estimate=pl.CostEstimate(
             flops=4 * images * slots * positions * features,
             bytes_accessed=4 * images * slots * features,
@@ -99,7 +145,7 @@
         ),
         compiler_params=pltpu.CompilerParams(vmem_limit_bytes=ROOM),
         name="dispatch",
-    )(keys, *blocks)
+    )(*weights, keys, *blocks)
 
 
 def merge_kernel(arrived, inputs):
@@ -136,6 +182,75 @@
     )(arrived)
 
 
+def expert_kernel(rows, first, second, *outs):
+    rank = lax.axis_index("dp")
+    experts = first.shape[0]
+    images, own_slots, _ = outs[0].shape
+    per_expert = own_slots // experts
+
+    def one(expert, carry):
+        cut = pl.ds(pl.multiple_of(expert * per_expert, per_expert), per_expert)
+        taken = [
+            rows[(rank ^ k) * images + b, cut, :]
+            for k in range(len(outs))
+            for b in range(images)
+        ]
+        hidden = jnp.dot(
+            jnp.concatenate(taken, axis=0), first[expert], preferred_element_type=jnp.float32
+        )
+        hidden = jax.nn.gelu(hidden, approximate=True).astype(jnp.bfloat16)
+        result = jnp.dot(hidden, second[expert], preferred_element_type=jnp.float32)
+        for k, out in enumerate(outs):
+            for b in range(images):
+                at = (k * images + b) * per_expert
+                out[b, cut, :] = result[at : at + per_expert].astype(out.dtype)
+        return carry
+
+    lax.fori_loop(0, experts, one, 0)
+
+
+def run_experts(rows, expert_in, expert_out, ranks):
+    images, own_slots = rows.shape[0] // ranks, rows.shape[1]
+    shape = (images, own_slots, rows.shape[2])
+    kinds = (jnp.float32, *(jnp.bfloat16 for _ in range(ranks - 1)))
+    return pl.pallas_call(
+        expert_kernel,
+        out_shape=[jax.ShapeDtypeStruct(shape, kind) for kind in kinds],
+        in_specs=[VMEM] * 3,
+        out_specs=[VMEM] * ranks,
+        cost_estimate=pl.CostEstimate(
+            flops=4 * rows.size * expert_in.shape[2],
+            bytes_accessed=4 * expert_in.size,
+            transcendentals=rows.size,
+        ),
+        compiler_params=pltpu.CompilerParams(vmem_limit_bytes=ROOM),
+        name="experts",
+    )(rows, expert_in, expert_out)
+
+
+def spread_kernel(own, first, second, third, copies):
+    total = own[...]
+    for piece in (first, second, third):
+        total = total + piece[...].astype(jnp.float32)
+    total = total.astype(jnp.bfloat16)
+    for k in range(copies.shape[0]):
+        copies[k] = total
+
+
+def spread(own, pieces, count):
+    return pl.pallas_call(
+        spread_kernel,
+        out_shape=jax.ShapeDtypeStruct((count, *own.shape), jnp.bfloat16),
+        in_specs=[VMEM] * 4,
+        out_specs=VMEM,
+        cost_estimate=pl.CostEstimate(
+            flops=4 * own.size, bytes_accessed=2 * count * own.size, transcendentals=0
+        ),
+        compiler_params=pltpu.CompilerParams(vmem_limit_bytes=ROOM),
+        name="spread",
+    )(own, *pieces)
+
+
 def combine_kernel(logits, own_stats, first, second, third, everyone, own, *rest):
     images, positions, _ = own.shape
     half = positions // 2
@@ -186,10 +301,7 @@
 
 
 def shards(tokens, slot_keys, expert_in, expert_out):
-    images, positions, features = tokens.shape
-    own_slots = slot_keys.shape[1]
-    experts = expert_in.shape[0]
-    per_expert = own_slots // experts
+    _, positions, _ = tokens.shape
     ranks = lax.axis_size("dp")
     half = positions // 2
     low, high = tokens[:, :half], tokens[:, half:]
@@ -201,26 +313,17 @@
     keys = to_everyone(slot_keys.T, OWNERS)
     f0 = ahead(r0, X, 1)
     f1 = ahead(l1, X, 3)
-    message, logits, row_stats = dispatch(keys, [tokens, r0, r1, f0, f1, l0, l1])
+    message, logits, row_stats, *weights = dispatch(
+        (expert_in, expert_out), keys, [tokens, r0, r1, f0, f1, l0, l1]
+    )
     arrived = all_to_all(message, OWNERS)
+    rows = lax.all_gather(merge(arrived), "dp", axis=0, tiled=True)
+    row_stats, rows = lax.optimization_barrier((row_stats, rows))
     other_stats = [ahead(row_stats, X, k) for k in (1, 2, 3)]
-    slot_inputs = merge(arrived)
-
-    rows = lax.all_gather(slot_inputs, "dp", axis=0, tiled=True)
-    rows = rows.reshape(ranks * images, experts, per_expert, features)
-    rows = rows.transpose(1, 0, 2, 3).reshape(experts, -1, features)
-    hidden = jnp.einsum("erd,edf->erf", rows, expert_in, preferred_element_type=jnp.float32)
-    hidden = jax.nn.gelu(hidden, approximate=True).astype(jnp.bfloat16)
-    result = jnp.einsum("erf,efd->erd", hidden, expert_out, preferred_element_type=jnp.float32)
-    result = result.reshape(experts, ranks, images, per_expert, features)
-    result = result.transpose(1, 2, 0, 3, 4).reshape(ranks, images, own_slots, features)
-    rank = lax.axis_index("dp")
-    outputs = lax.dynamic_index_in_dim(result, rank, 0, keepdims=False)
-    for k in (2, 3, 1):
-        piece = lax.dynamic_index_in_dim(result, rank ^ k, 0, keepdims=False)
-        piece = swapped(piece.astype(jnp.bfloat16), "dp", k)
-        outputs = outputs + piece.astype(jnp.float32)
-    everyone = to_everyone(outputs.astype(jnp.bfloat16), OWNERS)
+    own, *pieces = run_experts(rows, *weights, ranks)
+    pieces = [swapped(piece, "dp", k) for k, piece in zip((1, 2, 3), pieces)]
+    pieces, other_stats = lax.optimization_barrier((pieces, other_stats))
+    everyone = all_to_all(spread(own, pieces, lax.axis_size(OWNERS)), OWNERS)
 
     own, r0, r1, f0, f1, l0, l1 = combine(logits, row_stats, other_stats, everyone)
     p0 = ahead(f0, X, 3).astype(jnp.float32)

time: 169 us -> 155 us (0.917)
  blocking collectives: 8.28 us -> 63.9 us
  waiting for transfers between devices: 84.9 us -> 42.3 us
  local copies, waits for them, and re-layouts: 15.6 us -> 3.03 us
  starting transfers between devices: 41.3 us -> 29.3 us
  matrix products: 8.85 us -> 0 us
  Pallas kernels: 6.51 us -> 14.5 us
    all_to_all x0 -> x2, blocking collectives: none -> 56.1 us  [all_to_all(): return lax.all_to_all(array, axis, split_axis=0, concat_axis=0, tiled=True)]
    all_to_all x3 -> x1, waiting for transfers between devices: 40.4 us -> 0.01 us  [all_to_all(): return lax.all_to_all(array, axis, split_axis=0, concat_axis=0, tiled=True)]
    all_to_all x3 -> x1, starting transfers between devices: 18.6 us -> 8.07 us  [all_to_all(): return lax.all_to_all(array, axis, split_axis=0, concat_axis=0, tiled=True)]
    dot_general x1 -> x0, matrix products: 8.85 us -> none  [shards(): jnp.einsum('erf,efd->erd', hidden, expert_out, preferred_element_type=jnp...]
    unnamed x24 -> x4, local copies, waits for them, and re-layouts: 8.75 us -> 0.01 us
    ppermute x3, waiting for transfers between devices: 8.6 us -> 0.16 us  [swapped(): return lax.ppermute(array, axis, [(i, i ^ mask) for i in range(size)])]
    ppermute x15, waiting for transfers between devices: 35.8 us -> 42.2 us  [ahead(): lax.ppermute(array, axis, [((i + step) % size, i) for i in range(size)])]
    pallas_call x1, Pallas kernels: 4.2 us -> 8.57 us  [dispatch(): pl.pallas_call(dispatch_kernel, out_shape=(jax.ShapeDtypeStruct((owners,...]
  transfers between devices with their start and end apart: 21 -> 19, of which waited for: 14 -> 11; matrix products, arithmetic and copies ran while one was open for 1% -> 1% of each run, Pallas kernels for 0% -> 0%
where the time goes in v2:
time: 155 us
  blocking collectives  63.9 us (41%)
  waiting for transfers between devices  42.3 us (27%)
  starting transfers between devices  29.3 us (19%)
  Pallas kernels  14.5 us (9%)
  local copies, waits for them, and re-layouts  3.03 us (2%)
    all_to_all x2, blocking collectives, all_to_all(): return lax.all_to_all(array, axis, split_axis=0, concat_axis=0, tiled=True)  56.1 us
    ppermute x15, waiting for transfers between devices, ahead(): lax.ppermute(array, axis, [((i + step) % size, i) for i in range(size)])  42.2 us
    ppermute x15, starting transfers between devices, ahead(): lax.ppermute(array, axis, [((i + step) % size, i) for i in range(size)])  19.3 us
    pallas_call x1, Pallas kernels, dispatch(): pl.pallas_call(dispatch_kernel, out_shape=(jax.ShapeDtypeStruct((owners,...  8.57 us
    all_to_all x1, starting transfers between devices, all_to_all(): return lax.all_to_all(array, axis, split_axis=0, concat_axis=0, tiled=True)  8.07 us
    all_gather x1, blocking collectives, shards(): rows = lax.all_gather(merge(arrived), 'dp', axis=0, tiled=True)  7.78 us
    pallas_call x1, Pallas kernels, run_experts(): pl.pallas_call(expert_kernel, out_shape=[jax.ShapeDtypeStruct(shape, kind...  3.46 us
  transfers between devices with their start and end apart: 19, of which 11 were waited for; matrix products, arithmetic and copies ran while one was open for 1% of the time, Pallas kernels for 0%

profile of v2, /device:TPU:0, one launch (start us, length us, event | category | flops | bytes accessed | tf_op | source)
XLA Modules:
  0.0 154.6 jit_solution(17220817204740155532)
XLA Ops:
  0.0 2.2 %fusion = (bf16[3,64,1024]{2,1,0:T(8,128)(2,1)}, bf16[3,64,1024]{2,1,0:T(8,128)(2,1)}) fusion(bf16[3,128,1024]{2,1,0:T(8,128)(2,1)} %own.1), kind=kLoop, calls=%fused_computation.5 | loop fusion | bytes 1572864 | tf_op jit(solution)/shard_map/slice | solution.py:307
  2.2 1.6 %collective-permute-start.3 = (bf16[3,64,1024]{2,1,0:T(8,128)(2,1)}, bf16[3,64,1024]{2,1,0:T(8,128)(2,1)S(1)}, u32[]{:S(2)}, u32[]{:S(2)}) collective-permute-start(bf16[3,64,1024]{2,1,0:T(8,128)(2,1)} %get-tuple-element.55), channel_id=1, source_target_pairs={{96,0},{0,32},{32,64},{64,96},{97,1},{1,33},{33,65},{65,97},{98,2}... | collective-permute-start | bytes 1179656 | tf_op jit(solution)/shard_map/ppermute | solution.py:23
  3.8 1.6 %collective-permute-start = (bf16[3,64,1024]{2,1,0:T(8,128)(2,1)}, bf16[3,64,1024]{2,1,0:T(8,128)(2,1)S(1)}, u32[]{:S(2)}, u32[]{:S(2)}) collective-permute-start(bf16[3,64,1024]{2,1,0:T(8,128)(2,1)} %get-tuple-element.56), channel_id=1, source_target_pairs={{32,0},{64,32},{96,64},{0,96},{33,1},{65,33},{97,65},{1,97},{34,2}... | collective-permute-start | bytes 1179656 | tf_op jit(solution)/shard_map/ppermute | solution.py:23
  5.4 0.9 broadcast_in_dim.3
  6.3 8.1 %all-to-all-start = ((bf16[8,32,1024]{2,1,0:T(8,128)(2,1)}), bf16[8,32,1024]{2,1,0:T(8,128)(2,1)S(1)}, u32[]{:S(2)}, u32[]{:S(2)}) async-start(bf16[8,32,1024]{2,1,0:T(8,128)(2,1)} %broadcast_in_dim.3), calls=%async_computation | async-start | bytes 1048576 | tf_op jit(solution)/shard_map/all_to_all | solution.py:32
  14.3 1.5 %collective-permute-start.1 = (bf16[3,64,1024]{2,1,0:T(8,128)(2,1)}, bf16[3,64,1024]{2,1,0:T(8,128)(2,1)S(1)}, u32[]{:S(2)}, u32[]{:S(2)}) collective-permute-start(bf16[3,64,1024]{2,1,0:T(8,128)(2,1)} %get-tuple-element.55), channel_id=1, source_target_pairs={{32,0},{64,32},{96,64},{0,96},{33,1},{65,33},{97,65},{1,97},{34,2}... | collective-permute-start | bytes 1179656 | tf_op jit(solution)/shard_map/ppermute | solution.py:23
  15.9 0.5 collective-permute-start.5
  16.4 0.3 collective-permute-start.4
  16.6 0.0 collective-permute-done.r0
  16.6 3.0 %collective-permute-start.2 = (bf16[3,64,1024]{2,1,0:T(8,128)(2,1)S(1)}, bf16[3,64,1024]{2,1,0:T(8,128)(2,1)}, u32[]{:S(2)}, u32[]{:S(2)}) collective-permute-start(bf16[3,64,1024]{2,1,0:T(8,128)(2,1)S(1)} %collective-permute-done.r0), channel_id=1, source_target_pairs={{32,0},{64,32},{96,64},{0,96},{33,1},{65,33},{97,65},{1,97},{34,2}... | collective-permute-start | bytes 1179656 | tf_op jit(solution)/shard_map/ppermute | solution.py:23
  19.6 6.9 %collective-permute-done.1.r1 = bf16[3,64,1024]{2,1,0:T(8,128)(2,1)S(1)} collective-permute-done((bf16[3,64,1024]{2,1,0:T(8,128)(2,1)}, bf16[3,64,1024]{2,1,0:T(8,128)(2,1)S(1)}, u32[]{:S(2)}, u32[]{:S(2)}) %collective-permute-start.1) | collective-permute-done | bytes 393248 | tf_op jit(solution)/shard_map/ppermute | solution.py:23
  26.5 2.8 %collective-permute-done.5.l0 = bf16[3,64,1024]{2,1,0:T(8,128)(2,1)S(1)} collective-permute-done((bf16[3,64,1024]{2,1,0:T(8,128)(2,1)}, bf16[3,64,1024]{2,1,0:T(8,128)(2,1)S(1)}, u32[]{:S(2)}, u32[]{:S(2)}) %collective-permute-start.5) | collective-permute-done | bytes 393248 | tf_op jit(solution)/shard_map/ppermute | solution.py:23
  29.3 0.0 all-to-all-done.keys
  29.3 6.2 %collective-permute-done.4.f1 = bf16[3,64,1024]{2,1,0:T(8,128)(2,1)S(1)} collective-permute-done((bf16[3,64,1024]{2,1,0:T(8,128)(2,1)S(1)}, bf16[3,64,1024]{2,1,0:T(8,128)(2,1)S(1)}, u32[]{:S(2)}, u32[]{:S(2)}) %collective-permute-start.4) | collective-permute-done | bytes 393248 | tf_op jit(solution)/shard_map/ppermute | solution.py:23
  35.5 0.0 collective-permute-done.2.f0
  35.5 8.6 %dispatch.1 = (bf16[8,3,32,1152]{3,2,1,0:T(8,128)(2,1)S(1)}, f32[3,256,512]{2,1,0:T(8,128)S(1)}, f32[3,2,512]{2,1,0:T(2,128)S(1)}, bf16[4,1024,1024]{2,1,0:T(8,128)(2,1)S(1)}, bf16[4,1024,1024]{2,1,0:T(8,128)(2,1)S(1)}) custom-call(bf16[4,1024,1024]{2,1,0:T(8,128)(2,1)} %first.1, bf16[4,1024,1024]{2,1,0:T(8,128)(2,1)} %second.1, ...), custom_call_target="tpu_custom_call" | custom-call | flops 1610612736 | bytes 3145728 | tf_op jit(solution)/shard_map/dispatch/pallas_call | solution.py:126
  44.1 29.4 %all_to_all.15.arrived = bf16[8,3,32,1152]{3,2,1,0:T(8,128)(2,1)S(1)} all-to-all(bf16[8,3,32,1152]{3,2,1,0:T(8,128)(2,1)S(1)} %get-tuple-element.31), channel_id=1, replica_groups=mesh['slot_0'=4,'slot_1'=4,'slot_2'=2,'dp'=4] {'slot_1','slot_2'}, dimensions={0} | all-to-all | bytes 3538944 | tf_op jit(solution)/shard_map/all_to_all | solution.py:32
  73.5 0.8 merge.1
  74.3 7.8 %all_gather.3.rows = bf16[12,32,1024]{2,1,0:T(8,128)(2,1)S(1)} all-gather(bf16[3,32,1024]{2,1,0:T(8,128)(2,1)S(1)} %merge.1), channel_id=1, replica_groups=mesh['slot_0'=4,'slot_1'=4,'slot_2'=2,'dp'=4] {'dp'}, dimensions={0}, use_global_device_ids=true | all-gather | bytes 983040 | tf_op jit(solution)/shard_map/all_gather | solution.py:320
  82.1 3.5 %experts.1 = (f32[3,32,1024]{2,1,0:T(8,128)S(1)}, bf16[3,32,1024]{2,1,0:T(8,128)(2,1)S(1)}, bf16[3,32,1024]{2,1,0:T(8,128)(2,1)S(1)}, bf16[3,32,1024]{2,1,0:T(8,128)(2,1)S(1)}) custom-call(bf16[12,32,1024]{2,1,0:T(8,128)(2,1)S(1)} %all_gather.3.rows, bf16[4,1024,1024]{2,1,0:T(8,128)(2,1)S(1)} %get-tuple-element.34.first, ...), custom_call_target="tpu_custom_call" | custom-call | flops 1610612736 | bytes 16777216 | tf_op jit(solution)/shard_map/experts/pallas_call | solution.py:216
  85.5 0.4 collective-permute-start.6
  86.0 1.4 collective-permute-start.7
  87.3 0.2 collective-permute-start.8
  87.5 2.1 %collective-permute-start.10 = (f32[3,2,512]{2,1,0:T(2,128)S(1)}, f32[3,2,512]{2,1,0:T(2,128)S(1)}, u32[]{:S(2)}, u32[]{:S(2)}) collective-permute-start(f32[3,2,512]{2,1,0:T(2,128)S(1)} %get-tuple-element.32.own_stats), channel_id=1, source_target_pairs={{64,0},{96,32},{0,64},{32,96},{65,1},{97,33},{1,65},{33,97},{66,2}... | collective-permute-start | bytes 36872 | tf_op jit(solution)/shard_map/ppermute | solution.py:23
  89.6 2.9 %collective-permute-done.11.third = f32[3,2,512]{2,1,0:T(2,128)S(1)} collective-permute-done((f32[3,2,512]{2,1,0:T(2,128)S(1)}, f32[3,2,512]{2,1,0:T(2,128)S(1)}, u32[]{:S(2)}, u32[]{:S(2)}) %collective-permute-start.11) | collective-permute-done | bytes 12320 | tf_op jit(solution)/shard_map/ppermute | solution.py:23
  92.5 0.2 collective-permute-done.10.second
  92.7 3.5 %collective-permute-done.9.first = f32[3,2,512]{2,1,0:T(2,128)S(1)} collective-permute-done((f32[3,2,512]{2,1,0:T(2,128)S(1)}, f32[3,2,512]{2,1,0:T(2,128)S(1)}, u32[]{:S(2)}, u32[]{:S(2)}) %collective-permute-start.9) | collective-permute-done | bytes 12320 | tf_op jit(solution)/shard_map/ppermute | solution.py:23
  96.2 0.0 collective-permute-done.6.first
  96.2 0.0 collective-permute-done.7.second
  96.2 0.2 collective-permute-done.8.third
  96.3 0.1 spread.1
  96.5 26.7 %all_to_all.16.everyone = bf16[8,3,32,1024]{3,2,1,0:T(8,128)(2,1)S(1)} all-to-all(bf16[8,3,32,1024]{3,2,1,0:T(8,128)(2,1)S(1)} %spread.1), channel_id=1, replica_groups=mesh['slot_0'=4,'slot_1'=4,'slot_2'=2,'dp'=4] {'slot_1','slot_2'}, dimensions={0} | all-to-all | bytes 3145728 | tf_op jit(solution)/shard_map/all_to_all | solution.py:32
  123.2 1.5 combine.1
  124.7 0.1 collective-permute-start.12
  124.8 3.2 %collective-permute-start.16 = (bf16[3,64,1024]{2,1,0:T(8,128)(2,1)S(1)}, bf16[3,64,1024]{2,1,0:T(8,128)(2,1)S(1)}, u32[]{:S(2)}, u32[]{:S(2)}) collective-permute-start(bf16[3,64,1024]{2,1,0:T(8,128)(2,1)S(1)} %get-tuple-element.52), channel_id=1, source_target_pairs={{32,0},{64,32},{96,64},{0,96},{33,1},{65,33},{97,65},{1,97},{34,2}... | collective-permute-start | bytes 1179656 | tf_op jit(solution)/shard_map/ppermute | solution.py:23
  128.0 0.0 collective-permute-start.14
  128.0 2.0 %collective-permute-start.15 = (bf16[3,64,1024]{2,1,0:T(8,128)(2,1)S(1)}, bf16[3,64,1024]{2,1,0:T(8,128)(2,1)S(1)}, u32[]{:S(2)}, u32[]{:S(2)}) collective-permute-start(bf16[3,64,1024]{2,1,0:T(8,128)(2,1)S(1)} %get-tuple-element.50), channel_id=1, source_target_pairs={{96,0},{0,32},{32,64},{64,96},{97,1},{1,33},{33,65},{65,97},{98,2}... | collective-permute-start | bytes 1179656 | tf_op jit(solution)/shard_map/ppermute | solution.py:23
  130.0 7.9 %collective-permute-done.12 = bf16[3,64,1024]{2,1,0:T(8,128)(2,1)S(1)} collective-permute-done((bf16[3,64,1024]{2,1,0:T(8,128)(2,1)S(1)}, bf16[3,64,1024]{2,1,0:T(8,128)(2,1)S(1)}, u32[]{:S(2)}, u32[]{:S(2)}) %collective-permute-start.12) | collective-permute-done | bytes 393248 | tf_op jit(solution)/shard_map/ppermute | solution.py:23
  138.0 0.1 add_convert_fusion.3
  138.0 0.1 collective-permute-start.13
  138.1 0.1 add_convert_fusion.1
  138.2 3.3 %collective-permute-start.17 = (bf16[3,64,1024]{2,1,0:T(8,128)(2,1)S(1)}, bf16[3,64,1024]{2,1,0:T(8,128)(2,1)S(1)}, u32[]{:S(2)}, u32[]{:S(2)}) collective-permute-start(bf16[3,64,1024]{2,1,0:T(8,128)(2,1)S(1)} %add_convert_fusion.1), channel_id=1, source_target_pairs={{32,0},{64,32},{96,64},{0,96},{33,1},{65,33},{97,65},{1,97},{34,2}... | collective-permute-start | bytes 1179656 | tf_op jit(solution)/shard_map/ppermute | solution.py:23
  141.5 4.4 %collective-permute-done.14 = bf16[3,64,1024]{2,1,0:T(8,128)(2,1)S(1)} collective-permute-done((bf16[3,64,1024]{2,1,0:T(8,128)(2,1)S(1)}, bf16[3,64,1024]{2,1,0:T(8,128)(2,1)S(1)}, u32[]{:S(2)}, u32[]{:S(2)}) %collective-permute-start.14) | collective-permute-done | bytes 393248 | tf_op jit(solution)/shard_map/ppermute | solution.py:23
  145.9 0.5 collective-permute-done.15
  146.4 7.0 %collective-permute-done.13 = bf16[3,64,1024]{2,1,0:T(8,128)(2,1)S(1)} collective-permute-done((bf16[3,64,1024]{2,1,0:T(8,128)(2,1)S(1)}, bf16[3,64,1024]{2,1,0:T(8,128)(2,1)S(1)}, u32[]{:S(2)}, u32[]{:S(2)}) %collective-permute-start.13) | collective-permute-done | bytes 393248 | tf_op jit(solution)/shard_map/ppermute | solution.py:23
  153.3 0.0 collective-permute-done.17
  153.3 0.4 add_convert_fusion.2
  153.7 0.9 pad_maximum_fusion
  (8 shorter events, 0.0 us)
Async XLA Ops:
  0.0 35.5 %copy-start = (bf16[3,128,1024]{2,1,0:T(8,128)(2,1)S(1)}, bf16[3,128,1024]{2,1,0:T(8,128)(2,1)}, u32[]{:S(2)}) copy-start(bf16[3,128,1024]{2,1,0:T(8,128)(2,1)} %own.1) | copy-start | bytes 2359300
  0.0 5.4 %copy-start.1 = (bf16[1024,32]{0,1:T(8,128)(2,1)S(1)}, bf16[1024,32]{0,1:T(8,128)(2,1)}, u32[]{:S(2)}) copy-start(bf16[1024,32]{0,1:T(8,128)(2,1)} %param.5) | copy-start | bytes 196612
  2.2 14.2 %collective-permute-start.3 = (bf16[3,64,1024]{2,1,0:T(8,128)(2,1)}, bf16[3,64,1024]{2,1,0:T(8,128)(2,1)S(1)}, u32[]{:S(2)}, u32[]{:S(2)}) collective-permute-start(bf16[3,64,1024]{2,1,0:T(8,128)(2,1)} %get-tuple-element.55), channel_id=1, source_target_pairs={{96,0},{0,32},{32,64},{64,96},{97,1},{1,33},{33,65},{65,97},{98,2}... | collective-permute-start | bytes 1179656 | tf_op jit(solution)/shard_map/ppermute | solution.py:23
  3.8 12.9 %collective-permute-start = (bf16[3,64,1024]{2,1,0:T(8,128)(2,1)}, bf16[3,64,1024]{2,1,0:T(8,128)(2,1)S(1)}, u32[]{:S(2)}, u32[]{:S(2)}) collective-permute-start(bf16[3,64,1024]{2,1,0:T(8,128)(2,1)} %get-tuple-element.56), channel_id=1, source_target_pairs={{32,0},{64,32},{96,64},{0,96},{33,1},{65,33},{97,65},{1,97},{34,2}... | collective-permute-start | bytes 1179656 | tf_op jit(solution)/shard_map/ppermute | solution.py:23
  6.3 23.0 %all-to-all-start = ((bf16[8,32,1024]{2,1,0:T(8,128)(2,1)}), bf16[8,32,1024]{2,1,0:T(8,128)(2,1)S(1)}, u32[]{:S(2)}, u32[]{:S(2)}) async-start(bf16[8,32,1024]{2,1,0:T(8,128)(2,1)} %broadcast_in_dim.3), calls=%async_computation | async-start | bytes 1048576 | tf_op jit(solution)/shard_map/all_to_all | solution.py:32
  14.3 12.2 %collective-permute-start.1 = (bf16[3,64,1024]{2,1,0:T(8,128)(2,1)}, bf16[3,64,1024]{2,1,0:T(8,128)(2,1)S(1)}, u32[]{:S(2)}, u32[]{:S(2)}) collective-permute-start(bf16[3,64,1024]{2,1,0:T(8,128)(2,1)} %get-tuple-element.55), channel_id=1, source_target_pairs={{32,0},{64,32},{96,64},{0,96},{33,1},{65,33},{97,65},{1,97},{34,2}... | collective-permute-start | bytes 1179656 | tf_op jit(solution)/shard_map/ppermute | solution.py:23
  15.9 13.4 %collective-permute-start.5 = (bf16[3,64,1024]{2,1,0:T(8,128)(2,1)}, bf16[3,64,1024]{2,1,0:T(8,128)(2,1)S(1)}, u32[]{:S(2)}, u32[]{:S(2)}) collective-permute-start(bf16[3,64,1024]{2,1,0:T(8,128)(2,1)} %get-tuple-element.56), channel_id=1, source_target_pairs={{96,0},{0,32},{32,64},{64,96},{97,1},{1,33},{33,65},{65,97},{98,2}... | collective-permute-start | bytes 1179656 | tf_op jit(solution)/shard_map/ppermute | solution.py:23
  16.4 19.1 %collective-permute-start.4 = (bf16[3,64,1024]{2,1,0:T(8,128)(2,1)S(1)}, bf16[3,64,1024]{2,1,0:T(8,128)(2,1)S(1)}, u32[]{:S(2)}, u32[]{:S(2)}) collective-permute-start(bf16[3,64,1024]{2,1,0:T(8,128)(2,1)S(1)} %collective-permute-done.3.l1), channel_id=1, source_target_pairs={{96,0},{0,32},{32,64},{64,96},{97,1},{1,33},{33,65},{65,97},{98,2}... | collective-permute-start | bytes 1179656 | tf_op jit(solution)/shard_map/ppermute | solution.py:23
  16.6 18.8 %collective-permute-start.2 = (bf16[3,64,1024]{2,1,0:T(8,128)(2,1)S(1)}, bf16[3,64,1024]{2,1,0:T(8,128)(2,1)}, u32[]{:S(2)}, u32[]{:S(2)}) collective-permute-start(bf16[3,64,1024]{2,1,0:T(8,128)(2,1)S(1)} %collective-permute-done.r0), channel_id=1, source_target_pairs={{32,0},{64,32},{96,64},{0,96},{33,1},{65,33},{97,65},{1,97},{34,2}... | collective-permute-start | bytes 1179656 | tf_op jit(solution)/shard_map/ppermute | solution.py:23
  85.5 10.6 %collective-permute-start.6 = (bf16[3,32,1024]{2,1,0:T(8,128)(2,1)S(1)}, bf16[3,32,1024]{2,1,0:T(8,128)(2,1)S(1)}, u32[]{:S(2)}, u32[]{:S(2)}) collective-permute-start(bf16[3,32,1024]{2,1,0:T(8,128)(2,1)S(1)} %get-tuple-element.36), channel_id=1, source_target_pairs={{0,1},{1,0},{2,3},{3,2},{4,5},{5,4},{6,7},{7,6},{8,9},{9,8},{10,11... | collective-permute-start | bytes 589832 | tf_op jit(solution)/shard_map/ppermute | solution.py:28
  86.0 10.2 %collective-permute-start.7 = (bf16[3,32,1024]{2,1,0:T(8,128)(2,1)S(1)}, bf16[3,32,1024]{2,1,0:T(8,128)(2,1)S(1)}, u32[]{:S(2)}, u32[]{:S(2)}) collective-permute-start(bf16[3,32,1024]{2,1,0:T(8,128)(2,1)S(1)} %get-tuple-element.37), channel_id=1, source_target_pairs={{0,2},{1,3},{2,0},{3,1},{4,6},{5,7},{6,4},{7,5},{8,10},{9,11},{10,... | collective-permute-start | bytes 589832 | tf_op jit(solution)/shard_map/ppermute | solution.py:28
  87.3 9.0 %collective-permute-start.8 = (bf16[3,32,1024]{2,1,0:T(8,128)(2,1)S(1)}, bf16[3,32,1024]{2,1,0:T(8,128)(2,1)S(1)}, u32[]{:S(2)}, u32[]{:S(2)}) collective-permute-start(bf16[3,32,1024]{2,1,0:T(8,128)(2,1)S(1)} %get-tuple-element.38), channel_id=1, source_target_pairs={{0,3},{1,2},{2,1},{3,0},{4,7},{5,6},{6,5},{7,4},{8,11},{9,10},{10,... | collective-permute-start | bytes 589832 | tf_op jit(solution)/shard_map/ppermute | solution.py:28
  87.5 5.0 %collective-permute-start.11 = (f32[3,2,512]{2,1,0:T(2,128)S(1)}, f32[3,2,512]{2,1,0:T(2,128)S(1)}, u32[]{:S(2)}, u32[]{:S(2)}) collective-permute-start(f32[3,2,512]{2,1,0:T(2,128)S(1)} %get-tuple-element.32.own_stats), channel_id=1, source_target_pairs={{96,0},{0,32},{32,64},{64,96},{97,1},{1,33},{33,65},{65,97},{98,2}... | collective-permute-start | bytes 36872 | tf_op jit(solution)/shard_map/ppermute | solution.py:23
  87.5 5.2 %collective-permute-start.10 = (f32[3,2,512]{2,1,0:T(2,128)S(1)}, f32[3,2,512]{2,1,0:T(2,128)S(1)}, u32[]{:S(2)}, u32[]{:S(2)}) collective-permute-start(f32[3,2,512]{2,1,0:T(2,128)S(1)} %get-tuple-element.32.own_stats), channel_id=1, source_target_pairs={{64,0},{96,32},{0,64},{32,96},{65,1},{97,33},{1,65},{33,97},{66,2}... | collective-permute-start | bytes 36872 | tf_op jit(solution)/shard_map/ppermute | solution.py:23
  92.5 3.7 %collective-permute-start.9 = (f32[3,2,512]{2,1,0:T(2,128)S(1)}, f32[3,2,512]{2,1,0:T(2,128)S(1)}, u32[]{:S(2)}, u32[]{:S(2)}) collective-permute-start(f32[3,2,512]{2,1,0:T(2,128)S(1)} %get-tuple-element.32.own_stats), channel_id=1, source_target_pairs={{32,0},{64,32},{96,64},{0,96},{33,1},{65,33},{97,65},{1,97},{34,2}... | collective-permute-start | bytes 36872 | tf_op jit(solution)/shard_map/ppermute | solution.py:23
  124.7 13.3 %collective-permute-start.12 = (bf16[3,64,1024]{2,1,0:T(8,128)(2,1)S(1)}, bf16[3,64,1024]{2,1,0:T(8,128)(2,1)S(1)}, u32[]{:S(2)}, u32[]{:S(2)}) collective-permute-start(bf16[3,64,1024]{2,1,0:T(8,128)(2,1)S(1)} %get-tuple-element.48), channel_id=1, source_target_pairs={{96,0},{0,32},{32,64},{64,96},{97,1},{1,33},{33,65},{65,97},{98,2}... | collective-permute-start | bytes 1179656 | tf_op jit(solution)/shard_map/ppermute | solution.py:23
  124.8 13.4 %collective-permute-start.16 = (bf16[3,64,1024]{2,1,0:T(8,128)(2,1)S(1)}, bf16[3,64,1024]{2,1,0:T(8,128)(2,1)S(1)}, u32[]{:S(2)}, u32[]{:S(2)}) collective-permute-start(bf16[3,64,1024]{2,1,0:T(8,128)(2,1)S(1)} %get-tuple-element.52), channel_id=1, source_target_pairs={{32,0},{64,32},{96,64},{0,96},{33,1},{65,33},{97,65},{1,97},{34,2}... | collective-permute-start | bytes 1179656 | tf_op jit(solution)/shard_map/ppermute | solution.py:23
  128.0 17.9 %collective-permute-start.14 = (bf16[3,64,1024]{2,1,0:T(8,128)(2,1)S(1)}, bf16[3,64,1024]{2,1,0:T(8,128)(2,1)S(1)}, u32[]{:S(2)}, u32[]{:S(2)}) collective-permute-start(bf16[3,64,1024]{2,1,0:T(8,128)(2,1)S(1)} %get-tuple-element.49), channel_id=1, source_target_pairs={{32,0},{64,32},{96,64},{0,96},{33,1},{65,33},{97,65},{1,97},{34,2}... | collective-permute-start | bytes 1179656 | tf_op jit(solution)/shard_map/ppermute | solution.py:23
  128.0 18.4 %collective-permute-start.15 = (bf16[3,64,1024]{2,1,0:T(8,128)(2,1)S(1)}, bf16[3,64,1024]{2,1,0:T(8,128)(2,1)S(1)}, u32[]{:S(2)}, u32[]{:S(2)}) collective-permute-start(bf16[3,64,1024]{2,1,0:T(8,128)(2,1)S(1)} %get-tuple-element.50), channel_id=1, source_target_pairs={{96,0},{0,32},{32,64},{64,96},{97,1},{1,33},{33,65},{65,97},{98,2}... | collective-permute-start | bytes 1179656 | tf_op jit(solution)/shard_map/ppermute | solution.py:23
  138.0 15.3 %collective-permute-start.13 = (bf16[3,64,1024]{2,1,0:T(8,128)(2,1)S(1)}, bf16[3,64,1024]{2,1,0:T(8,128)(2,1)S(1)}, u32[]{:S(2)}, u32[]{:S(2)}) collective-permute-start(bf16[3,64,1024]{2,1,0:T(8,128)(2,1)S(1)} %add_convert_fusion.3), channel_id=1, source_target_pairs={{96,0},{0,32},{32,64},{64,96},{97,1},{1,33},{33,65},{65,97},{98,2}... | collective-permute-start | bytes 1179656 | tf_op jit(solution)/shard_map/ppermute | solution.py:23
  138.2 15.1 %collective-permute-start.17 = (bf16[3,64,1024]{2,1,0:T(8,128)(2,1)S(1)}, bf16[3,64,1024]{2,1,0:T(8,128)(2,1)S(1)}, u32[]{:S(2)}, u32[]{:S(2)}) collective-permute-start(bf16[3,64,1024]{2,1,0:T(8,128)(2,1)S(1)} %add_convert_fusion.1), channel_id=1, source_target_pairs={{32,0},{64,32},{96,64},{0,96},{33,1},{65,33},{97,65},{1,97},{34,2}... | collective-permute-start | bytes 1179656 | tf_op jit(solution)/shard_map/ppermute | solution.py:23

commit v3 on v2

v3 whole, which is shorter than its diff:
```python
import functools

import jax
import jax.numpy as jnp
from jax import lax
from jax.experimental import pallas as pl
from jax.experimental.pallas import tpu as pltpu
from jax.sharding import Mesh
from jax.sharding import PartitionSpec as P


X, Z, Y = "slot_0", "slot_1", "slot_2"
SLOT = (X, Z, Y)
TILE = tuple(
    tuple((x * 4 + z) * 2 + y for x in range(4) for z in range(4) if (x + 2 * z) % 4 == r for y in (0, 1))
    for r in range(4)
)
LANES = 128
ROOM = 24 * 1024 * 1024
VMEM = pl.BlockSpec(memory_space=pltpu.VMEM)
ANY = pl.BlockSpec(memory_space=pl.ANY)


def ahead(array, axis, step):
    size = lax.axis_size(axis)
    return lax.ppermute(array, axis, [((i + step) % size, i) for i in range(size)])


def swapped(array, axis, mask):
    size = lax.axis_size(axis)
    return lax.ppermute(array, axis, [(i, i ^ mask) for i in range(size)])


def all_to_all(array):
    return lax.all_to_all(
        array, SLOT, split_axis=0, concat_axis=0, axis_index_groups=TILE, tiled=True
    )


def dispatch_kernel(keys, first, *refs):
    *blocks, message, logits, s0, s1, s2, s3, first_here, field, arrivals, loaded = refs
    owners, own_slots, features = keys.shape
    slots = owners * own_slots
    images, positions, _ = blocks[0].shape

    def copies(b):
        return [
            pltpu.make_async_copy(
                block.at[b], field.at[b, k * positions : (k + 1) * positions], arrivals.at[b, k]
            )
            for k, block in enumerate(blocks)
        ]

    for b in range(images):
        for copy in copies(b):
            copy.start()
    load = pltpu.make_async_copy(first, first_here, loaded)
    load.start()

    def one(b, carry):
        for copy in copies(b):
            copy.wait()
        values = lax.dot_general(
            keys[...].reshape(slots, features),
            field[b],
            (((1,), (1,)), ((), ())),
            preferred_element_type=jnp.float32,
        )
        logits[b] = values
        row_top = jnp.max(values, axis=0, keepdims=True)
        row_total = jnp.sum(jnp.exp(values - row_top), axis=0, keepdims=True)
        row_stats = jnp.concatenate([row_top, row_total], axis=0)
        for k, out in enumerate((s0, s1, s2, s3)):
            out[b] = row_stats[:, k * positions : (k + 1) * positions]
        top = jnp.max(values, axis=1, keepdims=True).astype(jnp.bfloat16).astype(jnp.float32)
        raised = jnp.exp(values - top)
        rest = jnp.sum(raised, axis=1, keepdims=True)
        lane = lax.broadcasted_iota(jnp.int32, (slots, LANES), 1)
        stats = jnp.where(lane == 0, top, 0.0)
        for k in (1, 2, 3):
            piece = rest.astype(jnp.bfloat16).astype(jnp.float32)
            stats = jnp.where(lane == k, piece, stats)
            rest = rest - piece
        stats = stats.astype(jnp.bfloat16).reshape(owners, own_slots, LANES)
        sums = jnp.dot(
            raised.astype(jnp.bfloat16), field[b], preferred_element_type=jnp.float32
        ).astype(jnp.bfloat16)
        sums = sums.reshape(owners, own_slots, features)
        for k in range(owners):
            message[k, b, :, features:] = stats[k]
            message[k, b, :, :features] = sums[k]
        return carry

    lax.fori_loop(0, images, one, 0)
    load.wait()


def dispatch(keys, first, blocks):
    owners, own_slots, features = keys.shape
    images, positions, _ = blocks[0].shape
    slots, width = owners * own_slots, len(blocks) * positions
    return pl.pallas_call(
        dispatch_kernel,
        out_shape=(
            jax.ShapeDtypeStruct((owners, images, own_slots, features + LANES), jnp.bfloat16),
            jax.ShapeDtypeStruct((images, slots, width), jnp.float32),
            *(jax.ShapeDtypeStruct((images, 2, positions), jnp.float32) for _ in blocks),
            jax.ShapeDtypeStruct(first.shape, first.dtype),
        ),
        in_specs=[VMEM] + [ANY] * (1 + len(blocks)),
        out_specs=(VMEM,) * (3 + len(blocks)),
        scratch_shapes=[
            pltpu.VMEM((images, width, features), jnp.bfloat16),
            pltpu.SemaphoreType.DMA((images, len(blocks))),
            pltpu.SemaphoreType.DMA,
        ],
        cost_estimate=pl.CostEstimate(
            flops=4 * images * slots * width * features,
            bytes_accessed=4 * images * slots * features,
            transcendentals=2 * images * slots * width,
        ),
        compiler_params=pltpu.CompilerParams(vmem_limit_bytes=32 * 1024 * 1024),
        name="dispatch",
    )(keys, first, *blocks)


def merge_kernel(arrived, inputs):
    owners, images, _, _ = arrived.shape
    features = inputs.shape[2]
    for b in range(images):
        tops, totals = [], []
        for k in range(owners):
            stats = arrived[k, b, :, features:].astype(jnp.float32)
            tops.append(stats[:, 0:1])
            totals.append(stats[:, 1:2] + stats[:, 2:3] + stats[:, 3:4])
        peak = functools.reduce(jnp.maximum, tops)
        scales = [jnp.exp(top - peak) for top in tops]
        whole = sum(scale * total for scale, total in zip(scales, totals))
        summed = sum(
            (scales[k] / whole) * arrived[k, b, :, :features].astype(jnp.float32)
            for k in range(owners)
        )
        inputs[b] = summed.astype(jnp.bfloat16)


def merge(arrived):
    _, images, own_slots, width = arrived.shape
    return pl.pallas_call(
        merge_kernel,
        out_shape=jax.ShapeDtypeStruct((images, own_slots, width - LANES), jnp.bfloat16),
        in_specs=[VMEM],
        out_specs=VMEM,
        cost_estimate=pl.CostEstimate(
            flops=4 * arrived.size, bytes_accessed=2 * arrived.size, transcendentals=0
        ),
        compiler_params=pltpu.CompilerParams(vmem_limit_bytes=ROOM),
        name="merge",
    )(arrived)


def expert_kernel(rows, first, second, *refs):
    *outs, second_here, loaded = refs
    rank = lax.axis_index("dp")
    experts = first.shape[0]
    images, own_slots, _ = outs[0].shape
    per_expert = own_slots // experts

    def load(expert):
        return pltpu.make_async_copy(second.at[expert], second_here.at[expert], loaded.at[expert])

    for expert in range(experts):
        load(expert).start()

    def one(expert, carry):
        cut = pl.ds(pl.multiple_of(expert * per_expert, per_expert), per_expert)
        taken = [
            rows[(rank ^ k) * images + b, cut, :]
            for k in range(len(outs))
            for b in range(images)
        ]
        hidden = jnp.dot(
            jnp.concatenate(taken, axis=0), first[expert], preferred_element_type=jnp.float32
        )
        hidden = jax.nn.gelu(hidden, approximate=True).astype(jnp.bfloat16)
        load(expert).wait()
        result = jnp.dot(hidden, second_here[expert], preferred_element_type=jnp.float32)
        for k, out in enumerate(outs):
            for b in range(images):
                at = (k * images + b) * per_expert
                out[b, cut, :] = result[at : at + per_expert].astype(out.dtype)
        return carry

    lax.fori_loop(0, experts, one, 0)


def run_experts(rows, expert_in, expert_out, ranks):
    images, own_slots = rows.shape[0] // ranks, rows.shape[1]
    shape = (images, own_slots, rows.shape[2])
    kinds = (jnp.float32, *(jnp.bfloat16 for _ in range(ranks - 1)))
    return pl.pallas_call(
        expert_kernel,
        out_shape=[jax.ShapeDtypeStruct(shape, kind) for kind in kinds],
        in_specs=[VMEM, VMEM, ANY],
        out_specs=[VMEM] * ranks,
        scratch_shapes=[
            pltpu.VMEM(expert_out.shape, expert_out.dtype),
            pltpu.SemaphoreType.DMA((expert_out.shape[0],)),
        ],
        cost_estimate=pl.CostEstimate(
            flops=4 * rows.size * expert_in.shape[2],
            bytes_accessed=4 * expert_in.size,
            transcendentals=rows.size,
        ),
        compiler_params=pltpu.CompilerParams(vmem_limit_bytes=ROOM),
        name="experts",
    )(rows, expert_in, expert_out)


def spread_kernel(own, first, second, third, copies):
    total = own[...]
    for piece in (first, second, third):
        total = total + piece[...].astype(jnp.float32)
    total = total.astype(jnp.bfloat16)
    for k in range(copies.shape[0]):
        copies[k] = total


def spread(own, pieces, count):
    return pl.pallas_call(
        spread_kernel,
        out_shape=jax.ShapeDtypeStruct((count, *own.shape), jnp.bfloat16),
        in_specs=[VMEM] * 4,
        out_specs=VMEM,
        cost_estimate=pl.CostEstimate(
            flops=4 * own.size, bytes_accessed=2 * count * own.size, transcendentals=0
        ),
        compiler_params=pltpu.CompilerParams(vmem_limit_bytes=ROOM),
        name="spread",
    )(own, *pieces)


def combine_kernel(logits, everyone, *refs):
    stats, outs = refs[:4], refs[4:]
    images, positions, _ = outs[0].shape
    owners = everyone.shape[0]

    def one(b, carry):
        outputs = jnp.concatenate([everyone[k, b] for k in range(owners)], axis=0)
        for r in (3, 1, 2, 0):
            values = logits[b, :, r * positions : (r + 1) * positions]
            mix = jnp.exp(values - stats[r][b][0:1]).astype(jnp.bfloat16)
            outs[r][b] = lax.dot_general(
                mix, outputs, (((0,), (0,)), ((), ())), preferred_element_type=jnp.float32
            ).astype(outs[r].dtype)
        return carry

    lax.fori_loop(0, images, one, 0)


def combine(logits, everyone, stats):
    images, slots, width = logits.shape
    shape = (images, width // len(stats), everyone.shape[3])
    kinds = (jnp.float32, jnp.bfloat16, jnp.bfloat16, jnp.bfloat16)
    return pl.pallas_call(
        combine_kernel,
        out_shape=[jax.ShapeDtypeStruct(shape, kind) for kind in kinds],
        in_specs=[VMEM] * (2 + len(stats)),
        out_specs=(VMEM,) * len(kinds),
        cost_estimate=pl.CostEstimate(
            flops=2 * images * slots * width * shape[2],
            bytes_accessed=4 * images * slots * width,
            transcendentals=images * slots * width,
        ),
        compiler_params=pltpu.CompilerParams(vmem_limit_bytes=ROOM),
        name="combine",
    )(logits, everyone, *stats)


def finish_kernel(*refs):
    parts, stats, out = refs[:4], refs[4:8], refs[8]
    images, positions, _ = out.shape
    for b in range(images):
        tops = [s[b][0:1] for s in stats]
        highest = functools.reduce(jnp.maximum, tops)
        scales = [jnp.exp(top - highest) for top in tops]
        total = sum(scale * s[b][1:2] for scale, s in zip(scales, stats))
        shares = [scale / total for scale in scales]
        shares = jnp.concatenate(shares + [jnp.zeros((LANES - 4, positions), jnp.float32)], axis=0)
        shares = shares.T
        joined = sum(
            shares[:, k : k + 1] * part[b].astype(jnp.float32) for k, part in enumerate(parts)
        )
        out[b] = joined.astype(out.dtype)


def finish(parts, stats):
    shape = parts[0].shape
    return pl.pallas_call(
        finish_kernel,
        out_shape=jax.ShapeDtypeStruct(shape, jnp.bfloat16),
        in_specs=[VMEM] * 8,
        out_specs=VMEM,
        cost_estimate=pl.CostEstimate(
            flops=8 * parts[0].size, bytes_accessed=12 * parts[0].size, transcendentals=0
        ),
        compiler_params=pltpu.CompilerParams(vmem_limit_bytes=ROOM),
        name="finish",
    )(*parts, *stats)


def shards(tokens, slot_keys, expert_in, expert_out):
    ranks = lax.axis_size("dp")
    owners = len(TILE[0])
    near = [ahead(tokens, X, 1), ahead(tokens, X, 3), ahead(tokens, Z, 1)]
    keys = all_to_all(jnp.broadcast_to(slot_keys.T, (owners, *slot_keys.shape[::-1])))
    message, logits, *stats, first = dispatch(keys, expert_in, [tokens, *near])
    arrived = all_to_all(message)
    rows = lax.all_gather(merge(arrived), "dp", axis=0, tiled=True)
    away, rows = lax.optimization_barrier((stats[1:], rows))
    back = [ahead(away[0], X, 3), ahead(away[1], X, 1), ahead(away[2], Z, 3)]
    own, *pieces = run_experts(rows, first, expert_out, ranks)
    pieces = [swapped(piece, "dp", k) for k, piece in zip((1, 2, 3), pieces)]
    pieces, back = lax.optimization_barrier((pieces, back))
    everyone = all_to_all(spread(own, pieces, owners))
    own, right, left, up = combine(logits, everyone, stats)
    parts = [own, ahead(right, X, 3), ahead(left, X, 1), ahead(up, Z, 3)]
    return finish(parts, [stats[0], *back])


def solution(mesh):
    split = Mesh(mesh.devices.reshape(4, 4, 2, mesh.shape["dp"]), (X, Z, Y, "dp"))
    return jax.shard_map(
        shards,
        mesh=split,
        in_specs=(P("dp", SLOT, None), P(None, SLOT), P(SLOT, None, "dp"), P(SLOT, "dp", None)),
        out_specs=P("dp", SLOT, None),
        check_vma=False,
    )
```

time: 155 us -> 146 us (0.942)
  blocking collectives: 63.9 us -> 91.4 us
  waiting for transfers between devices: 42.3 us -> 25.4 us
  starting transfers between devices: 29.3 us -> 15.9 us
  local copies, waits for them, and re-layouts: 3.03 us -> 0.9 us
  Pallas kernels: 14.5 us -> 12.6 us
    all_to_all x2 -> x3, blocking collectives: 56.1 us -> 83.6 us  [all_to_all(): lax.all_to_all(array, SLOT, split_axis=0, concat_axis=0, axis_index_group...]
    ppermute x15 -> x9, waiting for transfers between devices: 42.2 us -> 25.3 us  [ahead(): lax.ppermute(array, axis, [((i + step) % size, i) for i in range(size)])]
    all_to_all x1 -> x0, starting transfers between devices: 8.07 us -> none  [all_to_all(): return lax.all_to_all(array, axis, split_axis=0, concat_axis=0, tiled=True)]
    ppermute x15 -> x9, starting transfers between devices: 19.3 us -> 13.9 us  [ahead(): lax.ppermute(array, axis, [((i + step) % size, i) for i in range(size)])]
    pallas_call x1, Pallas kernels: 8.57 us -> 3.87 us  [dispatch(): pl.pallas_call(dispatch_kernel, out_shape=(jax.ShapeDtypeStruct((owners,...]
    slice x1 -> x0, local copies, waits for them, and re-layouts: 2.17 us -> none  [shards(): low, high = (tokens[:, :half], tokens[:, half:])]
    pallas_call x1 -> x2, Pallas kernels: 1.5 us -> 3.18 us  [the longest x1 1.74 us: finish(): pl.pallas_call(finish_kernel, out_shape=jax.ShapeDtypeStruct(shape, jnp.b...]
  transfers between devices with their start and end apart: 19 -> 12, of which waited for: 11 -> 4; matrix products, arithmetic and copies ran while one was open for 1% -> 1% of each run, Pallas kernels for 0% -> 0%
where the time goes in v3:
time: 146 us
  blocking collectives  91.4 us (63%)
  waiting for transfers between devices  25.4 us (17%)
  starting transfers between devices  15.9 us (11%)
  Pallas kernels  12.6 us (9%)
    all_to_all x3, blocking collectives, all_to_all(): lax.all_to_all(array, SLOT, split_axis=0, concat_axis=0, axis_index_group...  83.6 us
    ppermute x9, waiting for transfers between devices, ahead(): lax.ppermute(array, axis, [((i + step) % size, i) for i in range(size)])  25.3 us
    ppermute x9, starting transfers between devices, ahead(): lax.ppermute(array, axis, [((i + step) % size, i) for i in range(size)])  13.9 us
    all_gather x1, blocking collectives, shards(): rows = lax.all_gather(merge(arrived), 'dp', axis=0, tiled=True)  7.78 us
    pallas_call x1, Pallas kernels, run_experts(): pl.pallas_call(expert_kernel, out_shape=[jax.ShapeDtypeStruct(shape, kind...  4.6 us
    pallas_call x1, Pallas kernels, dispatch(): pl.pallas_call(dispatch_kernel, out_shape=(jax.ShapeDtypeStruct((owners,...  3.87 us
  transfers between devices with their start and end apart: 12, of which 4 were waited for; matrix products, arithmetic and copies ran while one was open for 1% of the time, Pallas kernels for 0%

profile of v3, /device:TPU:0, one launch (start us, length us, event | category | flops | bytes accessed | tf_op | source)
XLA Modules:
  0.0 146.1 jit_solution(4001073316145504255)
XLA Ops:
  0.0 0.0 copy-start
  0.0 1.6 %collective-permute-start.1 = (bf16[3,128,1024]{2,1,0:T(8,128)(2,1)}, bf16[3,128,1024]{2,1,0:T(8,128)(2,1)S(1)}, u32[]{:S(2)}, u32[]{:S(2)}) collective-permute-start(bf16[3,128,1024]{2,1,0:T(8,128)(2,1)} %refs_0_.1), channel_id=1, source_target_pairs={{96,0},{0,32},{32,64},{64,96},{97,1},{1,33},{33,65},{65,97},{98,2}... | collective-permute-start | bytes 2359304 | tf_op jit(solution)/shard_map/ppermute | solution.py:26
  1.6 1.6 %collective-permute-start = (bf16[3,128,1024]{2,1,0:T(8,128)(2,1)}, bf16[3,128,1024]{2,1,0:T(8,128)(2,1)S(1)}, u32[]{:S(2)}, u32[]{:S(2)}) collective-permute-start(bf16[3,128,1024]{2,1,0:T(8,128)(2,1)} %refs_0_.1), channel_id=1, source_target_pairs={{32,0},{64,32},{96,64},{0,96},{33,1},{65,33},{97,65},{1,97},{34,2}... | collective-permute-start | bytes 2359304 | tf_op jit(solution)/shard_map/ppermute | solution.py:26
  3.2 4.1 %collective-permute-start.2 = (bf16[3,128,1024]{2,1,0:T(8,128)(2,1)}, bf16[3,128,1024]{2,1,0:T(8,128)(2,1)S(1)}, u32[]{:S(2)}, u32[]{:S(2)}) collective-permute-start(bf16[3,128,1024]{2,1,0:T(8,128)(2,1)} %refs_0_.1), channel_id=1, source_target_pairs={{8,0},{16,8},{24,16},{0,24},{9,1},{17,9},{25,17},{1,25},{10,2},{18... | collective-permute-start | bytes 2359304 | tf_op jit(solution)/shard_map/ppermute | solution.py:26
  7.4 0.9 broadcast_in_dim.3
  8.3 0.0 slice-start
  8.3 24.9 %all_to_all.15.keys = bf16[8,32,1024]{2,1,0:T(8,128)(2,1)S(1)} all-to-all(bf16[8,32,1024]{2,1,0:T(8,128)(2,1)S(1)} %broadcast_in_dim.3), channel_id=1, replica_groups={{0,4,16,20,72,76,88,92},{32,36,48,52,104,108,120,124},{8,12,24,28,64,68..., dimensions={0} | all-to-all | bytes 1048576 | tf_op jit(solution)/shard_map/all_to_all | solution.py:35
  33.2 0.0 slice-start.1
  33.2 0.0 collective-permute-done.1.refs_2_
  33.2 0.0 collective-permute-done.refs_1_
  33.2 0.0 collective-permute-done.2.refs_3_
  33.2 0.0 copy-done
  33.2 3.9 %dispatch.1 = (bf16[8,3,32,1152]{3,2,1,0:T(8,128)(2,1)S(1)}, f32[3,256,512]{2,1,0:T(8,128)S(1)}, f32[3,2,128]{2,1,0:T(2,128)S(1)}, f32[3,2,128]{2,1,0:T(2,128)S(...) custom-call(bf16[8,32,1024]{2,1,0:T(8,128)(2,1)S(1)} %all_to_all.15.keys, ...), custom_call_target="tpu_custom_call" | custom-call | flops 1610612736 | bytes 3145728 | tf_op jit(solution)/shard_map/dispatch/pallas_call | solution.py:102
  37.1 30.4 %all_to_all.16.arrived = bf16[8,3,32,1152]{3,2,1,0:T(8,128)(2,1)S(1)} all-to-all(bf16[8,3,32,1152]{3,2,1,0:T(8,128)(2,1)S(1)} %get-tuple-element.34), channel_id=1, replica_groups={{0,4,16,20,72,76,88,92},{32,36,48,52,104,108,120,124},{8,12,24,28,64,68..., dimensions={0} | all-to-all | bytes 3538944 | tf_op jit(solution)/shard_map/all_to_all | solution.py:35
  67.5 0.8 merge.1
  68.3 7.8 %all_gather.3.rows = bf16[12,32,1024]{2,1,0:T(8,128)(2,1)S(1)} all-gather(bf16[3,32,1024]{2,1,0:T(8,128)(2,1)S(1)} %merge.1), channel_id=1, replica_groups=mesh['slot_0'=4,'slot_1'=4,'slot_2'=2,'dp'=4] {'dp'}, dimensions={0}, use_global_device_ids=true | all-gather | bytes 983040 | tf_op jit(solution)/shard_map/all_gather | solution.py:318
  76.1 0.0 slice-done
  76.1 0.0 slice-done.1
  76.1 4.6 %experts.1 = (f32[3,32,1024]{2,1,0:T(8,128)S(1)}, bf16[3,32,1024]{2,1,0:T(8,128)(2,1)S(1)}, bf16[3,32,1024]{2,1,0:T(8,128)(2,1)S(1)}, bf16[3,32,1024]{2,1,0:T(8,128)(2,1)S(1)}) custom-call(bf16[12,32,1024]{2,1,0:T(8,128)(2,1)S(1)} %all_gather.3.rows, bf16[4,1024,1024]{2,1,0:T(8,128)(2,1)S(1)} %get-tuple-element.36.first, bf16[4,1024,1024]{2,1,0:T(8,128)(2,1)S(1)} %bitcast.2), custom_call_target="tpu_custom_call" | custom-call | flops 1610612736 | bytes 16777216 | tf_op jit(solution)/shard_map/experts/pallas_call | solution.py:200
  80.7 0.4 collective-permute-start.3
  81.1 1.4 collective-permute-start.4
  82.5 0.2 collective-permute-start.5
  82.6 0.7 collective-permute-start.6
  83.3 2.5 %collective-permute-start.7 = (f32[3,2,128]{2,1,0:T(2,128)S(1)}, f32[3,2,128]{2,1,0:T(2,128)S(1)}, u32[]{:S(2)}, u32[]{:S(2)}) collective-permute-start(f32[3,2,128]{2,1,0:T(2,128)S(1)} %get-tuple-element.42.refs_2_), channel_id=1, source_target_pairs={{32,0},{64,32},{96,64},{0,96},{33,1},{65,33},{97,65},{1,97},{34,2}... | collective-permute-start | bytes 9224 | tf_op jit(solution)/shard_map/ppermute | solution.py:26
  85.9 1.6 %collective-permute-done.6.refs_5_ = f32[3,2,128]{2,1,0:T(2,128)S(1)} collective-permute-done((f32[3,2,128]{2,1,0:T(2,128)S(1)}, f32[3,2,128]{2,1,0:T(2,128)S(1)}, u32[]{:S(2)}, u32[]{:S(2)}) %collective-permute-start.6) | collective-permute-done | bytes 3104 | tf_op jit(solution)/shard_map/ppermute | solution.py:26
  87.4 0.0 collective-permute-start.8
  87.4 0.0 collective-permute-done.7.refs_6_
  87.4 4.8 %collective-permute-done.8.refs_7_ = f32[3,2,128]{2,1,0:T(2,128)S(1)} collective-permute-done((f32[3,2,128]{2,1,0:T(2,128)S(1)}, f32[3,2,128]{2,1,0:T(2,128)S(1)}, u32[]{:S(2)}, u32[]{:S(2)}) %collective-permute-start.8) | collective-permute-done | bytes 3104 | tf_op jit(solution)/shard_map/ppermute | solution.py:26
  92.2 0.0 collective-permute-done.3.first
  92.3 0.0 collective-permute-done.4.second
  92.3 0.0 collective-permute-done.5.third
  92.3 0.1 spread.1
  92.4 28.3 %all_to_all.17.everyone = bf16[8,3,32,1024]{3,2,1,0:T(8,128)(2,1)S(1)} all-to-all(bf16[8,3,32,1024]{3,2,1,0:T(8,128)(2,1)S(1)} %spread.1), channel_id=1, replica_groups={{0,4,16,20,72,76,88,92},{32,36,48,52,104,108,120,124},{8,12,24,28,64,68..., dimensions={0} | all-to-all | bytes 3145728 | tf_op jit(solution)/shard_map/all_to_all | solution.py:35
  120.7 1.4 combine.1
  122.1 0.7 collective-permute-start.9
  122.9 2.6 %collective-permute-start.10 = (bf16[3,128,1024]{2,1,0:T(8,128)(2,1)S(1)}, bf16[3,128,1024]{2,1,0:T(8,128)(2,1)S(1)}, u32[]{:S(2)}, u32[]{:S(2)}) collective-permute-start(bf16[3,128,1024]{2,1,0:T(8,128)(2,1)S(1)} %get-tuple-element.50), channel_id=1, source_target_pairs={{32,0},{64,32},{96,64},{0,96},{33,1},{65,33},{97,65},{1,97},{34,2}... | collective-permute-start | bytes 2359304 | tf_op jit(solution)/shard_map/ppermute | solution.py:26
  125.4 0.0 collective-permute-start.11
  125.4 16.3 %collective-permute-done.9.refs_1_ = bf16[3,128,1024]{2,1,0:T(8,128)(2,1)S(1)} collective-permute-done((bf16[3,128,1024]{2,1,0:T(8,128)(2,1)S(1)}, bf16[3,128,1024]{2,1,0:T(8,128)(2,1)S(1)}, u32[]{:S(2)}, u32[]{:S(2)}) %collective-permute-start.9) | collective-permute-done | bytes 786464 | tf_op jit(solution)/shard_map/ppermute | solution.py:26
  141.7 0.0 collective-permute-done.10.refs_2_
  141.7 2.7 %collective-permute-done.11.refs_3_ = bf16[3,128,1024]{2,1,0:T(8,128)(2,1)S(1)} collective-permute-done((bf16[3,128,1024]{2,1,0:T(8,128)(2,1)S(1)}, bf16[3,128,1024]{2,1,0:T(8,128)(2,1)S(1)}, u32[]{:S(2)}, u32[]{:S(2)}) %collective-permute-start.11) | collective-permute-done | bytes 786464 | tf_op jit(solution)/shard_map/ppermute | solution.py:26
  144.4 1.7 %finish.1 = bf16[3,128,1024]{2,1,0:T(8,128)(2,1)} custom-call(f32[3,128,1024]{2,1,0:T(8,128)S(1)} %get-tuple-element.48.refs_0_, bf16[3,128,1024]{2,1,0:T(8,128)(2,1)S(1)} %collective-permute-done.9.refs_1_, bf16[3,128,1024]{2,1,0:T(8,128)(2,1)S(1)} %collective-permute-done.10.refs_2_, bf16[3,128,1024]{2,1,0:T(8,128)(2,1)S(1)} %collective-permute-done.11.refs_3_, ...), custom_call_target="tpu_custom_call" | custom-call | flops 3145728 | bytes 4718592 | tf_op jit(solution)/shard_map/finish/pallas_call | solution.py:298
  (1 shorter events, 0.0 us)
Async XLA Ops:
  0.0 33.2 %copy-start = (bf16[3,128,1024]{2,1,0:T(8,128)(2,1)S(1)}, bf16[3,128,1024]{2,1,0:T(8,128)(2,1)}, u32[]{:S(2)}) copy-start(bf16[3,128,1024]{2,1,0:T(8,128)(2,1)} %refs_0_.1) | copy-start | bytes 2359300
  0.0 33.2 %collective-permute-start.1 = (bf16[3,128,1024]{2,1,0:T(8,128)(2,1)}, bf16[3,128,1024]{2,1,0:T(8,128)(2,1)S(1)}, u32[]{:S(2)}, u32[]{:S(2)}) collective-permute-start(bf16[3,128,1024]{2,1,0:T(8,128)(2,1)} %refs_0_.1), channel_id=1, source_target_pairs={{96,0},{0,32},{32,64},{64,96},{97,1},{1,33},{33,65},{65,97},{98,2}... | collective-permute-start | bytes 2359304 | tf_op jit(solution)/shard_map/ppermute | solution.py:26
  1.6 31.6 %collective-permute-start = (bf16[3,128,1024]{2,1,0:T(8,128)(2,1)}, bf16[3,128,1024]{2,1,0:T(8,128)(2,1)S(1)}, u32[]{:S(2)}, u32[]{:S(2)}) collective-permute-start(bf16[3,128,1024]{2,1,0:T(8,128)(2,1)} %refs_0_.1), channel_id=1, source_target_pairs={{32,0},{64,32},{96,64},{0,96},{33,1},{65,33},{97,65},{1,97},{34,2}... | collective-permute-start | bytes 2359304 | tf_op jit(solution)/shard_map/ppermute | solution.py:26
  3.2 29.9 %collective-permute-start.2 = (bf16[3,128,1024]{2,1,0:T(8,128)(2,1)}, bf16[3,128,1024]{2,1,0:T(8,128)(2,1)S(1)}, u32[]{:S(2)}, u32[]{:S(2)}) collective-permute-start(bf16[3,128,1024]{2,1,0:T(8,128)(2,1)} %refs_0_.1), channel_id=1, source_target_pairs={{8,0},{16,8},{24,16},{0,24},{9,1},{17,9},{25,17},{1,25},{10,2},{18... | collective-permute-start | bytes 2359304 | tf_op jit(solution)/shard_map/ppermute | solution.py:26
  8.3 67.8 %slice-start = ((s8[8388608]{0:T(1024)(128)(4,1)}), s8[4194304]{0:T(1024)(128)(4,1)S(1)}, s32[]{:S(2)}) async-start(s8[8388608]{0:T(1024)(128)(4,1)} %bitcast.1), calls=%async_computation.3 | async-start | bytes 8388608
  33.2 42.9 %slice-start.1 = ((s8[8388608]{0:T(1024)(128)(4,1)}), s8[4194304]{0:T(1024)(128)(4,1)S(1)}, s32[]{:S(2)}) async-start(s8[8388608]{0:T(1024)(128)(4,1)} %bitcast.1), calls=%async_computation.4 | async-start | bytes 8388608
  80.7 11.6 %collective-permute-start.3 = (bf16[3,32,1024]{2,1,0:T(8,128)(2,1)S(1)}, bf16[3,32,1024]{2,1,0:T(8,128)(2,1)S(1)}, u32[]{:S(2)}, u32[]{:S(2)}) collective-permute-start(bf16[3,32,1024]{2,1,0:T(8,128)(2,1)S(1)} %get-tuple-element.38), channel_id=1, source_target_pairs={{0,1},{1,0},{2,3},{3,2},{4,5},{5,4},{6,7},{7,6},{8,9},{9,8},{10,11... | collective-permute-start | bytes 589832 | tf_op jit(solution)/shard_map/ppermute | solution.py:31
  81.1 11.1 %collective-permute-start.4 = (bf16[3,32,1024]{2,1,0:T(8,128)(2,1)S(1)}, bf16[3,32,1024]{2,1,0:T(8,128)(2,1)S(1)}, u32[]{:S(2)}, u32[]{:S(2)}) collective-permute-start(bf16[3,32,1024]{2,1,0:T(8,128)(2,1)S(1)} %get-tuple-element.39), channel_id=1, source_target_pairs={{0,2},{1,3},{2,0},{3,1},{4,6},{5,7},{6,4},{7,5},{8,10},{9,11},{10,... | collective-permute-start | bytes 589832 | tf_op jit(solution)/shard_map/ppermute | solution.py:31
  82.5 9.8 %collective-permute-start.5 = (bf16[3,32,1024]{2,1,0:T(8,128)(2,1)S(1)}, bf16[3,32,1024]{2,1,0:T(8,128)(2,1)S(1)}, u32[]{:S(2)}, u32[]{:S(2)}) collective-permute-start(bf16[3,32,1024]{2,1,0:T(8,128)(2,1)S(1)} %get-tuple-element.40), channel_id=1, source_target_pairs={{0,3},{1,2},{2,1},{3,0},{4,7},{5,6},{6,5},{7,4},{8,11},{9,10},{10,... | collective-permute-start | bytes 589832 | tf_op jit(solution)/shard_map/ppermute | solution.py:31
  82.6 4.8 %collective-permute-start.6 = (f32[3,2,128]{2,1,0:T(2,128)S(1)}, f32[3,2,128]{2,1,0:T(2,128)S(1)}, u32[]{:S(2)}, u32[]{:S(2)}) collective-permute-start(f32[3,2,128]{2,1,0:T(2,128)S(1)} %get-tuple-element.41.refs_1_), channel_id=1, source_target_pairs={{96,0},{0,32},{32,64},{64,96},{97,1},{1,33},{33,65},{65,97},{98,2}... | collective-permute-start | bytes 9224 | tf_op jit(solution)/shard_map/ppermute | solution.py:26
  83.3 4.1 %collective-permute-start.7 = (f32[3,2,128]{2,1,0:T(2,128)S(1)}, f32[3,2,128]{2,1,0:T(2,128)S(1)}, u32[]{:S(2)}, u32[]{:S(2)}) collective-permute-start(f32[3,2,128]{2,1,0:T(2,128)S(1)} %get-tuple-element.42.refs_2_), channel_id=1, source_target_pairs={{32,0},{64,32},{96,64},{0,96},{33,1},{65,33},{97,65},{1,97},{34,2}... | collective-permute-start | bytes 9224 | tf_op jit(solution)/shard_map/ppermute | solution.py:26
  87.4 4.8 %collective-permute-start.8 = (f32[3,2,128]{2,1,0:T(2,128)S(1)}, f32[3,2,128]{2,1,0:T(2,128)S(1)}, u32[]{:S(2)}, u32[]{:S(2)}) collective-permute-start(f32[3,2,128]{2,1,0:T(2,128)S(1)} %get-tuple-element.43.refs_3_), channel_id=1, source_target_pairs={{24,0},{0,8},{8,16},{16,24},{25,1},{1,9},{9,17},{17,25},{26,2},{2,... | collective-permute-start | bytes 9224 | tf_op jit(solution)/shard_map/ppermute | solution.py:26
  122.1 19.6 %collective-permute-start.9 = (bf16[3,128,1024]{2,1,0:T(8,128)(2,1)S(1)}, bf16[3,128,1024]{2,1,0:T(8,128)(2,1)S(1)}, u32[]{:S(2)}, u32[]{:S(2)}) collective-permute-start(bf16[3,128,1024]{2,1,0:T(8,128)(2,1)S(1)} %get-tuple-element.49), channel_id=1, source_target_pairs={{96,0},{0,32},{32,64},{64,96},{97,1},{1,33},{33,65},{65,97},{98,2}... | collective-permute-start | bytes 2359304 | tf_op jit(solution)/shard_map/ppermute | solution.py:26
  122.9 18.9 %collective-permute-start.10 = (bf16[3,128,1024]{2,1,0:T(8,128)(2,1)S(1)}, bf16[3,128,1024]{2,1,0:T(8,128)(2,1)S(1)}, u32[]{:S(2)}, u32[]{:S(2)}) collective-permute-start(bf16[3,128,1024]{2,1,0:T(8,128)(2,1)S(1)} %get-tuple-element.50), channel_id=1, source_target_pairs={{32,0},{64,32},{96,64},{0,96},{33,1},{65,33},{97,65},{1,97},{34,2}... | collective-permute-start | bytes 2359304 | tf_op jit(solution)/shard_map/ppermute | solution.py:26
  125.4 19.0 %collective-permute-start.11 = (bf16[3,128,1024]{2,1,0:T(8,128)(2,1)S(1)}, bf16[3,128,1024]{2,1,0:T(8,128)(2,1)S(1)}, u32[]{:S(2)}, u32[]{:S(2)}) collective-permute-start(bf16[3,128,1024]{2,1,0:T(8,128)(2,1)S(1)} %get-tuple-element.51), channel_id=1, source_target_pairs={{24,0},{0,8},{8,16},{16,24},{25,1},{1,9},{9,17},{17,25},{26,2},{2,... | collective-permute-start | bytes 2359304 | tf_op jit(solution)/shard_map/ppermute | solution.py:26

commit v4 on v3

--- a/solution.py
+++ b/solution.py
@@ -12,8 +12,13 @@
 X, Z, Y = "slot_0", "slot_1", "slot_2"
 SLOT = (X, Z, Y)
 TILE = tuple(
-    tuple((x * 4 + z) * 2 + y for x in range(4) for z in range(4) if (x + 2 * z) % 4 == r for y in (0, 1))
-    for r in range(4)
+    tuple(((r + 2 * y) % 4 * 4 + z) * 2 + y for y in (0, 1) for z in range(4)) for r in range(4)
+)
+PARTNER = tuple(
+    ((x * 4 + z) * 2 + y, ((x + 2) % 4 * 4 + z) * 2 + 1 - y)
+    for x in range(4)
+    for z in range(4)
+    for y in (0, 1)
 )
 LANES = 128
 ROOM = 24 * 1024 * 1024
@@ -21,6 +26,11 @@
 ANY = pl.BlockSpec(memory_space=pl.ANY)
 
 
+def place(step):
+    y, z = lax.axis_index(Y), lax.axis_index(Z)
+    return ((y + step % 2) % 2) * 4 + (z + step // 2) % 4
+
+
 def ahead(array, axis, step):
     size = lax.axis_size(axis)
     return lax.ppermute(array, axis, [((i + step) % size, i) for i in range(size)])
@@ -37,10 +47,12 @@
     )
 
 
-def dispatch_kernel(keys, first, *refs):
+def dispatch_kernel(first, k0, k1, k2, k3, *refs):
     *blocks, message, logits, s0, s1, s2, s3, first_here, field, arrivals, loaded = refs
-    owners, own_slots, features = keys.shape
+    owners, _, own_slots, _ = message.shape
     slots = owners * own_slots
+    features = k0.shape[1]
+    columns = jnp.concatenate([k0[...], k1[...], k2[...], k3[...]], axis=0)
     images, positions, _ = blocks[0].shape
 
     def copies(b):
@@ -61,7 +73,7 @@
         for copy in copies(b):
             copy.wait()
         values = lax.dot_general(
-            keys[...].reshape(slots, features),
+            columns,
             field[b],
             (((1,), (1,)), ((), ())),
             preferred_element_type=jnp.float32,
@@ -87,17 +99,17 @@
         ).astype(jnp.bfloat16)
         sums = sums.reshape(owners, own_slots, features)
         for k in range(owners):
-            message[k, b, :, features:] = stats[k]
-            message[k, b, :, :features] = sums[k]
+            message[place(k), b, :, features:] = stats[k]
+            message[place(k), b, :, :features] = sums[k]
         return carry
 
     lax.fori_loop(0, images, one, 0)
     load.wait()
 
 
-def dispatch(keys, first, blocks):
-    owners, own_slots, features = keys.shape
-    images, positions, _ = blocks[0].shape
+def dispatch(keys, first, blocks, own_slots):
+    images, positions, features = blocks[0].shape
+    owners = sum(key.shape[0] for key in keys) // own_slots
     slots, width = owners * own_slots, len(blocks) * positions
     return pl.pallas_call(
         dispatch_kernel,
@@ -107,7 +119,7 @@
             *(jax.ShapeDtypeStruct((images, 2, positions), jnp.float32) for _ in blocks),
             jax.ShapeDtypeStruct(first.shape, first.dtype),
         ),
-        in_specs=[VMEM] + [ANY] * (1 + len(blocks)),
+        in_specs=[ANY] + [VMEM] * len(keys) + [ANY] * len(blocks),
         out_specs=(VMEM,) * (3 + len(blocks)),
         scratch_shapes=[
             pltpu.VMEM((images, width, features), jnp.bfloat16),
@@ -121,7 +133,7 @@
         ),
         compiler_params=pltpu.CompilerParams(vmem_limit_bytes=32 * 1024 * 1024),
         name="dispatch",
-    )(keys, first, *blocks)
+    )(first, *keys, *blocks)
 
 
 def merge_kernel(arrived, inputs):
@@ -245,7 +257,7 @@
     owners = everyone.shape[0]
 
     def one(b, carry):
-        outputs = jnp.concatenate([everyone[k, b] for k in range(owners)], axis=0)
+        outputs = jnp.concatenate([everyone[place(k), b] for k in range(owners)], axis=0)
         for r in (3, 1, 2, 0):
             values = logits[b, :, r * positions : (r + 1) * positions]
             mix = jnp.exp(values - stats[r][b][0:1]).astype(jnp.bfloat16)
@@ -311,19 +323,22 @@
 def shards(tokens, slot_keys, expert_in, expert_out):
     ranks = lax.axis_size("dp")
     owners = len(TILE[0])
-    near = [ahead(tokens, X, 1), ahead(tokens, X, 3), ahead(tokens, Z, 1)]
-    keys = all_to_all(jnp.broadcast_to(slot_keys.T, (owners, *slot_keys.shape[::-1])))
-    message, logits, *stats, first = dispatch(keys, expert_in, [tokens, *near])
+    pair = lax.ppermute(slot_keys.T, SLOT, PARTNER)
+    near = [ahead(tokens, X, 1), ahead(tokens, X, 3), ahead(tokens, Y, 1)]
+    pair = jnp.concatenate([slot_keys.T, pair], axis=0)
+    keys = [pair, *(ahead(pair, Z, k) for k in (1, 2, 3))]
+    message, logits, *stats, first = dispatch(
+        keys, expert_in, [tokens, *near], slot_keys.shape[1]
+    )
     arrived = all_to_all(message)
     rows = lax.all_gather(merge(arrived), "dp", axis=0, tiled=True)
-    away, rows = lax.optimization_barrier((stats[1:], rows))
-    back = [ahead(away[0], X, 3), ahead(away[1], X, 1), ahead(away[2], Z, 3)]
     own, *pieces = run_experts(rows, first, expert_out, ranks)
     pieces = [swapped(piece, "dp", k) for k, piece in zip((1, 2, 3), pieces)]
+    back = [ahead(stats[1], X, 3), ahead(stats[2], X, 1), ahead(stats[3], Y, 1)]
     pieces, back = lax.optimization_barrier((pieces, back))
     everyone = all_to_all(spread(own, pieces, owners))
     own, right, left, up = combine(logits, everyone, stats)
-    parts = [own, ahead(right, X, 3), ahead(left, X, 1), ahead(up, Z, 3)]
+    parts = [own, ahead(right, X, 3), ahead(left, X, 1), ahead(up, Y, 1)]
     return finish(parts, [stats[0], *back])
 
 

time: 146 us -> 152 us (1.041)
  blocking collectives: 91.4 us -> 65.7 us
  waiting for transfers between devices: 25.4 us -> 47.5 us
  starting transfers between devices: 15.9 us -> 24.3 us
    all_to_all x3 -> x2, blocking collectives: 83.6 us -> 57 us  [all_to_all(): lax.all_to_all(array, SLOT, split_axis=0, concat_axis=0, axis_index_group...]
    ppermute x0 -> x1, waiting for transfers between devices: none -> 17.7 us  [shards(): pair = lax.ppermute(slot_keys.T, SLOT, PARTNER)]
    ppermute x9 -> x12, starting transfers between devices: 13.9 us -> 20.8 us  [ahead(): lax.ppermute(array, axis, [((i + step) % size, i) for i in range(size)])]
    ppermute x9 -> x12, waiting for transfers between devices: 25.3 us -> 29.7 us  [ahead(): lax.ppermute(array, axis, [((i + step) % size, i) for i in range(size)])]
    ppermute x0 -> x1, starting transfers between devices: none -> 1.59 us  [shards(): pair = lax.ppermute(slot_keys.T, SLOT, PARTNER)]
  transfers between devices with their start and end apart: 12 -> 16, of which waited for: 4 -> 8; matrix products, arithmetic and copies ran while one was open for 1% -> 1% of each run, Pallas kernels for 0% -> 0%
where the time goes in v4:
time: 152 us
  blocking collectives  65.7 us (43%)
  waiting for transfers between devices  47.5 us (31%)
  starting transfers between devices  24.3 us (16%)
  Pallas kernels  12.4 us (8%)
    all_to_all x2, blocking collectives, all_to_all(): lax.all_to_all(array, SLOT, split_axis=0, concat_axis=0, axis_index_group...  57 us
    ppermute x12, waiting for transfers between devices, ahead(): lax.ppermute(array, axis, [((i + step) % size, i) for i in range(size)])  29.7 us
    ppermute x12, starting transfers between devices, ahead(): lax.ppermute(array, axis, [((i + step) % size, i) for i in range(size)])  20.8 us
    ppermute x1, waiting for transfers between devices, shards(): pair = lax.ppermute(slot_keys.T, SLOT, PARTNER)  17.7 us
    all_gather x1, blocking collectives, shards(): rows = lax.all_gather(merge(arrived), 'dp', axis=0, tiled=True)  8.68 us
    pallas_call x1, Pallas kernels, run_experts(): pl.pallas_call(expert_kernel, out_shape=[jax.ShapeDtypeStruct(shape, kind...  4.6 us
    pallas_call x1, Pallas kernels, dispatch(): pl.pallas_call(dispatch_kernel, out_shape=(jax.ShapeDtypeStruct((owners,...  3.75 us
  transfers between devices with their start and end apart: 16, of which 8 were waited for; matrix products, arithmetic and copies ran while one was open for 1% of the time, Pallas kernels for 0%

profile of v4, /device:TPU:0, one launch (start us, length us, event | category | flops | bytes accessed | tf_op | source)
XLA Modules:
  0.0 152.1 jit_solution(12624457341346123614)
XLA Ops:
  0.0 1.6 %collective-permute-start.5 = (bf16[3,128,1024]{2,1,0:T(8,128)(2,1)}, bf16[3,128,1024]{2,1,0:T(8,128)(2,1)S(1)}, u32[]{:S(2)}, u32[]{:S(2)}) collective-permute-start(bf16[3,128,1024]{2,1,0:T(8,128)(2,1)} %refs_0_.1), channel_id=1, source_target_pairs={{96,0},{0,32},{32,64},{64,96},{97,1},{1,33},{33,65},{65,97},{98,2}... | collective-permute-start | bytes 2359304 | tf_op jit(solution)/shard_map/ppermute | solution.py:36
  1.6 1.6 %collective-permute-start.4 = (bf16[3,128,1024]{2,1,0:T(8,128)(2,1)}, bf16[3,128,1024]{2,1,0:T(8,128)(2,1)S(1)}, u32[]{:S(2)}, u32[]{:S(2)}) collective-permute-start(bf16[3,128,1024]{2,1,0:T(8,128)(2,1)} %refs_0_.1), channel_id=1, source_target_pairs={{32,0},{64,32},{96,64},{0,96},{33,1},{65,33},{97,65},{1,97},{34,2}... | collective-permute-start | bytes 2359304 | tf_op jit(solution)/shard_map/ppermute | solution.py:36
  3.2 3.3 %collective-permute-start.6 = (bf16[3,128,1024]{2,1,0:T(8,128)(2,1)}, bf16[3,128,1024]{2,1,0:T(8,128)(2,1)S(1)}, u32[]{:S(2)}, u32[]{:S(2)}) collective-permute-start(bf16[3,128,1024]{2,1,0:T(8,128)(2,1)} %refs_0_.1), channel_id=1, source_target_pairs={{4,0},{0,4},{5,1},{1,5},{6,2},{2,6},{7,3},{3,7},{12,8},{8,12},{13,... | collective-permute-start | bytes 2359304 | tf_op jit(solution)/shard_map/ppermute | solution.py:36
  6.5 1.6 %collective-permute-start = (bf16[32,1024]{1,0:T(8,128)(2,1)}, bf16[32,1024]{1,0:T(8,128)(2,1)S(1)}, u32[]{:S(2)}, u32[]{:S(2)}) collective-permute-start(bf16[32,1024]{1,0:T(8,128)(2,1)} %bitcast.3), channel_id=1, source_target_pairs={{0,68},{4,64},{8,76},{12,72},{16,84},{20,80},{24,92},{28,88},{32,1... | collective-permute-start | bytes 196616 | tf_op jit(solution)/shard_map/ppermute | solution.py:326
  8.1 17.7 %collective-permute-done = bf16[32,1024]{1,0:T(8,128)(2,1)S(1)} collective-permute-done((bf16[32,1024]{1,0:T(8,128)(2,1)}, bf16[32,1024]{1,0:T(8,128)(2,1)S(1)}, u32[]{:S(2)}, u32[]{:S(2)}) %collective-permute-start) | collective-permute-done | bytes 65568 | tf_op jit(solution)/shard_map/ppermute | solution.py:326
  25.8 0.0 slice-start
  25.8 1.0 pad_maximum_fusion.k0
  26.8 0.0 slice-start.1
  26.9 2.0 %collective-permute-start.3 = (bf16[64,1024]{1,0:T(8,128)(2,1)S(1)}, bf16[64,1024]{1,0:T(8,128)(2,1)S(1)}, u32[]{:S(2)}, u32[]{:S(2)}) collective-permute-start(bf16[64,1024]{1,0:T(8,128)(2,1)S(1)} %pad_maximum_fusion.k0), channel_id=1, source_target_pairs={{24,0},{0,8},{8,16},{16,24},{25,1},{1,9},{9,17},{17,25},{26,2},{2,... | collective-permute-start | bytes 393224 | tf_op jit(solution)/shard_map/ppermute | solution.py:36
  28.8 3.6 %collective-permute-start.2 = (bf16[64,1024]{1,0:T(8,128)(2,1)S(1)}, bf16[64,1024]{1,0:T(8,128)(2,1)S(1)}, u32[]{:S(2)}, u32[]{:S(2)}) collective-permute-start(bf16[64,1024]{1,0:T(8,128)(2,1)S(1)} %pad_maximum_fusion.k0), channel_id=1, source_target_pairs={{16,0},{24,8},{0,16},{8,24},{17,1},{25,9},{1,17},{9,25},{18,2},{26... | collective-permute-start | bytes 393224 | tf_op jit(solution)/shard_map/ppermute | solution.py:36
  32.4 2.9 %collective-permute-done.3.k3 = bf16[64,1024]{1,0:T(8,128)(2,1)S(1)} collective-permute-done((bf16[64,1024]{1,0:T(8,128)(2,1)S(1)}, bf16[64,1024]{1,0:T(8,128)(2,1)S(1)}, u32[]{:S(2)}, u32[]{:S(2)}) %collective-permute-start.3) | collective-permute-done | bytes 131104 | tf_op jit(solution)/shard_map/ppermute | solution.py:36
  35.3 1.1 collective-permute-start.1
  36.5 0.8 collective-permute-done.2.k2
  37.3 3.0 %collective-permute-done.1.k1 = bf16[64,1024]{1,0:T(8,128)(2,1)S(1)} collective-permute-done((bf16[64,1024]{1,0:T(8,128)(2,1)S(1)}, bf16[64,1024]{1,0:T(8,128)(2,1)S(1)}, u32[]{:S(2)}, u32[]{:S(2)}) %collective-permute-start.1) | collective-permute-done | bytes 131104 | tf_op jit(solution)/shard_map/ppermute | solution.py:36
  40.3 0.0 collective-permute-done.5.refs_2_
  40.3 0.0 collective-permute-done.4.refs_1_
  40.3 0.0 collective-permute-done.6.refs_3_
  40.3 0.0 copy-start
  40.3 1.1 copy-done
  41.4 3.7 %dispatch.1 = (bf16[8,3,32,1152]{3,2,1,0:T(8,128)(2,1)S(1)}, f32[3,256,512]{2,1,0:T(8,128)S(1)}, f32[3,2,128]{2,1,0:T(2,128)S(1)}, f32[3,2,128]{2,1,0:T(2,128)S(...) custom-call(bf16[4,1024,1024]{2,1,0:T(8,128)(2,1)} %first.1, ...), custom_call_target="tpu_custom_call" | custom-call | flops 1610612736 | bytes 3145728 | tf_op jit(solution)/shard_map/dispatch/pallas_call | solution.py:114
  45.2 27.3 %all_to_all.10.arrived = bf16[8,3,32,1152]{3,2,1,0:T(8,128)(2,1)S(1)} all-to-all(bf16[8,3,32,1152]{3,2,1,0:T(8,128)(2,1)S(1)} %get-tuple-element.27), channel_id=1, replica_groups={{0,8,16,24,68,76,84,92},{32,40,48,56,100,108,116,124},{64,72,80,88,4,12..., dimensions={0} | all-to-all | bytes 3538944 | tf_op jit(solution)/shard_map/all_to_all | solution.py:45
  72.5 0.8 merge.1
  73.3 8.7 %all_gather.3.rows = bf16[12,32,1024]{2,1,0:T(8,128)(2,1)S(1)} all-gather(bf16[3,32,1024]{2,1,0:T(8,128)(2,1)S(1)} %merge.1), channel_id=1, replica_groups=mesh['slot_0'=4,'slot_1'=4,'slot_2'=2,'dp'=4] {'dp'}, dimensions={0}, use_global_device_ids=true | all-gather | bytes 983040 | tf_op jit(solution)/shard_map/all_gather | solution.py:334
  82.0 0.0 slice-done
  82.0 0.0 slice-done.1
  82.0 4.6 %experts.1 = (f32[3,32,1024]{2,1,0:T(8,128)S(1)}, bf16[3,32,1024]{2,1,0:T(8,128)(2,1)S(1)}, bf16[3,32,1024]{2,1,0:T(8,128)(2,1)S(1)}, bf16[3,32,1024]{2,1,0:T(8,128)(2,1)S(1)}) custom-call(bf16[12,32,1024]{2,1,0:T(8,128)(2,1)S(1)} %all_gather.3.rows, bf16[4,1024,1024]{2,1,0:T(8,128)(2,1)S(1)} %get-tuple-element.28.first, bf16[4,1024,1024]{2,1,0:T(8,128)(2,1)S(1)} %bitcast.2), custom_call_target="tpu_custom_call" | custom-call | flops 1610612736 | bytes 16777216 | tf_op jit(solution)/shard_map/experts/pallas_call | solution.py:212
  86.6 0.4 collective-permute-start.7
  87.0 0.4 collective-permute-start.8
  87.5 1.1 collective-permute-start.9
  88.5 1.8 %collective-permute-start.10 = (f32[3,2,128]{2,1,0:T(2,128)S(1)}, f32[3,2,128]{2,1,0:T(2,128)S(1)}, u32[]{:S(2)}, u32[]{:S(2)}) collective-permute-start(f32[3,2,128]{2,1,0:T(2,128)S(1)} %get-tuple-element.33.refs_1_), channel_id=1, source_target_pairs={{96,0},{0,32},{32,64},{64,96},{97,1},{1,33},{33,65},{65,97},{98,2}... | collective-permute-start | bytes 9224 | tf_op jit(solution)/shard_map/ppermute | solution.py:36
  90.3 1.5 collective-permute-start.11
  91.8 1.6 %collective-permute-done.10.refs_5_ = f32[3,2,128]{2,1,0:T(2,128)S(1)} collective-permute-done((f32[3,2,128]{2,1,0:T(2,128)S(1)}, f32[3,2,128]{2,1,0:T(2,128)S(1)}, u32[]{:S(2)}, u32[]{:S(2)}) %collective-permute-start.10) | collective-permute-done | bytes 3104 | tf_op jit(solution)/shard_map/ppermute | solution.py:36
  93.3 1.0 collective-permute-start.12
  94.3 0.0 collective-permute-done.11.refs_6_
  94.3 4.1 %collective-permute-done.12.refs_7_ = f32[3,2,128]{2,1,0:T(2,128)S(1)} collective-permute-done((f32[3,2,128]{2,1,0:T(2,128)S(1)}, f32[3,2,128]{2,1,0:T(2,128)S(1)}, u32[]{:S(2)}, u32[]{:S(2)}) %collective-permute-start.12) | collective-permute-done | bytes 3104 | tf_op jit(solution)/shard_map/ppermute | solution.py:36
  98.4 0.0 collective-permute-done.7.first
  98.4 0.0 collective-permute-done.8.second
  98.4 0.0 collective-permute-done.9.third
  98.4 0.1 spread.1
  98.6 29.7 %all_to_all.11.everyone = bf16[8,3,32,1024]{3,2,1,0:T(8,128)(2,1)S(1)} all-to-all(bf16[8,3,32,1024]{3,2,1,0:T(8,128)(2,1)S(1)} %spread.1), channel_id=1, replica_groups={{0,8,16,24,68,76,84,92},{32,40,48,56,100,108,116,124},{64,72,80,88,4,12..., dimensions={0} | all-to-all | bytes 3145728 | tf_op jit(solution)/shard_map/all_to_all | solution.py:45
  128.3 1.4 combine.1
  129.7 1.2 collective-permute-start.13
  130.9 2.1 %collective-permute-start.14 = (bf16[3,128,1024]{2,1,0:T(8,128)(2,1)S(1)}, bf16[3,128,1024]{2,1,0:T(8,128)(2,1)S(1)}, u32[]{:S(2)}, u32[]{:S(2)}) collective-permute-start(bf16[3,128,1024]{2,1,0:T(8,128)(2,1)S(1)} %get-tuple-element.42), channel_id=1, source_target_pairs={{32,0},{64,32},{96,64},{0,96},{33,1},{65,33},{97,65},{1,97},{34,2}... | collective-permute-start | bytes 2359304 | tf_op jit(solution)/shard_map/ppermute | solution.py:36
  133.0 0.0 collective-permute-start.15
  133.1 14.3 %collective-permute-done.13.refs_1_ = bf16[3,128,1024]{2,1,0:T(8,128)(2,1)S(1)} collective-permute-done((bf16[3,128,1024]{2,1,0:T(8,128)(2,1)S(1)}, bf16[3,128,1024]{2,1,0:T(8,128)(2,1)S(1)}, u32[]{:S(2)}, u32[]{:S(2)}) %collective-permute-start.13) | collective-permute-done | bytes 786464 | tf_op jit(solution)/shard_map/ppermute | solution.py:36
  147.4 0.0 collective-permute-done.14.refs_2_
  147.4 3.0 %collective-permute-done.15.refs_3_ = bf16[3,128,1024]{2,1,0:T(8,128)(2,1)S(1)} collective-permute-done((bf16[3,128,1024]{2,1,0:T(8,128)(2,1)S(1)}, bf16[3,128,1024]{2,1,0:T(8,128)(2,1)S(1)}, u32[]{:S(2)}, u32[]{:S(2)}) %collective-permute-start.15) | collective-permute-done | bytes 786464 | tf_op jit(solution)/shard_map/ppermute | solution.py:36
  150.4 1.7 %finish.1 = bf16[3,128,1024]{2,1,0:T(8,128)(2,1)} custom-call(f32[3,128,1024]{2,1,0:T(8,128)S(1)} %get-tuple-element.40.refs_0_, bf16[3,128,1024]{2,1,0:T(8,128)(2,1)S(1)} %collective-permute-done.13.refs_1_, bf16[3,128,1024]{2,1,0:T(8,128)(2,1)S(1)} %collective-permute-done.14.refs_2_, bf16[3,128,1024]{2,1,0:T(8,128)(2,1)S(1)} %collective-permute-done.15.refs_3_, ...), custom_call_target="tpu_custom_call" | custom-call | flops 3145728 | bytes 4718592 | tf_op jit(solution)/shard_map/finish/pallas_call | solution.py:310
  (1 shorter events, 0.0 us)
Async XLA Ops:
  0.0 40.3 %collective-permute-start.5 = (bf16[3,128,1024]{2,1,0:T(8,128)(2,1)}, bf16[3,128,1024]{2,1,0:T(8,128)(2,1)S(1)}, u32[]{:S(2)}, u32[]{:S(2)}) collective-permute-start(bf16[3,128,1024]{2,1,0:T(8,128)(2,1)} %refs_0_.1), channel_id=1, source_target_pairs={{96,0},{0,32},{32,64},{64,96},{97,1},{1,33},{33,65},{65,97},{98,2}... | collective-permute-start | bytes 2359304 | tf_op jit(solution)/shard_map/ppermute | solution.py:36
  1.6 38.7 %collective-permute-start.4 = (bf16[3,128,1024]{2,1,0:T(8,128)(2,1)}, bf16[3,128,1024]{2,1,0:T(8,128)(2,1)S(1)}, u32[]{:S(2)}, u32[]{:S(2)}) collective-permute-start(bf16[3,128,1024]{2,1,0:T(8,128)(2,1)} %refs_0_.1), channel_id=1, source_target_pairs={{32,0},{64,32},{96,64},{0,96},{33,1},{65,33},{97,65},{1,97},{34,2}... | collective-permute-start | bytes 2359304 | tf_op jit(solution)/shard_map/ppermute | solution.py:36
  3.2 37.0 %collective-permute-start.6 = (bf16[3,128,1024]{2,1,0:T(8,128)(2,1)}, bf16[3,128,1024]{2,1,0:T(8,128)(2,1)S(1)}, u32[]{:S(2)}, u32[]{:S(2)}) collective-permute-start(bf16[3,128,1024]{2,1,0:T(8,128)(2,1)} %refs_0_.1), channel_id=1, source_target_pairs={{4,0},{0,4},{5,1},{1,5},{6,2},{2,6},{7,3},{3,7},{12,8},{8,12},{13,... | collective-permute-start | bytes 2359304 | tf_op jit(solution)/shard_map/ppermute | solution.py:36
  6.5 19.3 %collective-permute-start = (bf16[32,1024]{1,0:T(8,128)(2,1)}, bf16[32,1024]{1,0:T(8,128)(2,1)S(1)}, u32[]{:S(2)}, u32[]{:S(2)}) collective-permute-start(bf16[32,1024]{1,0:T(8,128)(2,1)} %bitcast.3), channel_id=1, source_target_pairs={{0,68},{4,64},{8,76},{12,72},{16,84},{20,80},{24,92},{28,88},{32,1... | collective-permute-start | bytes 196616 | tf_op jit(solution)/shard_map/ppermute | solution.py:326
  25.8 56.1 %slice-start = ((s8[8388608]{0:T(1024)(128)(4,1)}), s8[4194304]{0:T(1024)(128)(4,1)S(1)}, s32[]{:S(2)}) async-start(s8[8388608]{0:T(1024)(128)(4,1)} %bitcast.1), calls=%async_computation.2 | async-start | bytes 8388608
  26.8 55.1 %slice-start.1 = ((s8[8388608]{0:T(1024)(128)(4,1)}), s8[4194304]{0:T(1024)(128)(4,1)S(1)}, s32[]{:S(2)}) async-start(s8[8388608]{0:T(1024)(128)(4,1)} %bitcast.1), calls=%async_computation.3 | async-start | bytes 8388608
  26.9 8.5 %collective-permute-start.3 = (bf16[64,1024]{1,0:T(8,128)(2,1)S(1)}, bf16[64,1024]{1,0:T(8,128)(2,1)S(1)}, u32[]{:S(2)}, u32[]{:S(2)}) collective-permute-start(bf16[64,1024]{1,0:T(8,128)(2,1)S(1)} %pad_maximum_fusion.k0), channel_id=1, source_target_pairs={{24,0},{0,8},{8,16},{16,24},{25,1},{1,9},{9,17},{17,25},{26,2},{2,... | collective-permute-start | bytes 393224 | tf_op jit(solution)/shard_map/ppermute | solution.py:36
  28.8 8.5 %collective-permute-start.2 = (bf16[64,1024]{1,0:T(8,128)(2,1)S(1)}, bf16[64,1024]{1,0:T(8,128)(2,1)S(1)}, u32[]{:S(2)}, u32[]{:S(2)}) collective-permute-start(bf16[64,1024]{1,0:T(8,128)(2,1)S(1)} %pad_maximum_fusion.k0), channel_id=1, source_target_pairs={{16,0},{24,8},{0,16},{8,24},{17,1},{25,9},{1,17},{9,25},{18,2},{26... | collective-permute-start | bytes 393224 | tf_op jit(solution)/shard_map/ppermute | solution.py:36
  35.3 5.0 %collective-permute-start.1 = (bf16[64,1024]{1,0:T(8,128)(2,1)S(1)}, bf16[64,1024]{1,0:T(8,128)(2,1)S(1)}, u32[]{:S(2)}, u32[]{:S(2)}) collective-permute-start(bf16[64,1024]{1,0:T(8,128)(2,1)S(1)} %pad_maximum_fusion.k0), channel_id=1, source_target_pairs={{8,0},{16,8},{24,16},{0,24},{9,1},{17,9},{25,17},{1,25},{10,2},{18... | collective-permute-start | bytes 393224 | tf_op jit(solution)/shard_map/ppermute | solution.py:36
  40.3 1.1 copy-start
  86.6 11.9 %collective-permute-start.7 = (bf16[3,32,1024]{2,1,0:T(8,128)(2,1)S(1)}, bf16[3,32,1024]{2,1,0:T(8,128)(2,1)S(1)}, u32[]{:S(2)}, u32[]{:S(2)}) collective-permute-start(bf16[3,32,1024]{2,1,0:T(8,128)(2,1)S(1)} %get-tuple-element.30), channel_id=1, source_target_pairs={{0,1},{1,0},{2,3},{3,2},{4,5},{5,4},{6,7},{7,6},{8,9},{9,8},{10,11... | collective-permute-start | bytes 589832 | tf_op jit(solution)/shard_map/ppermute | solution.py:41
  87.0 11.4 %collective-permute-start.8 = (bf16[3,32,1024]{2,1,0:T(8,128)(2,1)S(1)}, bf16[3,32,1024]{2,1,0:T(8,128)(2,1)S(1)}, u32[]{:S(2)}, u32[]{:S(2)}) collective-permute-start(bf16[3,32,1024]{2,1,0:T(8,128)(2,1)S(1)} %get-tuple-element.31), channel_id=1, source_target_pairs={{0,2},{1,3},{2,0},{3,1},{4,6},{5,7},{6,4},{7,5},{8,10},{9,11},{10,... | collective-permute-start | bytes 589832 | tf_op jit(solution)/shard_map/ppermute | solution.py:41
  87.5 11.0 %collective-permute-start.9 = (bf16[3,32,1024]{2,1,0:T(8,128)(2,1)S(1)}, bf16[3,32,1024]{2,1,0:T(8,128)(2,1)S(1)}, u32[]{:S(2)}, u32[]{:S(2)}) collective-permute-start(bf16[3,32,1024]{2,1,0:T(8,128)(2,1)S(1)} %get-tuple-element.32), channel_id=1, source_target_pairs={{0,3},{1,2},{2,1},{3,0},{4,7},{5,6},{6,5},{7,4},{8,11},{9,10},{10,... | collective-permute-start | bytes 589832 | tf_op jit(solution)/shard_map/ppermute | solution.py:41
  88.5 4.8 %collective-permute-start.10 = (f32[3,2,128]{2,1,0:T(2,128)S(1)}, f32[3,2,128]{2,1,0:T(2,128)S(1)}, u32[]{:S(2)}, u32[]{:S(2)}) collective-permute-start(f32[3,2,128]{2,1,0:T(2,128)S(1)} %get-tuple-element.33.refs_1_), channel_id=1, source_target_pairs={{96,0},{0,32},{32,64},{64,96},{97,1},{1,33},{33,65},{65,97},{98,2}... | collective-permute-start | bytes 9224 | tf_op jit(solution)/shard_map/ppermute | solution.py:36
  90.3 4.0 %collective-permute-start.11 = (f32[3,2,128]{2,1,0:T(2,128)S(1)}, f32[3,2,128]{2,1,0:T(2,128)S(1)}, u32[]{:S(2)}, u32[]{:S(2)}) collective-permute-start(f32[3,2,128]{2,1,0:T(2,128)S(1)} %get-tuple-element.34.refs_2_), channel_id=1, source_target_pairs={{32,0},{64,32},{96,64},{0,96},{33,1},{65,33},{97,65},{1,97},{34,2}... | collective-permute-start | bytes 9224 | tf_op jit(solution)/shard_map/ppermute | solution.py:36
  93.3 5.1 %collective-permute-start.12 = (f32[3,2,128]{2,1,0:T(2,128)S(1)}, f32[3,2,128]{2,1,0:T(2,128)S(1)}, u32[]{:S(2)}, u32[]{:S(2)}) collective-permute-start(f32[3,2,128]{2,1,0:T(2,128)S(1)} %get-tuple-element.35.refs_3_), channel_id=1, source_target_pairs={{4,0},{0,4},{5,1},{1,5},{6,2},{2,6},{7,3},{3,7},{12,8},{8,12},{13,... | collective-permute-start | bytes 9224 | tf_op jit(solution)/shard_map/ppermute | solution.py:36
  129.7 17.7 %collective-permute-start.13 = (bf16[3,128,1024]{2,1,0:T(8,128)(2,1)S(1)}, bf16[3,128,1024]{2,1,0:T(8,128)(2,1)S(1)}, u32[]{:S(2)}, u32[]{:S(2)}) collective-permute-start(bf16[3,128,1024]{2,1,0:T(8,128)(2,1)S(1)} %get-tuple-element.41), channel_id=1, source_target_pairs={{96,0},{0,32},{32,64},{64,96},{97,1},{1,33},{33,65},{65,97},{98,2}... | collective-permute-start | bytes 2359304 | tf_op jit(solution)/shard_map/ppermute | solution.py:36
  130.9 16.5 %collective-permute-start.14 = (bf16[3,128,1024]{2,1,0:T(8,128)(2,1)S(1)}, bf16[3,128,1024]{2,1,0:T(8,128)(2,1)S(1)}, u32[]{:S(2)}, u32[]{:S(2)}) collective-permute-start(bf16[3,128,1024]{2,1,0:T(8,128)(2,1)S(1)} %get-tuple-element.42), channel_id=1, source_target_pairs={{32,0},{64,32},{96,64},{0,96},{33,1},{65,33},{97,65},{1,97},{34,2}... | collective-permute-start | bytes 2359304 | tf_op jit(solution)/shard_map/ppermute | solution.py:36
  133.0 17.3 %collective-permute-start.15 = (bf16[3,128,1024]{2,1,0:T(8,128)(2,1)S(1)}, bf16[3,128,1024]{2,1,0:T(8,128)(2,1)S(1)}, u32[]{:S(2)}, u32[]{:S(2)}) collective-permute-start(bf16[3,128,1024]{2,1,0:T(8,128)(2,1)S(1)} %get-tuple-element.43), channel_id=1, source_target_pairs={{4,0},{0,4},{5,1},{1,5},{6,2},{2,6},{7,3},{3,7},{12,8},{8,12},{13,... | collective-permute-start | bytes 2359304 | tf_op jit(solution)/shard_map/ppermute | solution.py:36

commit v5 on v4

--- a/solution.py
+++ b/solution.py
@@ -24,6 +24,7 @@
 ROOM = 24 * 1024 * 1024
 VMEM = pl.BlockSpec(memory_space=pltpu.VMEM)
 ANY = pl.BlockSpec(memory_space=pl.ANY)
+HBM = pl.BlockSpec(memory_space=pltpu.HBM)
 
 
 def place(step):
@@ -49,9 +50,9 @@
 
 def dispatch_kernel(first, k0, k1, k2, k3, *refs):
     *blocks, message, logits, s0, s1, s2, s3, first_here, field, arrivals, loaded = refs
-    owners, _, own_slots, _ = message.shape
-    slots = owners * own_slots
-    features = k0.shape[1]
+    owners = message.shape[0]
+    slots, features = 4 * k0.shape[0], k0.shape[1]
+    own_slots, tiles = slots // owners, features // LANES
     columns = jnp.concatenate([k0[...], k1[...], k2[...], k3[...]], axis=0)
     images, positions, _ = blocks[0].shape
 
@@ -93,14 +94,21 @@
             piece = rest.astype(jnp.bfloat16).astype(jnp.float32)
             stats = jnp.where(lane == k, piece, stats)
             rest = rest - piece
-        stats = stats.astype(jnp.bfloat16).reshape(owners, own_slots, LANES)
+        stats = stats.T[:8]
         sums = jnp.dot(
             raised.astype(jnp.bfloat16), field[b], preferred_element_type=jnp.float32
         ).astype(jnp.bfloat16)
-        sums = sums.reshape(owners, own_slots, features)
         for k in range(owners):
-            message[place(k), b, :, features:] = stats[k]
-            message[place(k), b, :, :features] = sums[k]
+            at, rows = place(k), slice(k * own_slots, (k + 1) * own_slots)
+            for t in range(tiles):
+                lanes = slice(t * LANES, (t + 1) * LANES)
+                to = pl.ds(pl.multiple_of((b * tiles + t) * own_slots, own_slots), own_slots)
+                message[at, to, :] = sums[rows, lanes]
+            line = stats
+            if k > 0:
+                line = jnp.concatenate([line[:, k * own_slots :], line[:, : k * own_slots]], axis=1)
+            to = pl.ds(pl.multiple_of((images * tiles) * own_slots + 8 * b, 8), 8)
+            message[at, to, :] = line[:, :LANES].astype(jnp.bfloat16)
         return carry
 
     lax.fori_loop(0, images, one, 0)
@@ -114,12 +122,14 @@
     return pl.pallas_call(
         dispatch_kernel,
         out_shape=(
-            jax.ShapeDtypeStruct((owners, images, own_slots, features + LANES), jnp.bfloat16),
+            jax.ShapeDtypeStruct(
+                (owners, images * (features // LANES * own_slots + 8), LANES), jnp.bfloat16
+            ),
             jax.ShapeDtypeStruct((images, slots, width), jnp.float32),
             *(jax.ShapeDtypeStruct((images, 2, positions), jnp.float32) for _ in blocks),
             jax.ShapeDtypeStruct(first.shape, first.dtype),
         ),
-        in_specs=[ANY] + [VMEM] * len(keys) + [ANY] * len(blocks),
+        in_specs=[HBM] + [VMEM] * len(keys) + [HBM] + [ANY] * (len(blocks) - 1),
         out_specs=(VMEM,) * (3 + len(blocks)),
         scratch_shapes=[
             pltpu.VMEM((images, width, features), jnp.bfloat16),
@@ -137,29 +147,37 @@
 
 
 def merge_kernel(arrived, inputs):
-    owners, images, _, _ = arrived.shape
-    features = inputs.shape[2]
+    owners = arrived.shape[0]
+    images, own_slots, features = inputs.shape
+    tiles = features // LANES
     for b in range(images):
         tops, totals = [], []
         for k in range(owners):
-            stats = arrived[k, b, :, features:].astype(jnp.float32)
-            tops.append(stats[:, 0:1])
-            totals.append(stats[:, 1:2] + stats[:, 2:3] + stats[:, 3:4])
+            at = images * tiles * own_slots + 8 * b
+            stats = arrived[k, at : at + 8, :].astype(jnp.float32)
+            tops.append(stats[0:1])
+            totals.append(stats[1:2] + stats[2:3] + stats[3:4])
         peak = functools.reduce(jnp.maximum, tops)
         scales = [jnp.exp(top - peak) for top in tops]
         whole = sum(scale * total for scale, total in zip(scales, totals))
-        summed = sum(
-            (scales[k] / whole) * arrived[k, b, :, :features].astype(jnp.float32)
-            for k in range(owners)
-        )
-        inputs[b] = summed.astype(jnp.bfloat16)
-
-
-def merge(arrived):
-    _, images, own_slots, width = arrived.shape
+        shares = [scale / whole for scale in scales]
+        shares = jnp.concatenate(
+            shares + [jnp.zeros((LANES - owners, LANES), jnp.float32)], axis=0
+        ).T
+        for t in range(tiles):
+            at = (b * tiles + t) * own_slots
+            summed = sum(
+                shares[:own_slots, k : k + 1]
+                * arrived[k, at : at + own_slots, :].astype(jnp.float32)
+                for k in range(owners)
+            )
+            inputs[b, :, t * LANES : (t + 1) * LANES] = summed.astype(jnp.bfloat16)
+
+
+def merge(arrived, shape):
     return pl.pallas_call(
         merge_kernel,
-        out_shape=jax.ShapeDtypeStruct((images, own_slots, width - LANES), jnp.bfloat16),
+        out_shape=jax.ShapeDtypeStruct(shape, jnp.bfloat16),
         in_specs=[VMEM],
         out_specs=VMEM,
         cost_estimate=pl.CostEstimate(
@@ -170,18 +188,11 @@
     )(arrived)
 
 
-def expert_kernel(rows, first, second, *refs):
-    *outs, second_here, loaded = refs
+def expert_kernel(rows, first, second, *outs):
     rank = lax.axis_index("dp")
     experts = first.shape[0]
     images, own_slots, _ = outs[0].shape
     per_expert = own_slots // experts
-
-    def load(expert):
-        return pltpu.make_async_copy(second.at[expert], second_here.at[expert], loaded.at[expert])
-
-    for expert in range(experts):
-        load(expert).start()
 
     def one(expert, carry):
         cut = pl.ds(pl.multiple_of(expert * per_expert, per_expert), per_expert)
@@ -194,8 +205,7 @@
             jnp.concatenate(taken, axis=0), first[expert], preferred_element_type=jnp.float32
         )
         hidden = jax.nn.gelu(hidden, approximate=True).astype(jnp.bfloat16)
-        load(expert).wait()
-        result = jnp.dot(hidden, second_here[expert], preferred_element_type=jnp.float32)
+        result = jnp.dot(hidden, second[expert], preferred_element_type=jnp.float32)
         for k, out in enumerate(outs):
             for b in range(images):
                 at = (k * images + b) * per_expert
@@ -212,12 +222,8 @@
     return pl.pallas_call(
         expert_kernel,
         out_shape=[jax.ShapeDtypeStruct(shape, kind) for kind in kinds],
-        in_specs=[VMEM, VMEM, ANY],
+        in_specs=[VMEM] * 3,
         out_specs=[VMEM] * ranks,
-        scratch_shapes=[
-            pltpu.VMEM(expert_out.shape, expert_out.dtype),
-            pltpu.SemaphoreType.DMA((expert_out.shape[0],)),
-        ],
         cost_estimate=pl.CostEstimate(
             flops=4 * rows.size * expert_in.shape[2],
             bytes_accessed=4 * expert_in.size,
@@ -289,8 +295,9 @@
 
 
 def finish_kernel(*refs):
-    parts, stats, out = refs[:4], refs[4:8], refs[8]
+    parts, stats, (out, ready, sent) = refs[:4], refs[4:8], refs[8:]
     images, positions, _ = out.shape
+    copies = [pltpu.make_async_copy(ready.at[b], out.at[b], sent.at[b]) for b in range(images)]
     for b in range(images):
         tops = [s[b][0:1] for s in stats]
         highest = functools.reduce(jnp.maximum, tops)
@@ -302,7 +309,10 @@
         joined = sum(
             shares[:, k : k + 1] * part[b].astype(jnp.float32) for k, part in enumerate(parts)
         )
-        out[b] = joined.astype(out.dtype)
+        ready[b] = joined.astype(out.dtype)
+        copies[b].start()
+    for copy in copies:
+        copy.wait()
 
 
 def finish(parts, stats):
@@ -311,7 +321,11 @@
         finish_kernel,
         out_shape=jax.ShapeDtypeStruct(shape, jnp.bfloat16),
         in_specs=[VMEM] * 8,
-        out_specs=VMEM,
+        out_specs=ANY,
+        scratch_shapes=[
+            pltpu.VMEM(shape, jnp.bfloat16),
+            pltpu.SemaphoreType.DMA((shape[0],)),
+        ],
         cost_estimate=pl.CostEstimate(
             flops=8 * parts[0].size, bytes_accessed=12 * parts[0].size, transcendentals=0
         ),
@@ -331,7 +345,8 @@
         keys, expert_in, [tokens, *near], slot_keys.shape[1]
     )
     arrived = all_to_all(message)
-    rows = lax.all_gather(merge(arrived), "dp", axis=0, tiled=True)
+    slot_inputs = merge(arrived, (tokens.shape[0], *slot_keys.shape[::-1]))
+    rows = lax.all_gather(slot_inputs, "dp", axis=0, tiled=True)
     own, *pieces = run_experts(rows, first, expert_out, ranks)
     pieces = [swapped(piece, "dp", k) for k, piece in zip((1, 2, 3), pieces)]
     back = [ahead(stats[1], X, 3), ahead(stats[2], X, 1), ahead(stats[3], Y, 1)]

time: 152 us -> 150 us (0.987)
  no operation moved by 1% of the time
where the time goes in v5:
time: 150 us; the launch traced here: 149 us
  blocking collectives  64.5 us (43%)
  waiting for transfers between devices  47.5 us (32%)
  starting transfers between devices  24.3 us (16%)
  Pallas kernels  10.9 us (7%)
    all_to_all x2, blocking collectives, all_to_all(): lax.all_to_all(array, SLOT, split_axis=0, concat_axis=0, axis_index_group...  55.8 us
    ppermute x12, waiting for transfers between devices, ahead(): lax.ppermute(array, axis, [((i + step) % size, i) for i in range(size)])  29.8 us
    ppermute x12, starting transfers between devices, ahead(): lax.ppermute(array, axis, [((i + step) % size, i) for i in range(size)])  20.7 us
    ppermute x1, waiting for transfers between devices, shards(): pair = lax.ppermute(slot_keys.T, SLOT, PARTNER)  17.7 us
    all_gather x1, blocking collectives, shards(): rows = lax.all_gather(slot_inputs, 'dp', axis=0, tiled=True)  8.68 us
    pallas_call x1, Pallas kernels, dispatch(): pl.pallas_call(dispatch_kernel, out_shape=(jax.ShapeDtypeStruct((owners,...  3.75 us
    pallas_call x1, Pallas kernels, run_experts(): pl.pallas_call(expert_kernel, out_shape=[jax.ShapeDtypeStruct(shape, kind...  3.46 us
  transfers between devices with their start and end apart: 16, of which 8 were waited for; matrix products, arithmetic and copies ran while one was open for 1% of the time, Pallas kernels for 0%

profile of v5, /device:TPU:0, one launch (start us, length us, event | category | flops | bytes accessed | tf_op | source)
XLA Modules:
  0.0 149.4 jit_solution(9861626059803954651)
XLA Ops:
  0.0 1.6 %collective-permute-start.5 = (bf16[3,128,1024]{2,1,0:T(8,128)(2,1)}, bf16[3,128,1024]{2,1,0:T(8,128)(2,1)S(1)}, u32[]{:S(2)}, u32[]{:S(2)}) collective-permute-start(bf16[3,128,1024]{2,1,0:T(8,128)(2,1)} %refs_0_.1), channel_id=1, source_target_pairs={{96,0},{0,32},{32,64},{64,96},{97,1},{1,33},{33,65},{65,97},{98,2}... | collective-permute-start | bytes 2359304 | tf_op jit(solution)/shard_map/ppermute | solution.py:37
  1.6 1.6 %collective-permute-start.4 = (bf16[3,128,1024]{2,1,0:T(8,128)(2,1)}, bf16[3,128,1024]{2,1,0:T(8,128)(2,1)S(1)}, u32[]{:S(2)}, u32[]{:S(2)}) collective-permute-start(bf16[3,128,1024]{2,1,0:T(8,128)(2,1)} %refs_0_.1), channel_id=1, source_target_pairs={{32,0},{64,32},{96,64},{0,96},{33,1},{65,33},{97,65},{1,97},{34,2}... | collective-permute-start | bytes 2359304 | tf_op jit(solution)/shard_map/ppermute | solution.py:37
  3.2 3.3 %collective-permute-start.6 = (bf16[3,128,1024]{2,1,0:T(8,128)(2,1)}, bf16[3,128,1024]{2,1,0:T(8,128)(2,1)S(1)}, u32[]{:S(2)}, u32[]{:S(2)}) collective-permute-start(bf16[3,128,1024]{2,1,0:T(8,128)(2,1)} %refs_0_.1), channel_id=1, source_target_pairs={{4,0},{0,4},{5,1},{1,5},{6,2},{2,6},{7,3},{3,7},{12,8},{8,12},{13,... | collective-permute-start | bytes 2359304 | tf_op jit(solution)/shard_map/ppermute | solution.py:37
  6.5 1.6 %collective-permute-start = (bf16[32,1024]{1,0:T(8,128)(2,1)}, bf16[32,1024]{1,0:T(8,128)(2,1)S(1)}, u32[]{:S(2)}, u32[]{:S(2)}) collective-permute-start(bf16[32,1024]{1,0:T(8,128)(2,1)} %bitcast.3), channel_id=1, source_target_pairs={{0,68},{4,64},{8,76},{12,72},{16,84},{20,80},{24,92},{28,88},{32,1... | collective-permute-start | bytes 196616 | tf_op jit(solution)/shard_map/ppermute | solution.py:340
  8.1 17.7 %collective-permute-done = bf16[32,1024]{1,0:T(8,128)(2,1)S(1)} collective-permute-done((bf16[32,1024]{1,0:T(8,128)(2,1)}, bf16[32,1024]{1,0:T(8,128)(2,1)S(1)}, u32[]{:S(2)}, u32[]{:S(2)}) %collective-permute-start) | collective-permute-done | bytes 65568 | tf_op jit(solution)/shard_map/ppermute | solution.py:340
  25.8 0.0 slice-start
  25.8 1.0 pad_maximum_fusion.k0
  26.8 0.0 slice-start.1
  26.9 2.0 %collective-permute-start.3 = (bf16[64,1024]{1,0:T(8,128)(2,1)S(1)}, bf16[64,1024]{1,0:T(8,128)(2,1)S(1)}, u32[]{:S(2)}, u32[]{:S(2)}) collective-permute-start(bf16[64,1024]{1,0:T(8,128)(2,1)S(1)} %pad_maximum_fusion.k0), channel_id=1, source_target_pairs={{24,0},{0,8},{8,16},{16,24},{25,1},{1,9},{9,17},{17,25},{26,2},{2,... | collective-permute-start | bytes 393224 | tf_op jit(solution)/shard_map/ppermute | solution.py:37
  28.8 3.6 %collective-permute-start.2 = (bf16[64,1024]{1,0:T(8,128)(2,1)S(1)}, bf16[64,1024]{1,0:T(8,128)(2,1)S(1)}, u32[]{:S(2)}, u32[]{:S(2)}) collective-permute-start(bf16[64,1024]{1,0:T(8,128)(2,1)S(1)} %pad_maximum_fusion.k0), channel_id=1, source_target_pairs={{16,0},{24,8},{0,16},{8,24},{17,1},{25,9},{1,17},{9,25},{18,2},{26... | collective-permute-start | bytes 393224 | tf_op jit(solution)/shard_map/ppermute | solution.py:37
  32.4 2.9 %collective-permute-done.3.k3 = bf16[64,1024]{1,0:T(8,128)(2,1)S(1)} collective-permute-done((bf16[64,1024]{1,0:T(8,128)(2,1)S(1)}, bf16[64,1024]{1,0:T(8,128)(2,1)S(1)}, u32[]{:S(2)}, u32[]{:S(2)}) %collective-permute-start.3) | collective-permute-done | bytes 131104 | tf_op jit(solution)/shard_map/ppermute | solution.py:37
  35.3 1.1 collective-permute-start.1
  36.5 0.8 collective-permute-done.2.k2
  37.3 3.0 %collective-permute-done.1.k1 = bf16[64,1024]{1,0:T(8,128)(2,1)S(1)} collective-permute-done((bf16[64,1024]{1,0:T(8,128)(2,1)S(1)}, bf16[64,1024]{1,0:T(8,128)(2,1)S(1)}, u32[]{:S(2)}, u32[]{:S(2)}) %collective-permute-start.1) | collective-permute-done | bytes 131104 | tf_op jit(solution)/shard_map/ppermute | solution.py:37
  40.3 0.0 collective-permute-done.5.refs_2_
  40.3 0.0 collective-permute-done.4.refs_1_
  40.3 0.0 collective-permute-done.6.refs_3_
  40.3 0.0 copy-start
  40.3 1.1 copy-done
  41.4 3.7 %dispatch.1 = (bf16[8,792,128]{2,1,0:T(8,128)(2,1)S(1)}, f32[3,256,512]{2,1,0:T(8,128)S(1)}, f32[3,2,128]{2,1,0:T(2,128)S(1)}, f32[3,2,128]{2,1,0:T(2,128)S(1)},...) custom-call(bf16[4,1024,1024]{2,1,0:T(8,128)(2,1)} %first.1, ...), custom_call_target="tpu_custom_call" | custom-call | flops 1610612736 | bytes 3145728 | tf_op jit(solution)/shard_map/dispatch/pallas_call | solution.py:122
  45.2 25.9 %all_to_all.10.arrived = bf16[8,792,128]{2,1,0:T(8,128)(2,1)S(1)} all-to-all(bf16[8,792,128]{2,1,0:T(8,128)(2,1)S(1)} %get-tuple-element.27), channel_id=1, replica_groups={{0,8,16,24,68,76,84,92},{32,40,48,56,100,108,116,124},{64,72,80,88,4,12..., dimensions={0} | all-to-all | bytes 3244032 | tf_op jit(solution)/shard_map/all_to_all | solution.py:46
  71.1 0.5 merge.1
  71.5 8.7 %all_gather.3.rows = bf16[12,32,1024]{2,1,0:T(8,128)(2,1)S(1)} all-gather(bf16[3,32,1024]{2,1,0:T(8,128)(2,1)S(1)} %merge.1), channel_id=1, replica_groups=mesh['slot_0'=4,'slot_1'=4,'slot_2'=2,'dp'=4] {'dp'}, dimensions={0}, use_global_device_ids=true | all-gather | bytes 983040 | tf_op jit(solution)/shard_map/all_gather | solution.py:349
  80.2 0.0 slice-done
  80.2 0.0 slice-done.1
  80.2 3.5 %experts.1 = (f32[3,32,1024]{2,1,0:T(8,128)S(1)}, bf16[3,32,1024]{2,1,0:T(8,128)(2,1)S(1)}, bf16[3,32,1024]{2,1,0:T(8,128)(2,1)S(1)}, bf16[3,32,1024]{2,1,0:T(8,128)(2,1)S(1)}) custom-call(bf16[12,32,1024]{2,1,0:T(8,128)(2,1)S(1)} %all_gather.3.rows, bf16[4,1024,1024]{2,1,0:T(8,128)(2,1)S(1)} %get-tuple-element.28.first, bf16[4,1024,1024]{2,1,0:T(8,128)(2,1)S(1)} %bitcast.2), custom_call_target="tpu_custom_call" | custom-call | flops 1610612736 | bytes 16777216 | tf_op jit(solution)/shard_map/experts/pallas_call | solution.py:222
  83.7 0.4 collective-permute-start.7
  84.1 0.4 collective-permute-start.8
  84.6 1.1 collective-permute-start.9
  85.6 1.8 %collective-permute-start.10 = (f32[3,2,128]{2,1,0:T(2,128)S(1)}, f32[3,2,128]{2,1,0:T(2,128)S(1)}, u32[]{:S(2)}, u32[]{:S(2)}) collective-permute-start(f32[3,2,128]{2,1,0:T(2,128)S(1)} %get-tuple-element.33.refs_1_), channel_id=1, source_target_pairs={{96,0},{0,32},{32,64},{64,96},{97,1},{1,33},{33,65},{65,97},{98,2}... | collective-permute-start | bytes 9224 | tf_op jit(solution)/shard_map/ppermute | solution.py:37
  87.4 1.5 collective-permute-start.11
  88.9 1.6 %collective-permute-done.10.refs_5_ = f32[3,2,128]{2,1,0:T(2,128)S(1)} collective-permute-done((f32[3,2,128]{2,1,0:T(2,128)S(1)}, f32[3,2,128]{2,1,0:T(2,128)S(1)}, u32[]{:S(2)}, u32[]{:S(2)}) %collective-permute-start.10) | collective-permute-done | bytes 3104 | tf_op jit(solution)/shard_map/ppermute | solution.py:37
  90.5 0.9 collective-permute-start.12
  91.4 0.0 collective-permute-done.11.refs_6_
  91.4 4.2 %collective-permute-done.12.refs_7_ = f32[3,2,128]{2,1,0:T(2,128)S(1)} collective-permute-done((f32[3,2,128]{2,1,0:T(2,128)S(1)}, f32[3,2,128]{2,1,0:T(2,128)S(1)}, u32[]{:S(2)}, u32[]{:S(2)}) %collective-permute-start.12) | collective-permute-done | bytes 3104 | tf_op jit(solution)/shard_map/ppermute | solution.py:37
  95.6 0.0 collective-permute-done.7.first
  95.6 0.0 collective-permute-done.8.second
  95.6 0.0 collective-permute-done.9.third
  95.6 0.1 spread.1
  95.7 30.0 %all_to_all.11.everyone = bf16[8,3,32,1024]{3,2,1,0:T(8,128)(2,1)S(1)} all-to-all(bf16[8,3,32,1024]{3,2,1,0:T(8,128)(2,1)S(1)} %spread.1), channel_id=1, replica_groups={{0,8,16,24,68,76,84,92},{32,40,48,56,100,108,116,124},{64,72,80,88,4,12..., dimensions={0} | all-to-all | bytes 3145728 | tf_op jit(solution)/shard_map/all_to_all | solution.py:46
  125.6 1.5 combine.1
  127.1 1.2 collective-permute-start.13
  128.3 2.1 %collective-permute-start.14 = (bf16[3,128,1024]{2,1,0:T(8,128)(2,1)S(1)}, bf16[3,128,1024]{2,1,0:T(8,128)(2,1)S(1)}, u32[]{:S(2)}, u32[]{:S(2)}) collective-permute-start(bf16[3,128,1024]{2,1,0:T(8,128)(2,1)S(1)} %get-tuple-element.42), channel_id=1, source_target_pairs={{32,0},{64,32},{96,64},{0,96},{33,1},{65,33},{97,65},{1,97},{34,2}... | collective-permute-start | bytes 2359304 | tf_op jit(solution)/shard_map/ppermute | solution.py:37
  130.4 0.0 collective-permute-start.15
  130.4 14.3 %collective-permute-done.13.refs_1_ = bf16[3,128,1024]{2,1,0:T(8,128)(2,1)S(1)} collective-permute-done((bf16[3,128,1024]{2,1,0:T(8,128)(2,1)S(1)}, bf16[3,128,1024]{2,1,0:T(8,128)(2,1)S(1)}, u32[]{:S(2)}, u32[]{:S(2)}) %collective-permute-start.13) | collective-permute-done | bytes 786464 | tf_op jit(solution)/shard_map/ppermute | solution.py:37
  144.7 0.0 collective-permute-done.14.refs_2_
  144.8 3.0 %collective-permute-done.15.refs_3_ = bf16[3,128,1024]{2,1,0:T(8,128)(2,1)S(1)} collective-permute-done((bf16[3,128,1024]{2,1,0:T(8,128)(2,1)S(1)}, bf16[3,128,1024]{2,1,0:T(8,128)(2,1)S(1)}, u32[]{:S(2)}, u32[]{:S(2)}) %collective-permute-start.15) | collective-permute-done | bytes 786464 | tf_op jit(solution)/shard_map/ppermute | solution.py:37
  147.7 1.7 %finish.1 = bf16[3,128,1024]{2,1,0:T(8,128)(2,1)} custom-call(f32[3,128,1024]{2,1,0:T(8,128)S(1)} %get-tuple-element.40.refs_0_, bf16[3,128,1024]{2,1,0:T(8,128)(2,1)S(1)} %collective-permute-done.13.refs_1_, bf16[3,128,1024]{2,1,0:T(8,128)(2,1)S(1)} %collective-permute-done.14.refs_2_, bf16[3,128,1024]{2,1,0:T(8,128)(2,1)S(1)} %collective-permute-done.15.refs_3_, ...), custom_call_target="tpu_custom_call" | custom-call | flops 3145728 | bytes 4718592 | tf_op jit(solution)/shard_map/finish/pallas_call | solution.py:320
  (1 shorter events, 0.0 us)
Async XLA Ops:
  0.0 40.3 %collective-permute-start.5 = (bf16[3,128,1024]{2,1,0:T(8,128)(2,1)}, bf16[3,128,1024]{2,1,0:T(8,128)(2,1)S(1)}, u32[]{:S(2)}, u32[]{:S(2)}) collective-permute-start(bf16[3,128,1024]{2,1,0:T(8,128)(2,1)} %refs_0_.1), channel_id=1, source_target_pairs={{96,0},{0,32},{32,64},{64,96},{97,1},{1,33},{33,65},{65,97},{98,2}... | collective-permute-start | bytes 2359304 | tf_op jit(solution)/shard_map/ppermute | solution.py:37
  1.6 38.7 %collective-permute-start.4 = (bf16[3,128,1024]{2,1,0:T(8,128)(2,1)}, bf16[3,128,1024]{2,1,0:T(8,128)(2,1)S(1)}, u32[]{:S(2)}, u32[]{:S(2)}) collective-permute-start(bf16[3,128,1024]{2,1,0:T(8,128)(2,1)} %refs_0_.1), channel_id=1, source_target_pairs={{32,0},{64,32},{96,64},{0,96},{33,1},{65,33},{97,65},{1,97},{34,2}... | collective-permute-start | bytes 2359304 | tf_op jit(solution)/shard_map/ppermute | solution.py:37
  3.2 37.0 %collective-permute-start.6 = (bf16[3,128,1024]{2,1,0:T(8,128)(2,1)}, bf16[3,128,1024]{2,1,0:T(8,128)(2,1)S(1)}, u32[]{:S(2)}, u32[]{:S(2)}) collective-permute-start(bf16[3,128,1024]{2,1,0:T(8,128)(2,1)} %refs_0_.1), channel_id=1, source_target_pairs={{4,0},{0,4},{5,1},{1,5},{6,2},{2,6},{7,3},{3,7},{12,8},{8,12},{13,... | collective-permute-start | bytes 2359304 | tf_op jit(solution)/shard_map/ppermute | solution.py:37
  6.5 19.3 %collective-permute-start = (bf16[32,1024]{1,0:T(8,128)(2,1)}, bf16[32,1024]{1,0:T(8,128)(2,1)S(1)}, u32[]{:S(2)}, u32[]{:S(2)}) collective-permute-start(bf16[32,1024]{1,0:T(8,128)(2,1)} %bitcast.3), channel_id=1, source_target_pairs={{0,68},{4,64},{8,76},{12,72},{16,84},{20,80},{24,92},{28,88},{32,1... | collective-permute-start | bytes 196616 | tf_op jit(solution)/shard_map/ppermute | solution.py:340
  25.8 54.4 %slice-start = ((s8[8388608]{0:T(1024)(128)(4,1)}), s8[4194304]{0:T(1024)(128)(4,1)S(1)}, s32[]{:S(2)}) async-start(s8[8388608]{0:T(1024)(128)(4,1)} %bitcast.1), calls=%async_computation.2 | async-start | bytes 8388608
  26.8 53.4 %slice-start.1 = ((s8[8388608]{0:T(1024)(128)(4,1)}), s8[4194304]{0:T(1024)(128)(4,1)S(1)}, s32[]{:S(2)}) async-start(s8[8388608]{0:T(1024)(128)(4,1)} %bitcast.1), calls=%async_computation.3 | async-start | bytes 8388608
  26.9 8.5 %collective-permute-start.3 = (bf16[64,1024]{1,0:T(8,128)(2,1)S(1)}, bf16[64,1024]{1,0:T(8,128)(2,1)S(1)}, u32[]{:S(2)}, u32[]{:S(2)}) collective-permute-start(bf16[64,1024]{1,0:T(8,128)(2,1)S(1)} %pad_maximum_fusion.k0), channel_id=1, source_target_pairs={{24,0},{0,8},{8,16},{16,24},{25,1},{1,9},{9,17},{17,25},{26,2},{2,... | collective-permute-start | bytes 393224 | tf_op jit(solution)/shard_map/ppermute | solution.py:37
  28.8 8.5 %collective-permute-start.2 = (bf16[64,1024]{1,0:T(8,128)(2,1)S(1)}, bf16[64,1024]{1,0:T(8,128)(2,1)S(1)}, u32[]{:S(2)}, u32[]{:S(2)}) collective-permute-start(bf16[64,1024]{1,0:T(8,128)(2,1)S(1)} %pad_maximum_fusion.k0), channel_id=1, source_target_pairs={{16,0},{24,8},{0,16},{8,24},{17,1},{25,9},{1,17},{9,25},{18,2},{26... | collective-permute-start | bytes 393224 | tf_op jit(solution)/shard_map/ppermute | solution.py:37
  35.3 5.0 %collective-permute-start.1 = (bf16[64,1024]{1,0:T(8,128)(2,1)S(1)}, bf16[64,1024]{1,0:T(8,128)(2,1)S(1)}, u32[]{:S(2)}, u32[]{:S(2)}) collective-permute-start(bf16[64,1024]{1,0:T(8,128)(2,1)S(1)} %pad_maximum_fusion.k0), channel_id=1, source_target_pairs={{8,0},{16,8},{24,16},{0,24},{9,1},{17,9},{25,17},{1,25},{10,2},{18... | collective-permute-start | bytes 393224 | tf_op jit(solution)/shard_map/ppermute | solution.py:37
  40.3 1.1 copy-start
  83.7 11.9 %collective-permute-start.7 = (bf16[3,32,1024]{2,1,0:T(8,128)(2,1)S(1)}, bf16[3,32,1024]{2,1,0:T(8,128)(2,1)S(1)}, u32[]{:S(2)}, u32[]{:S(2)}) collective-permute-start(bf16[3,32,1024]{2,1,0:T(8,128)(2,1)S(1)} %get-tuple-element.30), channel_id=1, source_target_pairs={{0,1},{1,0},{2,3},{3,2},{4,5},{5,4},{6,7},{7,6},{8,9},{9,8},{10,11... | collective-permute-start | bytes 589832 | tf_op jit(solution)/shard_map/ppermute | solution.py:42
  84.1 11.4 %collective-permute-start.8 = (bf16[3,32,1024]{2,1,0:T(8,128)(2,1)S(1)}, bf16[3,32,1024]{2,1,0:T(8,128)(2,1)S(1)}, u32[]{:S(2)}, u32[]{:S(2)}) collective-permute-start(bf16[3,32,1024]{2,1,0:T(8,128)(2,1)S(1)} %get-tuple-element.31), channel_id=1, source_target_pairs={{0,2},{1,3},{2,0},{3,1},{4,6},{5,7},{6,4},{7,5},{8,10},{9,11},{10,... | collective-permute-start | bytes 589832 | tf_op jit(solution)/shard_map/ppermute | solution.py:42
  84.6 11.0 %collective-permute-start.9 = (bf16[3,32,1024]{2,1,0:T(8,128)(2,1)S(1)}, bf16[3,32,1024]{2,1,0:T(8,128)(2,1)S(1)}, u32[]{:S(2)}, u32[]{:S(2)}) collective-permute-start(bf16[3,32,1024]{2,1,0:T(8,128)(2,1)S(1)} %get-tuple-element.32), channel_id=1, source_target_pairs={{0,3},{1,2},{2,1},{3,0},{4,7},{5,6},{6,5},{7,4},{8,11},{9,10},{10,... | collective-permute-start | bytes 589832 | tf_op jit(solution)/shard_map/ppermute | solution.py:42
  85.6 4.8 %collective-permute-start.10 = (f32[3,2,128]{2,1,0:T(2,128)S(1)}, f32[3,2,128]{2,1,0:T(2,128)S(1)}, u32[]{:S(2)}, u32[]{:S(2)}) collective-permute-start(f32[3,2,128]{2,1,0:T(2,128)S(1)} %get-tuple-element.33.refs_1_), channel_id=1, source_target_pairs={{96,0},{0,32},{32,64},{64,96},{97,1},{1,33},{33,65},{65,97},{98,2}... | collective-permute-start | bytes 9224 | tf_op jit(solution)/shard_map/ppermute | solution.py:37
  87.4 4.0 %collective-permute-start.11 = (f32[3,2,128]{2,1,0:T(2,128)S(1)}, f32[3,2,128]{2,1,0:T(2,128)S(1)}, u32[]{:S(2)}, u32[]{:S(2)}) collective-permute-start(f32[3,2,128]{2,1,0:T(2,128)S(1)} %get-tuple-element.34.refs_2_), channel_id=1, source_target_pairs={{32,0},{64,32},{96,64},{0,96},{33,1},{65,33},{97,65},{1,97},{34,2}... | collective-permute-start | bytes 9224 | tf_op jit(solution)/shard_map/ppermute | solution.py:37
  90.5 5.1 %collective-permute-start.12 = (f32[3,2,128]{2,1,0:T(2,128)S(1)}, f32[3,2,128]{2,1,0:T(2,128)S(1)}, u32[]{:S(2)}, u32[]{:S(2)}) collective-permute-start(f32[3,2,128]{2,1,0:T(2,128)S(1)} %get-tuple-element.35.refs_3_), channel_id=1, source_target_pairs={{4,0},{0,4},{5,1},{1,5},{6,2},{2,6},{7,3},{3,7},{12,8},{8,12},{13,... | collective-permute-start | bytes 9224 | tf_op jit(solution)/shard_map/ppermute | solution.py:37
  127.1 17.6 %collective-permute-start.13 = (bf16[3,128,1024]{2,1,0:T(8,128)(2,1)S(1)}, bf16[3,128,1024]{2,1,0:T(8,128)(2,1)S(1)}, u32[]{:S(2)}, u32[]{:S(2)}) collective-permute-start(bf16[3,128,1024]{2,1,0:T(8,128)(2,1)S(1)} %get-tuple-element.41), channel_id=1, source_target_pairs={{96,0},{0,32},{32,64},{64,96},{97,1},{1,33},{33,65},{65,97},{98,2}... | collective-permute-start | bytes 2359304 | tf_op jit(solution)/shard_map/ppermute | solution.py:37
  128.3 16.4 %collective-permute-start.14 = (bf16[3,128,1024]{2,1,0:T(8,128)(2,1)S(1)}, bf16[3,128,1024]{2,1,0:T(8,128)(2,1)S(1)}, u32[]{:S(2)}, u32[]{:S(2)}) collective-permute-start(bf16[3,128,1024]{2,1,0:T(8,128)(2,1)S(1)} %get-tuple-element.42), channel_id=1, source_target_pairs={{32,0},{64,32},{96,64},{0,96},{33,1},{65,33},{97,65},{1,97},{34,2}... | collective-permute-start | bytes 2359304 | tf_op jit(solution)/shard_map/ppermute | solution.py:37
  130.4 17.3 %collective-permute-start.15 = (bf16[3,128,1024]{2,1,0:T(8,128)(2,1)S(1)}, bf16[3,128,1024]{2,1,0:T(8,128)(2,1)S(1)}, u32[]{:S(2)}, u32[]{:S(2)}) collective-permute-start(bf16[3,128,1024]{2,1,0:T(8,128)(2,1)S(1)} %get-tuple-element.43), channel_id=1, source_target_pairs={{4,0},{0,4},{5,1},{1,5},{6,2},{2,6},{7,3},{3,7},{12,8},{8,12},{13,... | collective-permute-start | bytes 2359304 | tf_op jit(solution)/shard_map/ppermute | solution.py:37

commit v6 on v5

--- a/solution.py
+++ b/solution.py
@@ -48,8 +48,48 @@
     )
 
 
-def dispatch_kernel(first, k0, k1, k2, k3, *refs):
-    *blocks, message, logits, s0, s1, s2, s3, first_here, field, arrivals, loaded = refs
+def early_kernel(first, own, k0, k1, k2, k3, first_here, own_here, logits, loaded):
+    images = own.shape[0]
+    columns = jnp.concatenate([k0[...], k1[...], k2[...], k3[...]], axis=0)
+    blocks = [pltpu.make_async_copy(own.at[b], own_here.at[b], loaded.at[b]) for b in range(images)]
+    load = pltpu.make_async_copy(first, first_here, loaded.at[images])
+    for block in blocks:
+        block.start()
+    load.start()
+    for b in range(images):
+        blocks[b].wait()
+        logits[b] = lax.dot_general(
+            columns,
+            own_here[b],
+            (((1,), (1,)), ((), ())),
+            preferred_element_type=jnp.float32,
+        )
+    load.wait()
+
+
+def early(first, own, keys):
+    images, positions, _ = own.shape
+    slots = sum(key.shape[0] for key in keys)
+    return pl.pallas_call(
+        early_kernel,
+        out_shape=(
+            jax.ShapeDtypeStruct(first.shape, first.dtype),
+            jax.ShapeDtypeStruct(own.shape, own.dtype),
+            jax.ShapeDtypeStruct((images, slots, positions), jnp.float32),
+        ),
+        in_specs=[HBM] * 2 + [VMEM] * len(keys),
+        out_specs=(VMEM,) * 3,
+        scratch_shapes=[pltpu.SemaphoreType.DMA((images + 1,))],
+        cost_estimate=pl.CostEstimate(
+            flops=2 * slots * own.size, bytes_accessed=2 * first.size, transcendentals=0
+        ),
+        compiler_params=pltpu.CompilerParams(vmem_limit_bytes=40 * 1024 * 1024),
+        name="early",
+    )(first, own, *keys)
+
+
+def dispatch_kernel(own_logits, k0, k1, k2, k3, *refs):
+    *blocks, message, logits, s0, s1, s2, s3, field, arrivals = refs
     owners = message.shape[0]
     slots, features = 4 * k0.shape[0], k0.shape[1]
     own_slots, tiles = slots // owners, features // LANES
@@ -67,18 +107,17 @@
     for b in range(images):
         for copy in copies(b):
             copy.start()
-    load = pltpu.make_async_copy(first, first_here, loaded)
-    load.start()
 
     def one(b, carry):
         for copy in copies(b):
             copy.wait()
-        values = lax.dot_general(
+        near = lax.dot_general(
             columns,
-            field[b],
+            field[b, positions:],
             (((1,), (1,)), ((), ())),
             preferred_element_type=jnp.float32,
         )
+        values = jnp.concatenate([own_logits[b], near], axis=1)
         logits[b] = values
         row_top = jnp.max(values, axis=0, keepdims=True)
         row_total = jnp.sum(jnp.exp(values - row_top), axis=0, keepdims=True)
@@ -112,10 +151,9 @@
         return carry
 
     lax.fori_loop(0, images, one, 0)
-    load.wait()
-
-
-def dispatch(keys, first, blocks, own_slots):
+
+
+def dispatch(own_logits, keys, blocks, own_slots):
     images, positions, features = blocks[0].shape
     owners = sum(key.shape[0] for key in keys) // own_slots
     slots, width = owners * own_slots, len(blocks) * positions
@@ -127,14 +165,12 @@
             ),
             jax.ShapeDtypeStruct((images, slots, width), jnp.float32),
             *(jax.ShapeDtypeStruct((images, 2, positions), jnp.float32) for _ in blocks),
-            jax.ShapeDtypeStruct(first.shape, first.dtype),
-        ),
-        in_specs=[HBM] + [VMEM] * len(keys) + [HBM] + [ANY] * (len(blocks) - 1),
-        out_specs=(VMEM,) * (3 + len(blocks)),
+        ),
+        in_specs=[VMEM] + [VMEM] * len(keys) + [ANY] * len(blocks),
+        out_specs=(VMEM,) * (2 + len(blocks)),
         scratch_shapes=[
             pltpu.VMEM((images, width, features), jnp.bfloat16),
             pltpu.SemaphoreType.DMA((images, len(blocks))),
-            pltpu.SemaphoreType.DMA,
         ],
         cost_estimate=pl.CostEstimate(
             flops=4 * images * slots * width * features,
@@ -143,7 +179,7 @@
         ),
         compiler_params=pltpu.CompilerParams(vmem_limit_bytes=32 * 1024 * 1024),
         name="dispatch",
-    )(first, *keys, *blocks)
+    )(own_logits, *keys, *blocks)
 
 
 def merge_kernel(arrived, inputs):
@@ -257,41 +293,40 @@
     )(own, *pieces)
 
 
-def combine_kernel(logits, everyone, *refs):
-    stats, outs = refs[:4], refs[4:]
+def combine_kernel(blocks, logits, everyone, *refs):
+    stats, outs = refs[: len(blocks)], refs[len(blocks) :]
     images, positions, _ = outs[0].shape
     owners = everyone.shape[0]
 
     def one(b, carry):
         outputs = jnp.concatenate([everyone[place(k), b] for k in range(owners)], axis=0)
-        for r in (3, 1, 2, 0):
-            values = logits[b, :, r * positions : (r + 1) * positions]
-            mix = jnp.exp(values - stats[r][b][0:1]).astype(jnp.bfloat16)
-            outs[r][b] = lax.dot_general(
+        for block, stat, out in zip(blocks, stats, outs):
+            values = logits[b, :, block * positions : (block + 1) * positions]
+            mix = jnp.exp(values - stat[b][0:1]).astype(jnp.bfloat16)
+            out[b] = lax.dot_general(
                 mix, outputs, (((0,), (0,)), ((), ())), preferred_element_type=jnp.float32
-            ).astype(outs[r].dtype)
+            ).astype(out.dtype)
         return carry
 
     lax.fori_loop(0, images, one, 0)
 
 
-def combine(logits, everyone, stats):
-    images, slots, width = logits.shape
-    shape = (images, width // len(stats), everyone.shape[3])
-    kinds = (jnp.float32, jnp.bfloat16, jnp.bfloat16, jnp.bfloat16)
-    return pl.pallas_call(
-        combine_kernel,
-        out_shape=[jax.ShapeDtypeStruct(shape, kind) for kind in kinds],
-        in_specs=[VMEM] * (2 + len(stats)),
-        out_specs=(VMEM,) * len(kinds),
-        cost_estimate=pl.CostEstimate(
-            flops=2 * images * slots * width * shape[2],
-            bytes_accessed=4 * images * slots * width,
-            transcendentals=images * slots * width,
+def combine(blocks, kind, logits, everyone, stats):
+    images, slots, _ = logits.shape
+    shape = (images, stats[0].shape[2], everyone.shape[3])
+    return pl.pallas_call(
+        functools.partial(combine_kernel, blocks),
+        out_shape=[jax.ShapeDtypeStruct(shape, kind) for _ in blocks],
+        in_specs=[VMEM] * (2 + len(blocks)),
+        out_specs=[VMEM] * len(blocks),
+        cost_estimate=pl.CostEstimate(
+            flops=2 * len(blocks) * slots * images * shape[1] * shape[2],
+            bytes_accessed=4 * logits.size,
+            transcendentals=logits.size,
         ),
         compiler_params=pltpu.CompilerParams(vmem_limit_bytes=ROOM),
         name="combine",
-    )(logits, everyone, *stats)
+    )(logits, everyone, *(stats[block] for block in blocks))
 
 
 def finish_kernel(*refs):
@@ -306,10 +341,13 @@
         shares = [scale / total for scale in scales]
         shares = jnp.concatenate(shares + [jnp.zeros((LANES - 4, positions), jnp.float32)], axis=0)
         shares = shares.T
-        joined = sum(
-            shares[:, k : k + 1] * part[b].astype(jnp.float32) for k, part in enumerate(parts)
-        )
-        ready[b] = joined.astype(out.dtype)
+        for t in range(out.shape[2] // LANES):
+            lanes = slice(t * LANES, (t + 1) * LANES)
+            joined = sum(
+                shares[:, k : k + 1] * part[b, :, lanes].astype(jnp.float32)
+                for k, part in enumerate(parts)
+            )
+            ready[b, :, lanes] = joined.astype(out.dtype)
         copies[b].start()
     for copy in copies:
         copy.wait()
@@ -341,9 +379,8 @@
     near = [ahead(tokens, X, 1), ahead(tokens, X, 3), ahead(tokens, Y, 1)]
     pair = jnp.concatenate([slot_keys.T, pair], axis=0)
     keys = [pair, *(ahead(pair, Z, k) for k in (1, 2, 3))]
-    message, logits, *stats, first = dispatch(
-        keys, expert_in, [tokens, *near], slot_keys.shape[1]
-    )
+    first, own, own_logits = early(expert_in, tokens, keys)
+    message, logits, *stats = dispatch(own_logits, keys, [own, *near], slot_keys.shape[1])
     arrived = all_to_all(message)
     slot_inputs = merge(arrived, (tokens.shape[0], *slot_keys.shape[::-1]))
     rows = lax.all_gather(slot_inputs, "dp", axis=0, tiled=True)
@@ -352,8 +389,9 @@
     back = [ahead(stats[1], X, 3), ahead(stats[2], X, 1), ahead(stats[3], Y, 1)]
     pieces, back = lax.optimization_barrier((pieces, back))
     everyone = all_to_all(spread(own, pieces, owners))
-    own, right, left, up = combine(logits, everyone, stats)
-    parts = [own, ahead(right, X, 3), ahead(left, X, 1), ahead(up, Y, 1)]
+    right, left, up = combine((1, 2, 3), jnp.bfloat16, logits, everyone, stats)
+    parts = [ahead(right, X, 3), ahead(left, X, 1), ahead(up, Y, 1)]
+    parts = [*combine((0,), jnp.float32, logits, everyone, stats), *parts]
     return finish(parts, [stats[0], *back])
 
 

time: 150 us -> 156 us (1.040)
  Pallas kernels: 10.9 us -> 14.8 us
  blocking collectives: 64.5 us -> 67.4 us
    pallas_call x1 -> x3, Pallas kernels: 1.45 us -> 5.67 us  [the longest x1 3.65 us: early(): pl.pallas_call(early_kernel, out_shape=(jax.ShapeDtypeStruct(first.shape,...]
    all_to_all x2, blocking collectives: 55.8 us -> 59.6 us  [all_to_all(): lax.all_to_all(array, SLOT, split_axis=0, concat_axis=0, axis_index_group...]
    ppermute x12, starting transfers between devices: 20.7 us -> 19.1 us  [ahead(): lax.ppermute(array, axis, [((i + step) % size, i) for i in range(size)])]
  transfers between devices with their start and end apart: 16 -> 16, of which waited for: 8 -> 8; matrix products, arithmetic and copies ran while one was open for 1% -> 1% of each run, Pallas kernels for 0% -> 3%
where the time goes in v6:
time: 156 us
  blocking collectives  67.4 us (43%)
  waiting for transfers between devices  48.4 us (31%)
  starting transfers between devices  23.1 us (15%)
  Pallas kernels  14.8 us (9%)
    all_to_all x2, blocking collectives, all_to_all(): lax.all_to_all(array, SLOT, split_axis=0, concat_axis=0, axis_index_group...  59.6 us
    ppermute x12, waiting for transfers between devices, ahead(): lax.ppermute(array, axis, [((i + step) % size, i) for i in range(size)])  30 us
    ppermute x12, starting transfers between devices, ahead(): lax.ppermute(array, axis, [((i + step) % size, i) for i in range(size)])  19.1 us
    ppermute x1, waiting for transfers between devices, shards(): pair = lax.ppermute(slot_keys.T, SLOT, PARTNER)  18.4 us
    all_gather x1, blocking collectives, shards(): rows = lax.all_gather(slot_inputs, 'dp', axis=0, tiled=True)  7.78 us
    pallas_call x1, Pallas kernels, early(): pl.pallas_call(early_kernel, out_shape=(jax.ShapeDtypeStruct(first.shape,...  3.65 us
    pallas_call x1, Pallas kernels, run_experts(): pl.pallas_call(expert_kernel, out_shape=[jax.ShapeDtypeStruct(shape, kind...  3.47 us
    pallas_call x1, Pallas kernels, dispatch(): pl.pallas_call(dispatch_kernel, out_shape=(jax.ShapeDtypeStruct((owners,...  3.33 us
  transfers between devices with their start and end apart: 16, of which 8 were waited for; matrix products, arithmetic and copies ran while one was open for 1% of the time, Pallas kernels for 3%

profile of v6, /device:TPU:0, one launch (start us, length us, event | category | flops | bytes accessed | tf_op | source)
XLA Modules:
  0.0 155.8 jit_solution(5281781605662138658)
XLA Ops:
  0.0 2.9 %collective-permute-start.4 = (bf16[3,128,1024]{2,1,0:T(8,128)(2,1)}, bf16[3,128,1024]{2,1,0:T(8,128)(2,1)S(1)}, u32[]{:S(2)}, u32[]{:S(2)}) collective-permute-start(bf16[3,128,1024]{2,1,0:T(8,128)(2,1)} %own.1), channel_id=1, source_target_pairs={{32,0},{64,32},{96,64},{0,96},{33,1},{65,33},{97,65},{1,97},{34,2}... | collective-permute-start | bytes 2359304 | tf_op jit(solution)/shard_map/ppermute | solution.py:37
  2.9 3.2 %collective-permute-start.6 = (bf16[3,128,1024]{2,1,0:T(8,128)(2,1)}, bf16[3,128,1024]{2,1,0:T(8,128)(2,1)S(1)}, u32[]{:S(2)}, u32[]{:S(2)}) collective-permute-start(bf16[3,128,1024]{2,1,0:T(8,128)(2,1)} %own.1), channel_id=1, source_target_pairs={{4,0},{0,4},{5,1},{1,5},{6,2},{2,6},{7,3},{3,7},{12,8},{8,12},{13,... | collective-permute-start | bytes 2359304 | tf_op jit(solution)/shard_map/ppermute | solution.py:37
  6.1 0.0 collective-permute-start.5
  6.1 2.1 %collective-permute-start = (bf16[32,1024]{1,0:T(8,128)(2,1)}, bf16[32,1024]{1,0:T(8,128)(2,1)S(1)}, u32[]{:S(2)}, u32[]{:S(2)}) collective-permute-start(bf16[32,1024]{1,0:T(8,128)(2,1)} %bitcast.3), channel_id=1, source_target_pairs={{0,68},{4,64},{8,76},{12,72},{16,84},{20,80},{24,92},{28,88},{32,1... | collective-permute-start | bytes 196616 | tf_op jit(solution)/shard_map/ppermute | solution.py:378
  8.1 18.4 %collective-permute-done = bf16[32,1024]{1,0:T(8,128)(2,1)S(1)} collective-permute-done((bf16[32,1024]{1,0:T(8,128)(2,1)}, bf16[32,1024]{1,0:T(8,128)(2,1)S(1)}, u32[]{:S(2)}, u32[]{:S(2)}) %collective-permute-start) | collective-permute-done | bytes 65568 | tf_op jit(solution)/shard_map/ppermute | solution.py:378
  26.5 0.8 pad_maximum_fusion.k0
  27.4 2.0 %collective-permute-start.3 = (bf16[64,1024]{1,0:T(8,128)(2,1)S(1)}, bf16[64,1024]{1,0:T(8,128)(2,1)S(1)}, u32[]{:S(2)}, u32[]{:S(2)}) collective-permute-start(bf16[64,1024]{1,0:T(8,128)(2,1)S(1)} %pad_maximum_fusion.k0), channel_id=1, source_target_pairs={{24,0},{0,8},{8,16},{16,24},{25,1},{1,9},{9,17},{17,25},{26,2},{2,... | collective-permute-start | bytes 393224 | tf_op jit(solution)/shard_map/ppermute | solution.py:37
  29.4 3.6 %collective-permute-start.2 = (bf16[64,1024]{1,0:T(8,128)(2,1)S(1)}, bf16[64,1024]{1,0:T(8,128)(2,1)S(1)}, u32[]{:S(2)}, u32[]{:S(2)}) collective-permute-start(bf16[64,1024]{1,0:T(8,128)(2,1)S(1)} %pad_maximum_fusion.k0), channel_id=1, source_target_pairs={{16,0},{24,8},{0,16},{8,24},{17,1},{25,9},{1,17},{9,25},{18,2},{26... | collective-permute-start | bytes 393224 | tf_op jit(solution)/shard_map/ppermute | solution.py:37
  33.0 2.8 %collective-permute-done.3.k3 = bf16[64,1024]{1,0:T(8,128)(2,1)S(1)} collective-permute-done((bf16[64,1024]{1,0:T(8,128)(2,1)S(1)}, bf16[64,1024]{1,0:T(8,128)(2,1)S(1)}, u32[]{:S(2)}, u32[]{:S(2)}) %collective-permute-start.3) | collective-permute-done | bytes 131104 | tf_op jit(solution)/shard_map/ppermute | solution.py:37
  35.8 0.7 collective-permute-start.1
  36.5 0.8 collective-permute-done.2.k2
  37.3 3.4 %collective-permute-done.1.k1 = bf16[64,1024]{1,0:T(8,128)(2,1)S(1)} collective-permute-done((bf16[64,1024]{1,0:T(8,128)(2,1)S(1)}, bf16[64,1024]{1,0:T(8,128)(2,1)S(1)}, u32[]{:S(2)}, u32[]{:S(2)}) %collective-permute-start.1) | collective-permute-done | bytes 131104 | tf_op jit(solution)/shard_map/ppermute | solution.py:37
  40.7 1.1 copy-done
  41.9 3.7 %early.1 = (bf16[4,1024,1024]{2,1,0:T(8,128)(2,1)S(1)}, bf16[3,128,1024]{2,1,0:T(8,128)(2,1)S(1)}, f32[3,256,128]{2,1,0:T(8,128)S(1)}) custom-call(bf16[4,1024,1024]{2,1,0:T(8,128)(2,1)} %first.1, bf16[3,128,1024]{2,1,0:T(8,128)(2,1)S(1)} %copy-done, bf16[64,1024]{1,0:T(8,128)(2,1)S(1)} %pad_maximum_fusion.k0, ...), custom_call_target="tpu_custom_call" | custom-call | flops 201326592 | bytes 8388608 | tf_op jit(solution)/shard_map/early/pallas_call | solution.py:73
  45.5 0.0 collective-permute-done.4.refs_1_
  45.5 0.0 collective-permute-done.6.refs_3_
  45.5 0.0 collective-permute-done.5.refs_2_
  45.6 0.0 slice-start.1
  45.6 3.3 %dispatch.1 = (bf16[8,792,128]{2,1,0:T(8,128)(2,1)S(1)}, f32[3,256,512]{2,1,0:T(8,128)S(1)}, f32[3,2,128]{2,1,0:T(2,128)S(1)}, f32[3,2,128]{2,1,0:T(2,128)S(1)},...) custom-call(f32[3,256,128]{2,1,0:T(8,128)S(1)} %get-tuple-element.27.own_logits, ...), custom_call_target="tpu_custom_call" | custom-call | flops 1610612736 | bytes 3145728 | tf_op jit(solution)/shard_map/dispatch/pallas_call | solution.py:160
  48.9 29.4 %all_to_all.10.arrived = bf16[8,792,128]{2,1,0:T(8,128)(2,1)S(1)} all-to-all(bf16[8,792,128]{2,1,0:T(8,128)(2,1)S(1)} %get-tuple-element.30), channel_id=1, replica_groups={{0,8,16,24,68,76,84,92},{32,40,48,56,100,108,116,124},{64,72,80,88,4,12..., dimensions={0} | all-to-all | bytes 3244032 | tf_op jit(solution)/shard_map/all_to_all | solution.py:46
  78.3 0.5 merge.1
  78.8 7.8 %all_gather.3.rows = bf16[12,32,1024]{2,1,0:T(8,128)(2,1)S(1)} all-gather(bf16[3,32,1024]{2,1,0:T(8,128)(2,1)S(1)} %merge.1), channel_id=1, replica_groups=mesh['slot_0'=4,'slot_1'=4,'slot_2'=2,'dp'=4] {'dp'}, dimensions={0}, use_global_device_ids=true | all-gather | bytes 983040 | tf_op jit(solution)/shard_map/all_gather | solution.py:386
  86.6 0.0 slice-done
  86.6 0.0 slice-done.1
  86.6 3.5 %experts.1 = (f32[3,32,1024]{2,1,0:T(8,128)S(1)}, bf16[3,32,1024]{2,1,0:T(8,128)(2,1)S(1)}, bf16[3,32,1024]{2,1,0:T(8,128)(2,1)S(1)}, bf16[3,32,1024]{2,1,0:T(8,128)(2,1)S(1)}) custom-call(bf16[12,32,1024]{2,1,0:T(8,128)(2,1)S(1)} %all_gather.3.rows, bf16[4,1024,1024]{2,1,0:T(8,128)(2,1)S(1)} %get-tuple-element.31.first, bf16[4,1024,1024]{2,1,0:T(8,128)(2,1)S(1)} %bitcast.2), custom_call_target="tpu_custom_call" | custom-call | flops 1610612736 | bytes 16777216 | tf_op jit(solution)/shard_map/experts/pallas_call | solution.py:258
  90.0 0.4 collective-permute-start.7
  90.5 1.3 collective-permute-start.8
  91.8 0.2 collective-permute-start.9
  92.0 0.0 collective-permute-start.10
  92.0 3.2 %collective-permute-start.11 = (f32[3,2,128]{2,1,0:T(2,128)S(1)}, f32[3,2,128]{2,1,0:T(2,128)S(1)}, u32[]{:S(2)}, u32[]{:S(2)}) collective-permute-start(f32[3,2,128]{2,1,0:T(2,128)S(1)} %get-tuple-element.37.refs_1_), channel_id=1, source_target_pairs={{32,0},{64,32},{96,64},{0,96},{33,1},{65,33},{97,65},{1,97},{34,2}... | collective-permute-start | bytes 9224 | tf_op jit(solution)/shard_map/ppermute | solution.py:37
  95.2 1.6 %collective-permute-done.10.refs_5_ = f32[3,2,128]{2,1,0:T(2,128)S(1)} collective-permute-done((f32[3,2,128]{2,1,0:T(2,128)S(1)}, f32[3,2,128]{2,1,0:T(2,128)S(1)}, u32[]{:S(2)}, u32[]{:S(2)}) %collective-permute-start.10) | collective-permute-done | bytes 3104 | tf_op jit(solution)/shard_map/ppermute | solution.py:37
  96.8 0.3 collective-permute-start.12
  97.1 0.0 collective-permute-done.11.refs_6_
  97.1 4.8 %collective-permute-done.12.refs_7_ = f32[3,2,128]{2,1,0:T(2,128)S(1)} collective-permute-done((f32[3,2,128]{2,1,0:T(2,128)S(1)}, f32[3,2,128]{2,1,0:T(2,128)S(1)}, u32[]{:S(2)}, u32[]{:S(2)}) %collective-permute-start.12) | collective-permute-done | bytes 3104 | tf_op jit(solution)/shard_map/ppermute | solution.py:37
  101.9 0.0 collective-permute-done.7.first
  101.9 0.0 collective-permute-done.8.second
  101.9 0.0 collective-permute-done.9.third
  101.9 0.1 spread.1
  102.0 30.2 %all_to_all.11.everyone = bf16[8,3,32,1024]{3,2,1,0:T(8,128)(2,1)S(1)} all-to-all(bf16[8,3,32,1024]{3,2,1,0:T(8,128)(2,1)S(1)} %spread.1), channel_id=1, replica_groups={{0,8,16,24,68,76,84,92},{32,40,48,56,100,108,116,124},{64,72,80,88,4,12..., dimensions={0} | all-to-all | bytes 3145728 | tf_op jit(solution)/shard_map/all_to_all | solution.py:46
  132.2 1.2 combine.3
  133.5 0.1 collective-permute-start.13
  133.5 3.2 %collective-permute-start.14 = (bf16[3,128,1024]{2,1,0:T(8,128)(2,1)S(1)}, bf16[3,128,1024]{2,1,0:T(8,128)(2,1)S(1)}, u32[]{:S(2)}, u32[]{:S(2)}) collective-permute-start(bf16[3,128,1024]{2,1,0:T(8,128)(2,1)S(1)} %get-tuple-element.44), channel_id=1, source_target_pairs={{32,0},{64,32},{96,64},{0,96},{33,1},{65,33},{97,65},{1,97},{34,2}... | collective-permute-start | bytes 2359304 | tf_op jit(solution)/shard_map/ppermute | solution.py:37
  136.8 0.0 collective-permute-start.15
  136.8 0.8 combine.2.refs_0_
  137.6 13.6 %collective-permute-done.13.refs_1_ = bf16[3,128,1024]{2,1,0:T(8,128)(2,1)S(1)} collective-permute-done((bf16[3,128,1024]{2,1,0:T(8,128)(2,1)S(1)}, bf16[3,128,1024]{2,1,0:T(8,128)(2,1)S(1)}, u32[]{:S(2)}, u32[]{:S(2)}) %collective-permute-start.13) | collective-permute-done | bytes 786464 | tf_op jit(solution)/shard_map/ppermute | solution.py:37
  151.1 0.0 collective-permute-done.14.refs_2_
  151.1 3.0 %collective-permute-done.15.refs_3_ = bf16[3,128,1024]{2,1,0:T(8,128)(2,1)S(1)} collective-permute-done((bf16[3,128,1024]{2,1,0:T(8,128)(2,1)S(1)}, bf16[3,128,1024]{2,1,0:T(8,128)(2,1)S(1)}, u32[]{:S(2)}, u32[]{:S(2)}) %collective-permute-start.15) | collective-permute-done | bytes 786464 | tf_op jit(solution)/shard_map/ppermute | solution.py:37
  154.1 1.7 %finish.1 = bf16[3,128,1024]{2,1,0:T(8,128)(2,1)} custom-call(f32[3,128,1024]{2,1,0:T(8,128)S(1)} %combine.2.refs_0_, bf16[3,128,1024]{2,1,0:T(8,128)(2,1)S(1)} %collective-permute-done.13.refs_1_, bf16[3,128,1024]{2,1,0:T(8,128)(2,1)S(1)} %collective-permute-done.14.refs_2_, bf16[3,128,1024]{2,1,0:T(8,128)(2,1)S(1)} %collective-permute-done.15.refs_3_, ...), custom_call_target="tpu_custom_call" | custom-call | flops 3145728 | bytes 4718592 | tf_op jit(solution)/shard_map/finish/pallas_call | solution.py:358
  (3 shorter events, 0.0 us)
Async XLA Ops:
  0.0 45.5 %collective-permute-start.4 = (bf16[3,128,1024]{2,1,0:T(8,128)(2,1)}, bf16[3,128,1024]{2,1,0:T(8,128)(2,1)S(1)}, u32[]{:S(2)}, u32[]{:S(2)}) collective-permute-start(bf16[3,128,1024]{2,1,0:T(8,128)(2,1)} %own.1), channel_id=1, source_target_pairs={{32,0},{64,32},{96,64},{0,96},{33,1},{65,33},{97,65},{1,97},{34,2}... | collective-permute-start | bytes 2359304 | tf_op jit(solution)/shard_map/ppermute | solution.py:37
  2.9 42.7 %collective-permute-start.6 = (bf16[3,128,1024]{2,1,0:T(8,128)(2,1)}, bf16[3,128,1024]{2,1,0:T(8,128)(2,1)S(1)}, u32[]{:S(2)}, u32[]{:S(2)}) collective-permute-start(bf16[3,128,1024]{2,1,0:T(8,128)(2,1)} %own.1), channel_id=1, source_target_pairs={{4,0},{0,4},{5,1},{1,5},{6,2},{2,6},{7,3},{3,7},{12,8},{8,12},{13,... | collective-permute-start | bytes 2359304 | tf_op jit(solution)/shard_map/ppermute | solution.py:37
  6.1 39.5 %collective-permute-start.5 = (bf16[3,128,1024]{2,1,0:T(8,128)(2,1)}, bf16[3,128,1024]{2,1,0:T(8,128)(2,1)S(1)}, u32[]{:S(2)}, u32[]{:S(2)}) collective-permute-start(bf16[3,128,1024]{2,1,0:T(8,128)(2,1)} %own.1), channel_id=1, source_target_pairs={{96,0},{0,32},{32,64},{64,96},{97,1},{1,33},{33,65},{65,97},{98,2}... | collective-permute-start | bytes 2359304 | tf_op jit(solution)/shard_map/ppermute | solution.py:37
  6.1 20.5 %collective-permute-start = (bf16[32,1024]{1,0:T(8,128)(2,1)}, bf16[32,1024]{1,0:T(8,128)(2,1)S(1)}, u32[]{:S(2)}, u32[]{:S(2)}) collective-permute-start(bf16[32,1024]{1,0:T(8,128)(2,1)} %bitcast.3), channel_id=1, source_target_pairs={{0,68},{4,64},{8,76},{12,72},{16,84},{20,80},{24,92},{28,88},{32,1... | collective-permute-start | bytes 196616 | tf_op jit(solution)/shard_map/ppermute | solution.py:378
  27.4 8.4 %collective-permute-start.3 = (bf16[64,1024]{1,0:T(8,128)(2,1)S(1)}, bf16[64,1024]{1,0:T(8,128)(2,1)S(1)}, u32[]{:S(2)}, u32[]{:S(2)}) collective-permute-start(bf16[64,1024]{1,0:T(8,128)(2,1)S(1)} %pad_maximum_fusion.k0), channel_id=1, source_target_pairs={{24,0},{0,8},{8,16},{16,24},{25,1},{1,9},{9,17},{17,25},{26,2},{2,... | collective-permute-start | bytes 393224 | tf_op jit(solution)/shard_map/ppermute | solution.py:37
  29.4 7.9 %collective-permute-start.2 = (bf16[64,1024]{1,0:T(8,128)(2,1)S(1)}, bf16[64,1024]{1,0:T(8,128)(2,1)S(1)}, u32[]{:S(2)}, u32[]{:S(2)}) collective-permute-start(bf16[64,1024]{1,0:T(8,128)(2,1)S(1)} %pad_maximum_fusion.k0), channel_id=1, source_target_pairs={{16,0},{24,8},{0,16},{8,24},{17,1},{25,9},{1,17},{9,25},{18,2},{26... | collective-permute-start | bytes 393224 | tf_op jit(solution)/shard_map/ppermute | solution.py:37
  35.8 5.0 %collective-permute-start.1 = (bf16[64,1024]{1,0:T(8,128)(2,1)S(1)}, bf16[64,1024]{1,0:T(8,128)(2,1)S(1)}, u32[]{:S(2)}, u32[]{:S(2)}) collective-permute-start(bf16[64,1024]{1,0:T(8,128)(2,1)S(1)} %pad_maximum_fusion.k0), channel_id=1, source_target_pairs={{8,0},{16,8},{24,16},{0,24},{9,1},{17,9},{25,17},{1,25},{10,2},{18... | collective-permute-start | bytes 393224 | tf_op jit(solution)/shard_map/ppermute | solution.py:37
  40.7 1.1 copy-start
  41.9 44.7 %slice-start = ((s8[8388608]{0:T(1024)(128)(4,1)}), s8[4194304]{0:T(1024)(128)(4,1)S(1)}, s32[]{:S(2)}) async-start(s8[8388608]{0:T(1024)(128)(4,1)} %bitcast.1), calls=%async_computation.2 | async-start | bytes 8388608
  45.6 41.0 %slice-start.1 = ((s8[8388608]{0:T(1024)(128)(4,1)}), s8[4194304]{0:T(1024)(128)(4,1)S(1)}, s32[]{:S(2)}) async-start(s8[8388608]{0:T(1024)(128)(4,1)} %bitcast.1), calls=%async_computation.3 | async-start | bytes 8388608
  90.0 11.9 %collective-permute-start.7 = (bf16[3,32,1024]{2,1,0:T(8,128)(2,1)S(1)}, bf16[3,32,1024]{2,1,0:T(8,128)(2,1)S(1)}, u32[]{:S(2)}, u32[]{:S(2)}) collective-permute-start(bf16[3,32,1024]{2,1,0:T(8,128)(2,1)S(1)} %get-tuple-element.33), channel_id=1, source_target_pairs={{0,1},{1,0},{2,3},{3,2},{4,5},{5,4},{6,7},{7,6},{8,9},{9,8},{10,11... | collective-permute-start | bytes 589832 | tf_op jit(solution)/shard_map/ppermute | solution.py:42
  90.5 11.4 %collective-permute-start.8 = (bf16[3,32,1024]{2,1,0:T(8,128)(2,1)S(1)}, bf16[3,32,1024]{2,1,0:T(8,128)(2,1)S(1)}, u32[]{:S(2)}, u32[]{:S(2)}) collective-permute-start(bf16[3,32,1024]{2,1,0:T(8,128)(2,1)S(1)} %get-tuple-element.34), channel_id=1, source_target_pairs={{0,2},{1,3},{2,0},{3,1},{4,6},{5,7},{6,4},{7,5},{8,10},{9,11},{10,... | collective-permute-start | bytes 589832 | tf_op jit(solution)/shard_map/ppermute | solution.py:42
  91.8 10.1 %collective-permute-start.9 = (bf16[3,32,1024]{2,1,0:T(8,128)(2,1)S(1)}, bf16[3,32,1024]{2,1,0:T(8,128)(2,1)S(1)}, u32[]{:S(2)}, u32[]{:S(2)}) collective-permute-start(bf16[3,32,1024]{2,1,0:T(8,128)(2,1)S(1)} %get-tuple-element.35), channel_id=1, source_target_pairs={{0,3},{1,2},{2,1},{3,0},{4,7},{5,6},{6,5},{7,4},{8,11},{9,10},{10,... | collective-permute-start | bytes 589832 | tf_op jit(solution)/shard_map/ppermute | solution.py:42
  92.0 4.8 %collective-permute-start.10 = (f32[3,2,128]{2,1,0:T(2,128)S(1)}, f32[3,2,128]{2,1,0:T(2,128)S(1)}, u32[]{:S(2)}, u32[]{:S(2)}) collective-permute-start(f32[3,2,128]{2,1,0:T(2,128)S(1)} %get-tuple-element.36.refs_0_), channel_id=1, source_target_pairs={{96,0},{0,32},{32,64},{64,96},{97,1},{1,33},{33,65},{65,97},{98,2}... | collective-permute-start | bytes 9224 | tf_op jit(solution)/shard_map/ppermute | solution.py:37
  92.0 5.1 %collective-permute-start.11 = (f32[3,2,128]{2,1,0:T(2,128)S(1)}, f32[3,2,128]{2,1,0:T(2,128)S(1)}, u32[]{:S(2)}, u32[]{:S(2)}) collective-permute-start(f32[3,2,128]{2,1,0:T(2,128)S(1)} %get-tuple-element.37.refs_1_), channel_id=1, source_target_pairs={{32,0},{64,32},{96,64},{0,96},{33,1},{65,33},{97,65},{1,97},{34,2}... | collective-permute-start | bytes 9224 | tf_op jit(solution)/shard_map/ppermute | solution.py:37
  96.8 5.1 %collective-permute-start.12 = (f32[3,2,128]{2,1,0:T(2,128)S(1)}, f32[3,2,128]{2,1,0:T(2,128)S(1)}, u32[]{:S(2)}, u32[]{:S(2)}) collective-permute-start(f32[3,2,128]{2,1,0:T(2,128)S(1)} %get-tuple-element.38.refs_2_), channel_id=1, source_target_pairs={{4,0},{0,4},{5,1},{1,5},{6,2},{2,6},{7,3},{3,7},{12,8},{8,12},{13,... | collective-permute-start | bytes 9224 | tf_op jit(solution)/shard_map/ppermute | solution.py:37
  133.5 17.7 %collective-permute-start.13 = (bf16[3,128,1024]{2,1,0:T(8,128)(2,1)S(1)}, bf16[3,128,1024]{2,1,0:T(8,128)(2,1)S(1)}, u32[]{:S(2)}, u32[]{:S(2)}) collective-permute-start(bf16[3,128,1024]{2,1,0:T(8,128)(2,1)S(1)} %get-tuple-element.43), channel_id=1, source_target_pairs={{96,0},{0,32},{32,64},{64,96},{97,1},{1,33},{33,65},{65,97},{98,2}... | collective-permute-start | bytes 2359304 | tf_op jit(solution)/shard_map/ppermute | solution.py:37
  133.5 17.6 %collective-permute-start.14 = (bf16[3,128,1024]{2,1,0:T(8,128)(2,1)S(1)}, bf16[3,128,1024]{2,1,0:T(8,128)(2,1)S(1)}, u32[]{:S(2)}, u32[]{:S(2)}) collective-permute-start(bf16[3,128,1024]{2,1,0:T(8,128)(2,1)S(1)} %get-tuple-element.44), channel_id=1, source_target_pairs={{32,0},{64,32},{96,64},{0,96},{33,1},{65,33},{97,65},{1,97},{34,2}... | collective-permute-start | bytes 2359304 | tf_op jit(solution)/shard_map/ppermute | solution.py:37
  136.8 17.3 %collective-permute-start.15 = (bf16[3,128,1024]{2,1,0:T(8,128)(2,1)S(1)}, bf16[3,128,1024]{2,1,0:T(8,128)(2,1)S(1)}, u32[]{:S(2)}, u32[]{:S(2)}) collective-permute-start(bf16[3,128,1024]{2,1,0:T(8,128)(2,1)S(1)} %get-tuple-element.45), channel_id=1, source_target_pairs={{4,0},{0,4},{5,1},{1,5},{6,2},{2,6},{7,3},{3,7},{12,8},{8,12},{13,... | collective-permute-start | bytes 2359304 | tf_op jit(solution)/shard_map/ppermute | solution.py:37

commit v7 on v6

--- a/solution.py
+++ b/solution.py
@@ -270,36 +270,34 @@
     )(rows, expert_in, expert_out)
 
 
-def spread_kernel(own, first, second, third, copies):
+def total_kernel(own, first, second, third, out):
     total = own[...]
     for piece in (first, second, third):
         total = total + piece[...].astype(jnp.float32)
-    total = total.astype(jnp.bfloat16)
-    for k in range(copies.shape[0]):
-        copies[k] = total
-
-
-def spread(own, pieces, count):
-    return pl.pallas_call(
-        spread_kernel,
-        out_shape=jax.ShapeDtypeStruct((count, *own.shape), jnp.bfloat16),
+    out[...] = total.astype(jnp.bfloat16)
+
+
+def add_up(own, pieces):
+    return pl.pallas_call(
+        total_kernel,
+        out_shape=jax.ShapeDtypeStruct(own.shape, jnp.bfloat16),
         in_specs=[VMEM] * 4,
         out_specs=VMEM,
         cost_estimate=pl.CostEstimate(
-            flops=4 * own.size, bytes_accessed=2 * count * own.size, transcendentals=0
+            flops=4 * own.size, bytes_accessed=12 * own.size, transcendentals=0
         ),
         compiler_params=pltpu.CompilerParams(vmem_limit_bytes=ROOM),
-        name="spread",
+        name="total",
     )(own, *pieces)
 
 
-def combine_kernel(blocks, logits, everyone, *refs):
+def combine_kernel(blocks, logits, *refs):
+    everyone, refs = refs[:8], refs[8:]
     stats, outs = refs[: len(blocks)], refs[len(blocks) :]
     images, positions, _ = outs[0].shape
-    owners = everyone.shape[0]
 
     def one(b, carry):
-        outputs = jnp.concatenate([everyone[place(k), b] for k in range(owners)], axis=0)
+        outputs = jnp.concatenate([piece[b] for piece in everyone], axis=0)
         for block, stat, out in zip(blocks, stats, outs):
             values = logits[b, :, block * positions : (block + 1) * positions]
             mix = jnp.exp(values - stat[b][0:1]).astype(jnp.bfloat16)
@@ -313,11 +311,11 @@
 
 def combine(blocks, kind, logits, everyone, stats):
     images, slots, _ = logits.shape
-    shape = (images, stats[0].shape[2], everyone.shape[3])
+    shape = (images, stats[0].shape[2], everyone[0].shape[2])
     return pl.pallas_call(
         functools.partial(combine_kernel, blocks),
         out_shape=[jax.ShapeDtypeStruct(shape, kind) for _ in blocks],
-        in_specs=[VMEM] * (2 + len(blocks)),
+        in_specs=[VMEM] * (1 + len(everyone) + len(blocks)),
         out_specs=[VMEM] * len(blocks),
         cost_estimate=pl.CostEstimate(
             flops=2 * len(blocks) * slots * images * shape[1] * shape[2],
@@ -326,7 +324,7 @@
         ),
         compiler_params=pltpu.CompilerParams(vmem_limit_bytes=ROOM),
         name="combine",
-    )(logits, everyone, *(stats[block] for block in blocks))
+    )(logits, *everyone, *(stats[block] for block in blocks))
 
 
 def finish_kernel(*refs):
@@ -374,7 +372,6 @@
 
 def shards(tokens, slot_keys, expert_in, expert_out):
     ranks = lax.axis_size("dp")
-    owners = len(TILE[0])
     pair = lax.ppermute(slot_keys.T, SLOT, PARTNER)
     near = [ahead(tokens, X, 1), ahead(tokens, X, 3), ahead(tokens, Y, 1)]
     pair = jnp.concatenate([slot_keys.T, pair], axis=0)
@@ -388,7 +385,13 @@
     pieces = [swapped(piece, "dp", k) for k, piece in zip((1, 2, 3), pieces)]
     back = [ahead(stats[1], X, 3), ahead(stats[2], X, 1), ahead(stats[3], Y, 1)]
     pieces, back = lax.optimization_barrier((pieces, back))
-    everyone = all_to_all(spread(own, pieces, owners))
+    here = add_up(own, pieces)
+    there = lax.ppermute(here, SLOT, PARTNER)
+    after, before = ahead(here, Z, 1), ahead(here, Z, 3)
+    across = ahead(here, Z, 2)
+    there_after, there_before = ahead(there, Z, 1), ahead(there, Z, 3)
+    there_across = ahead(there_before, Z, 3)
+    everyone = [here, there, after, there_after, across, there_across, before, there_before]
     right, left, up = combine((1, 2, 3), jnp.bfloat16, logits, everyone, stats)
     parts = [ahead(right, X, 3), ahead(left, X, 1), ahead(up, Y, 1)]
     parts = [*combine((0,), jnp.float32, logits, everyone, stats), *parts]

time: 156 us -> 157 us (level)
  blocking collectives: 67.4 us -> 37.2 us
  waiting for transfers between devices: 48.4 us -> 69.5 us
  starting transfers between devices: 23.1 us -> 33.6 us
    all_to_all x2 -> x1, blocking collectives: 59.6 us -> 29.4 us  [all_to_all(): lax.all_to_all(array, SLOT, split_axis=0, concat_axis=0, axis_index_group...]
    ppermute x12 -> x18, waiting for transfers between devices: 30 us -> 44.7 us  [ahead(): lax.ppermute(array, axis, [((i + step) % size, i) for i in range(size)])]
    ppermute x0 -> x1, waiting for transfers between devices: none -> 6.43 us  [shards(): there = lax.ppermute(here, SLOT, PARTNER)]
    ppermute x12 -> x18, starting transfers between devices: 19.1 us -> 25.3 us  [ahead(): lax.ppermute(array, axis, [((i + step) % size, i) for i in range(size)])]
    ppermute x0 -> x1, starting transfers between devices: none -> 4.26 us  [shards(): there = lax.ppermute(here, SLOT, PARTNER)]
  transfers between devices with their start and end apart: 16 -> 23, of which waited for: 8 -> 12; matrix products, arithmetic and copies ran while one was open for 1% -> 1% of each run, Pallas kernels for 3% -> 3%
where the time goes in v7:
time: 157 us
  waiting for transfers between devices  69.5 us (44%)
  blocking collectives  37.2 us (24%)
  starting transfers between devices  33.6 us (21%)
  Pallas kernels  14.7 us (9%)
    ppermute x18, waiting for transfers between devices, ahead(): lax.ppermute(array, axis, [((i + step) % size, i) for i in range(size)])  44.7 us
    all_to_all x1, blocking collectives, all_to_all(): lax.all_to_all(array, SLOT, split_axis=0, concat_axis=0, axis_index_group...  29.4 us
    ppermute x18, starting transfers between devices, ahead(): lax.ppermute(array, axis, [((i + step) % size, i) for i in range(size)])  25.3 us
    ppermute x1, waiting for transfers between devices, shards(): pair = lax.ppermute(slot_keys.T, SLOT, PARTNER)  18.4 us
    all_gather x1, blocking collectives, shards(): rows = lax.all_gather(slot_inputs, 'dp', axis=0, tiled=True)  7.78 us
    ppermute x1, waiting for transfers between devices, shards(): there = lax.ppermute(here, SLOT, PARTNER)  6.43 us
    ppermute x1, starting transfers between devices, shards(): there = lax.ppermute(here, SLOT, PARTNER)  4.26 us
    pallas_call x1, Pallas kernels, early(): pl.pallas_call(early_kernel, out_shape=(jax.ShapeDtypeStruct(first.shape,...  3.65 us
  transfers between devices with their start and end apart: 23, of which 12 were waited for; matrix products, arithmetic and copies ran while one was open for 1% of the time, Pallas kernels for 3%

profile of v7, /device:TPU:0, one launch (start us, length us, event | category | flops | bytes accessed | tf_op | source)
XLA Modules:
  0.0 157.2 jit_solution(10222584497234978355)
XLA Ops:
  0.0 2.9 %collective-permute-start.4 = (bf16[3,128,1024]{2,1,0:T(8,128)(2,1)}, bf16[3,128,1024]{2,1,0:T(8,128)(2,1)S(1)}, u32[]{:S(2)}, u32[]{:S(2)}) collective-permute-start(bf16[3,128,1024]{2,1,0:T(8,128)(2,1)} %own.1), channel_id=1, source_target_pairs={{32,0},{64,32},{96,64},{0,96},{33,1},{65,33},{97,65},{1,97},{34,2}... | collective-permute-start | bytes 2359304 | tf_op jit(solution)/shard_map/ppermute | solution.py:37
  2.9 3.2 %collective-permute-start.6 = (bf16[3,128,1024]{2,1,0:T(8,128)(2,1)}, bf16[3,128,1024]{2,1,0:T(8,128)(2,1)S(1)}, u32[]{:S(2)}, u32[]{:S(2)}) collective-permute-start(bf16[3,128,1024]{2,1,0:T(8,128)(2,1)} %own.1), channel_id=1, source_target_pairs={{4,0},{0,4},{5,1},{1,5},{6,2},{2,6},{7,3},{3,7},{12,8},{8,12},{13,... | collective-permute-start | bytes 2359304 | tf_op jit(solution)/shard_map/ppermute | solution.py:37
  6.1 0.0 collective-permute-start.5
  6.1 2.1 %collective-permute-start = (bf16[32,1024]{1,0:T(8,128)(2,1)}, bf16[32,1024]{1,0:T(8,128)(2,1)S(1)}, u32[]{:S(2)}, u32[]{:S(2)}) collective-permute-start(bf16[32,1024]{1,0:T(8,128)(2,1)} %bitcast.3), channel_id=1, source_target_pairs={{0,68},{4,64},{8,76},{12,72},{16,84},{20,80},{24,92},{28,88},{32,1... | collective-permute-start | bytes 196616 | tf_op jit(solution)/shard_map/ppermute | solution.py:375
  8.1 18.4 %collective-permute-done = bf16[32,1024]{1,0:T(8,128)(2,1)S(1)} collective-permute-done((bf16[32,1024]{1,0:T(8,128)(2,1)}, bf16[32,1024]{1,0:T(8,128)(2,1)S(1)}, u32[]{:S(2)}, u32[]{:S(2)}) %collective-permute-start) | collective-permute-done | bytes 65568 | tf_op jit(solution)/shard_map/ppermute | solution.py:375
  26.5 0.8 pad_maximum_fusion.k0
  27.4 2.0 %collective-permute-start.3 = (bf16[64,1024]{1,0:T(8,128)(2,1)S(1)}, bf16[64,1024]{1,0:T(8,128)(2,1)S(1)}, u32[]{:S(2)}, u32[]{:S(2)}) collective-permute-start(bf16[64,1024]{1,0:T(8,128)(2,1)S(1)} %pad_maximum_fusion.k0), channel_id=1, source_target_pairs={{24,0},{0,8},{8,16},{16,24},{25,1},{1,9},{9,17},{17,25},{26,2},{2,... | collective-permute-start | bytes 393224 | tf_op jit(solution)/shard_map/ppermute | solution.py:37
  29.4 3.6 %collective-permute-start.2 = (bf16[64,1024]{1,0:T(8,128)(2,1)S(1)}, bf16[64,1024]{1,0:T(8,128)(2,1)S(1)}, u32[]{:S(2)}, u32[]{:S(2)}) collective-permute-start(bf16[64,1024]{1,0:T(8,128)(2,1)S(1)} %pad_maximum_fusion.k0), channel_id=1, source_target_pairs={{16,0},{24,8},{0,16},{8,24},{17,1},{25,9},{1,17},{9,25},{18,2},{26... | collective-permute-start | bytes 393224 | tf_op jit(solution)/shard_map/ppermute | solution.py:37
  33.0 2.8 %collective-permute-done.3.k3 = bf16[64,1024]{1,0:T(8,128)(2,1)S(1)} collective-permute-done((bf16[64,1024]{1,0:T(8,128)(2,1)S(1)}, bf16[64,1024]{1,0:T(8,128)(2,1)S(1)}, u32[]{:S(2)}, u32[]{:S(2)}) %collective-permute-start.3) | collective-permute-done | bytes 131104 | tf_op jit(solution)/shard_map/ppermute | solution.py:37
  35.8 0.7 collective-permute-start.1
  36.5 0.8 collective-permute-done.2.k2
  37.3 3.4 %collective-permute-done.1.k1 = bf16[64,1024]{1,0:T(8,128)(2,1)S(1)} collective-permute-done((bf16[64,1024]{1,0:T(8,128)(2,1)S(1)}, bf16[64,1024]{1,0:T(8,128)(2,1)S(1)}, u32[]{:S(2)}, u32[]{:S(2)}) %collective-permute-start.1) | collective-permute-done | bytes 131104 | tf_op jit(solution)/shard_map/ppermute | solution.py:37
  40.7 1.1 copy-done
  41.9 3.7 %early.1 = (bf16[4,1024,1024]{2,1,0:T(8,128)(2,1)S(1)}, bf16[3,128,1024]{2,1,0:T(8,128)(2,1)S(1)}, f32[3,256,128]{2,1,0:T(8,128)S(1)}) custom-call(bf16[4,1024,1024]{2,1,0:T(8,128)(2,1)} %first.1, bf16[3,128,1024]{2,1,0:T(8,128)(2,1)S(1)} %copy-done, bf16[64,1024]{1,0:T(8,128)(2,1)S(1)} %pad_maximum_fusion.k0, ...), custom_call_target="tpu_custom_call" | custom-call | flops 201326592 | bytes 8388608 | tf_op jit(solution)/shard_map/early/pallas_call | solution.py:73
  45.5 0.0 collective-permute-done.4.refs_1_
  45.6 0.0 slice-start.1
  45.6 3.3 %dispatch.1 = (bf16[8,792,128]{2,1,0:T(8,128)(2,1)S(1)}, f32[3,256,512]{2,1,0:T(8,128)S(1)}, f32[3,2,128]{2,1,0:T(2,128)S(1)}, f32[3,2,128]{2,1,0:T(2,128)S(1)},...) custom-call(f32[3,256,128]{2,1,0:T(8,128)S(1)} %get-tuple-element.27.own_logits, ...), custom_call_target="tpu_custom_call" | custom-call | flops 1610612736 | bytes 3145728 | tf_op jit(solution)/shard_map/dispatch/pallas_call | solution.py:160
  48.9 29.4 %all_to_all.5.arrived = bf16[8,792,128]{2,1,0:T(8,128)(2,1)S(1)} all-to-all(bf16[8,792,128]{2,1,0:T(8,128)(2,1)S(1)} %get-tuple-element.30), channel_id=1, replica_groups={{0,8,16,24,68,76,84,92},{32,40,48,56,100,108,116,124},{64,72,80,88,4,12..., dimensions={0} | all-to-all | bytes 3244032 | tf_op jit(solution)/shard_map/all_to_all | solution.py:46
  78.3 0.5 merge.1
  78.8 7.8 %all_gather.3.rows = bf16[12,32,1024]{2,1,0:T(8,128)(2,1)S(1)} all-gather(bf16[3,32,1024]{2,1,0:T(8,128)(2,1)S(1)} %merge.1), channel_id=1, replica_groups=mesh['slot_0'=4,'slot_1'=4,'slot_2'=2,'dp'=4] {'dp'}, dimensions={0}, use_global_device_ids=true | all-gather | bytes 983040 | tf_op jit(solution)/shard_map/all_gather | solution.py:383
  86.6 3.5 %experts.1 = (f32[3,32,1024]{2,1,0:T(8,128)S(1)}, bf16[3,32,1024]{2,1,0:T(8,128)(2,1)S(1)}, bf16[3,32,1024]{2,1,0:T(8,128)(2,1)S(1)}, bf16[3,32,1024]{2,1,0:T(8,128)(2,1)S(1)}) custom-call(bf16[12,32,1024]{2,1,0:T(8,128)(2,1)S(1)} %all_gather.3.rows, bf16[4,1024,1024]{2,1,0:T(8,128)(2,1)S(1)} %get-tuple-element.31.first, bf16[4,1024,1024]{2,1,0:T(8,128)(2,1)S(1)} %bitcast.2), custom_call_target="tpu_custom_call" | custom-call | flops 1610612736 | bytes 16777216 | tf_op jit(solution)/shard_map/experts/pallas_call | solution.py:258
  90.0 0.4 collective-permute-start.7
  90.5 1.3 collective-permute-start.8
  91.8 0.2 collective-permute-start.9
  92.0 3.2 %collective-permute-start.11 = (f32[3,2,128]{2,1,0:T(2,128)S(1)}, f32[3,2,128]{2,1,0:T(2,128)S(1)}, u32[]{:S(2)}, u32[]{:S(2)}) collective-permute-start(f32[3,2,128]{2,1,0:T(2,128)S(1)} %get-tuple-element.37.refs_9_), channel_id=1, source_target_pairs={{32,0},{64,32},{96,64},{0,96},{33,1},{65,33},{97,65},{1,97},{34,2}... | collective-permute-start | bytes 9224 | tf_op jit(solution)/shard_map/ppermute | solution.py:37
  95.2 1.6 collective-permute-done.10.refs_5_
  96.8 0.3 collective-permute-start.12
  97.1 4.8 %collective-permute-done.12.refs_7_ = f32[3,2,128]{2,1,0:T(2,128)S(1)} collective-permute-done((f32[3,2,128]{2,1,0:T(2,128)S(1)}, f32[3,2,128]{2,1,0:T(2,128)S(1)}, u32[]{:S(2)}, u32[]{:S(2)}) %collective-permute-start.12) | collective-permute-done | bytes 3104 | tf_op jit(solution)/shard_map/ppermute | solution.py:37
  101.9 0.1 total.1.refs_0_
  102.0 4.3 %collective-permute-start.13 = (bf16[3,32,1024]{2,1,0:T(8,128)(2,1)S(1)}, bf16[3,32,1024]{2,1,0:T(8,128)(2,1)S(1)}, u32[]{:S(2)}, u32[]{:S(2)}) collective-permute-start(bf16[3,32,1024]{2,1,0:T(8,128)(2,1)S(1)} %total.1.refs_0_), channel_id=1, source_target_pairs={{0,68},{4,64},{8,76},{12,72},{16,84},{20,80},{24,92},{28,88},{32,1... | collective-permute-start | bytes 589832 | tf_op jit(solution)/shard_map/ppermute | solution.py:389
  106.3 6.4 %collective-permute-done.13.refs_1_ = bf16[3,32,1024]{2,1,0:T(8,128)(2,1)S(1)} collective-permute-done((bf16[3,32,1024]{2,1,0:T(8,128)(2,1)S(1)}, bf16[3,32,1024]{2,1,0:T(8,128)(2,1)S(1)}, u32[]{:S(2)}, u32[]{:S(2)}) %collective-permute-start.13) | collective-permute-done | bytes 196640 | tf_op jit(solution)/shard_map/ppermute | solution.py:389
  112.7 0.6 collective-permute-start.17
  113.2 0.5 collective-permute-start.19
  113.7 3.6 %collective-permute-start.16 = (bf16[3,32,1024]{2,1,0:T(8,128)(2,1)S(1)}, bf16[3,32,1024]{2,1,0:T(8,128)(2,1)S(1)}, u32[]{:S(2)}, u32[]{:S(2)}) collective-permute-start(bf16[3,32,1024]{2,1,0:T(8,128)(2,1)S(1)} %total.1.refs_0_), channel_id=1, source_target_pairs={{16,0},{24,8},{0,16},{8,24},{17,1},{25,9},{1,17},{9,25},{18,2},{26... | collective-permute-start | bytes 589832 | tf_op jit(solution)/shard_map/ppermute | solution.py:37
  117.4 0.6 collective-permute-start.14
  117.9 0.0 collective-permute-start.15
  118.0 4.0 %collective-permute-done.17.refs_7_ = bf16[3,32,1024]{2,1,0:T(8,128)(2,1)S(1)} collective-permute-done((bf16[3,32,1024]{2,1,0:T(8,128)(2,1)S(1)}, bf16[3,32,1024]{2,1,0:T(8,128)(2,1)S(1)}, u32[]{:S(2)}, u32[]{:S(2)}) %collective-permute-start.17) | collective-permute-done | bytes 196640 | tf_op jit(solution)/shard_map/ppermute | solution.py:37
  121.9 8.2 %collective-permute-done.19.refs_6_ = bf16[3,32,1024]{2,1,0:T(8,128)(2,1)S(1)} collective-permute-done((bf16[3,32,1024]{2,1,0:T(8,128)(2,1)S(1)}, bf16[3,32,1024]{2,1,0:T(8,128)(2,1)S(1)}, u32[]{:S(2)}, u32[]{:S(2)}) %collective-permute-start.19) | collective-permute-done | bytes 196640 | tf_op jit(solution)/shard_map/ppermute | solution.py:37
  130.1 2.3 %collective-permute-done.18.refs_5_ = bf16[3,32,1024]{2,1,0:T(8,128)(2,1)S(1)} collective-permute-done((bf16[3,32,1024]{2,1,0:T(8,128)(2,1)S(1)}, bf16[3,32,1024]{2,1,0:T(8,128)(2,1)S(1)}, u32[]{:S(2)}, u32[]{:S(2)}) %collective-permute-start.18) | collective-permute-done | bytes 196640 | tf_op jit(solution)/shard_map/ppermute | solution.py:37
  132.4 1.2 combine.3
  133.6 0.1 collective-permute-start.20
  133.7 3.2 %collective-permute-start.21 = (bf16[3,128,1024]{2,1,0:T(8,128)(2,1)S(1)}, bf16[3,128,1024]{2,1,0:T(8,128)(2,1)S(1)}, u32[]{:S(2)}, u32[]{:S(2)}) collective-permute-start(bf16[3,128,1024]{2,1,0:T(8,128)(2,1)S(1)} %get-tuple-element.44), channel_id=1, source_target_pairs={{32,0},{64,32},{96,64},{0,96},{33,1},{65,33},{97,65},{1,97},{34,2}... | collective-permute-start | bytes 2359304 | tf_op jit(solution)/shard_map/ppermute | solution.py:37
  136.9 0.9 collective-permute-start.22
  137.8 0.8 combine.2.refs_0_
  138.7 13.9 %collective-permute-done.20.refs_1_ = bf16[3,128,1024]{2,1,0:T(8,128)(2,1)S(1)} collective-permute-done((bf16[3,128,1024]{2,1,0:T(8,128)(2,1)S(1)}, bf16[3,128,1024]{2,1,0:T(8,128)(2,1)S(1)}, u32[]{:S(2)}, u32[]{:S(2)}) %collective-permute-start.20) | collective-permute-done | bytes 786464 | tf_op jit(solution)/shard_map/ppermute | solution.py:37
  152.5 0.0 collective-permute-done.21.refs_2_
  152.6 2.9 %collective-permute-done.22.refs_3_ = bf16[3,128,1024]{2,1,0:T(8,128)(2,1)S(1)} collective-permute-done((bf16[3,128,1024]{2,1,0:T(8,128)(2,1)S(1)}, bf16[3,128,1024]{2,1,0:T(8,128)(2,1)S(1)}, u32[]{:S(2)}, u32[]{:S(2)}) %collective-permute-start.22) | collective-permute-done | bytes 786464 | tf_op jit(solution)/shard_map/ppermute | solution.py:37
  155.5 1.6 %finish.1 = bf16[3,128,1024]{2,1,0:T(8,128)(2,1)} custom-call(f32[3,128,1024]{2,1,0:T(8,128)S(1)} %combine.2.refs_0_, bf16[3,128,1024]{2,1,0:T(8,128)(2,1)S(1)} %collective-permute-done.20.refs_1_, bf16[3,128,1024]{2,1,0:T(8,128)(2,1)S(1)} %collective-permute-done.21.refs_2_, bf16[3,128,1024]{2,1,0:T(8,128)(2,1)S(1)} %collective-permute-done.22.refs_3_, ...), custom_call_target="tpu_custom_call" | custom-call | flops 3145728 | bytes 4718592 | tf_op jit(solution)/shard_map/finish/pallas_call | solution.py:356
  (16 shorter events, 0.0 us)
Async XLA Ops:
  0.0 45.5 %collective-permute-start.4 = (bf16[3,128,1024]{2,1,0:T(8,128)(2,1)}, bf16[3,128,1024]{2,1,0:T(8,128)(2,1)S(1)}, u32[]{:S(2)}, u32[]{:S(2)}) collective-permute-start(bf16[3,128,1024]{2,1,0:T(8,128)(2,1)} %own.1), channel_id=1, source_target_pairs={{32,0},{64,32},{96,64},{0,96},{33,1},{65,33},{97,65},{1,97},{34,2}... | collective-permute-start | bytes 2359304 | tf_op jit(solution)/shard_map/ppermute | solution.py:37
  2.9 42.7 %collective-permute-start.6 = (bf16[3,128,1024]{2,1,0:T(8,128)(2,1)}, bf16[3,128,1024]{2,1,0:T(8,128)(2,1)S(1)}, u32[]{:S(2)}, u32[]{:S(2)}) collective-permute-start(bf16[3,128,1024]{2,1,0:T(8,128)(2,1)} %own.1), channel_id=1, source_target_pairs={{4,0},{0,4},{5,1},{1,5},{6,2},{2,6},{7,3},{3,7},{12,8},{8,12},{13,... | collective-permute-start | bytes 2359304 | tf_op jit(solution)/shard_map/ppermute | solution.py:37
  6.1 39.5 %collective-permute-start.5 = (bf16[3,128,1024]{2,1,0:T(8,128)(2,1)}, bf16[3,128,1024]{2,1,0:T(8,128)(2,1)S(1)}, u32[]{:S(2)}, u32[]{:S(2)}) collective-permute-start(bf16[3,128,1024]{2,1,0:T(8,128)(2,1)} %own.1), channel_id=1, source_target_pairs={{96,0},{0,32},{32,64},{64,96},{97,1},{1,33},{33,65},{65,97},{98,2}... | collective-permute-start | bytes 2359304 | tf_op jit(solution)/shard_map/ppermute | solution.py:37
  6.1 20.5 %collective-permute-start = (bf16[32,1024]{1,0:T(8,128)(2,1)}, bf16[32,1024]{1,0:T(8,128)(2,1)S(1)}, u32[]{:S(2)}, u32[]{:S(2)}) collective-permute-start(bf16[32,1024]{1,0:T(8,128)(2,1)} %bitcast.3), channel_id=1, source_target_pairs={{0,68},{4,64},{8,76},{12,72},{16,84},{20,80},{24,92},{28,88},{32,1... | collective-permute-start | bytes 196616 | tf_op jit(solution)/shard_map/ppermute | solution.py:375
  27.4 8.4 %collective-permute-start.3 = (bf16[64,1024]{1,0:T(8,128)(2,1)S(1)}, bf16[64,1024]{1,0:T(8,128)(2,1)S(1)}, u32[]{:S(2)}, u32[]{:S(2)}) collective-permute-start(bf16[64,1024]{1,0:T(8,128)(2,1)S(1)} %pad_maximum_fusion.k0), channel_id=1, source_target_pairs={{24,0},{0,8},{8,16},{16,24},{25,1},{1,9},{9,17},{17,25},{26,2},{2,... | collective-permute-start | bytes 393224 | tf_op jit(solution)/shard_map/ppermute | solution.py:37
  29.4 7.9 %collective-permute-start.2 = (bf16[64,1024]{1,0:T(8,128)(2,1)S(1)}, bf16[64,1024]{1,0:T(8,128)(2,1)S(1)}, u32[]{:S(2)}, u32[]{:S(2)}) collective-permute-start(bf16[64,1024]{1,0:T(8,128)(2,1)S(1)} %pad_maximum_fusion.k0), channel_id=1, source_target_pairs={{16,0},{24,8},{0,16},{8,24},{17,1},{25,9},{1,17},{9,25},{18,2},{26... | collective-permute-start | bytes 393224 | tf_op jit(solution)/shard_map/ppermute | solution.py:37
  35.8 5.0 %collective-permute-start.1 = (bf16[64,1024]{1,0:T(8,128)(2,1)S(1)}, bf16[64,1024]{1,0:T(8,128)(2,1)S(1)}, u32[]{:S(2)}, u32[]{:S(2)}) collective-permute-start(bf16[64,1024]{1,0:T(8,128)(2,1)S(1)} %pad_maximum_fusion.k0), channel_id=1, source_target_pairs={{8,0},{16,8},{24,16},{0,24},{9,1},{17,9},{25,17},{1,25},{10,2},{18... | collective-permute-start | bytes 393224 | tf_op jit(solution)/shard_map/ppermute | solution.py:37
  40.7 1.1 copy-start
  41.9 44.7 %slice-start = ((s8[8388608]{0:T(1024)(128)(4,1)}), s8[4194304]{0:T(1024)(128)(4,1)S(1)}, s32[]{:S(2)}) async-start(s8[8388608]{0:T(1024)(128)(4,1)} %bitcast.1), calls=%async_computation.1 | async-start | bytes 8388608
  45.6 41.0 %slice-start.1 = ((s8[8388608]{0:T(1024)(128)(4,1)}), s8[4194304]{0:T(1024)(128)(4,1)S(1)}, s32[]{:S(2)}) async-start(s8[8388608]{0:T(1024)(128)(4,1)} %bitcast.1), calls=%async_computation.2 | async-start | bytes 8388608
  90.0 11.9 %collective-permute-start.7 = (bf16[3,32,1024]{2,1,0:T(8,128)(2,1)S(1)}, bf16[3,32,1024]{2,1,0:T(8,128)(2,1)S(1)}, u32[]{:S(2)}, u32[]{:S(2)}) collective-permute-start(bf16[3,32,1024]{2,1,0:T(8,128)(2,1)S(1)} %get-tuple-element.33), channel_id=1, source_target_pairs={{0,1},{1,0},{2,3},{3,2},{4,5},{5,4},{6,7},{7,6},{8,9},{9,8},{10,11... | collective-permute-start | bytes 589832 | tf_op jit(solution)/shard_map/ppermute | solution.py:42
  90.5 11.4 %collective-permute-start.8 = (bf16[3,32,1024]{2,1,0:T(8,128)(2,1)S(1)}, bf16[3,32,1024]{2,1,0:T(8,128)(2,1)S(1)}, u32[]{:S(2)}, u32[]{:S(2)}) collective-permute-start(bf16[3,32,1024]{2,1,0:T(8,128)(2,1)S(1)} %get-tuple-element.34), channel_id=1, source_target_pairs={{0,2},{1,3},{2,0},{3,1},{4,6},{5,7},{6,4},{7,5},{8,10},{9,11},{10,... | collective-permute-start | bytes 589832 | tf_op jit(solution)/shard_map/ppermute | solution.py:42
  91.8 10.1 %collective-permute-start.9 = (bf16[3,32,1024]{2,1,0:T(8,128)(2,1)S(1)}, bf16[3,32,1024]{2,1,0:T(8,128)(2,1)S(1)}, u32[]{:S(2)}, u32[]{:S(2)}) collective-permute-start(bf16[3,32,1024]{2,1,0:T(8,128)(2,1)S(1)} %get-tuple-element.35), channel_id=1, source_target_pairs={{0,3},{1,2},{2,1},{3,0},{4,7},{5,6},{6,5},{7,4},{8,11},{9,10},{10,... | collective-permute-start | bytes 589832 | tf_op jit(solution)/shard_map/ppermute | solution.py:42
  92.0 4.8 %collective-permute-start.10 = (f32[3,2,128]{2,1,0:T(2,128)S(1)}, f32[3,2,128]{2,1,0:T(2,128)S(1)}, u32[]{:S(2)}, u32[]{:S(2)}) collective-permute-start(f32[3,2,128]{2,1,0:T(2,128)S(1)} %get-tuple-element.36.refs_8_), channel_id=1, source_target_pairs={{96,0},{0,32},{32,64},{64,96},{97,1},{1,33},{33,65},{65,97},{98,2}... | collective-permute-start | bytes 9224 | tf_op jit(solution)/shard_map/ppermute | solution.py:37
  92.0 5.1 %collective-permute-start.11 = (f32[3,2,128]{2,1,0:T(2,128)S(1)}, f32[3,2,128]{2,1,0:T(2,128)S(1)}, u32[]{:S(2)}, u32[]{:S(2)}) collective-permute-start(f32[3,2,128]{2,1,0:T(2,128)S(1)} %get-tuple-element.37.refs_9_), channel_id=1, source_target_pairs={{32,0},{64,32},{96,64},{0,96},{33,1},{65,33},{97,65},{1,97},{34,2}... | collective-permute-start | bytes 9224 | tf_op jit(solution)/shard_map/ppermute | solution.py:37
  96.8 5.1 %collective-permute-start.12 = (f32[3,2,128]{2,1,0:T(2,128)S(1)}, f32[3,2,128]{2,1,0:T(2,128)S(1)}, u32[]{:S(2)}, u32[]{:S(2)}) collective-permute-start(f32[3,2,128]{2,1,0:T(2,128)S(1)} %get-tuple-element.38.refs_10_), channel_id=1, source_target_pairs={{4,0},{0,4},{5,1},{1,5},{6,2},{2,6},{7,3},{3,7},{12,8},{8,12},{13,... | collective-permute-start | bytes 9224 | tf_op jit(solution)/shard_map/ppermute | solution.py:37
  102.0 10.7 %collective-permute-start.13 = (bf16[3,32,1024]{2,1,0:T(8,128)(2,1)S(1)}, bf16[3,32,1024]{2,1,0:T(8,128)(2,1)S(1)}, u32[]{:S(2)}, u32[]{:S(2)}) collective-permute-start(bf16[3,32,1024]{2,1,0:T(8,128)(2,1)S(1)} %total.1.refs_0_), channel_id=1, source_target_pairs={{0,68},{4,64},{8,76},{12,72},{16,84},{20,80},{24,92},{28,88},{32,1... | collective-permute-start | bytes 589832 | tf_op jit(solution)/shard_map/ppermute | solution.py:389
  112.7 9.2 %collective-permute-start.17 = (bf16[3,32,1024]{2,1,0:T(8,128)(2,1)S(1)}, bf16[3,32,1024]{2,1,0:T(8,128)(2,1)S(1)}, u32[]{:S(2)}, u32[]{:S(2)}) collective-permute-start(bf16[3,32,1024]{2,1,0:T(8,128)(2,1)S(1)} %collective-permute-done.13.refs_1_), channel_id=1, source_target_pairs={{24,0},{0,8},{8,16},{16,24},{25,1},{1,9},{9,17},{17,25},{26,2},{2,... | collective-permute-start | bytes 589832 | tf_op jit(solution)/shard_map/ppermute | solution.py:37
  113.2 16.8 %collective-permute-start.19 = (bf16[3,32,1024]{2,1,0:T(8,128)(2,1)S(1)}, bf16[3,32,1024]{2,1,0:T(8,128)(2,1)S(1)}, u32[]{:S(2)}, u32[]{:S(2)}) collective-permute-start(bf16[3,32,1024]{2,1,0:T(8,128)(2,1)S(1)} %total.1.refs_0_), channel_id=1, source_target_pairs={{24,0},{0,8},{8,16},{16,24},{25,1},{1,9},{9,17},{17,25},{26,2},{2,... | collective-permute-start | bytes 589832 | tf_op jit(solution)/shard_map/ppermute | solution.py:37
  113.7 16.4 %collective-permute-start.16 = (bf16[3,32,1024]{2,1,0:T(8,128)(2,1)S(1)}, bf16[3,32,1024]{2,1,0:T(8,128)(2,1)S(1)}, u32[]{:S(2)}, u32[]{:S(2)}) collective-permute-start(bf16[3,32,1024]{2,1,0:T(8,128)(2,1)S(1)} %total.1.refs_0_), channel_id=1, source_target_pairs={{16,0},{24,8},{0,16},{8,24},{17,1},{25,9},{1,17},{9,25},{18,2},{26... | collective-permute-start | bytes 589832 | tf_op jit(solution)/shard_map/ppermute | solution.py:37
  117.4 12.7 %collective-permute-start.14 = (bf16[3,32,1024]{2,1,0:T(8,128)(2,1)S(1)}, bf16[3,32,1024]{2,1,0:T(8,128)(2,1)S(1)}, u32[]{:S(2)}, u32[]{:S(2)}) collective-permute-start(bf16[3,32,1024]{2,1,0:T(8,128)(2,1)S(1)} %total.1.refs_0_), channel_id=1, source_target_pairs={{8,0},{16,8},{24,16},{0,24},{9,1},{17,9},{25,17},{1,25},{10,2},{18... | collective-permute-start | bytes 589832 | tf_op jit(solution)/shard_map/ppermute | solution.py:37
  117.9 12.2 %collective-permute-start.15 = (bf16[3,32,1024]{2,1,0:T(8,128)(2,1)S(1)}, bf16[3,32,1024]{2,1,0:T(8,128)(2,1)S(1)}, u32[]{:S(2)}, u32[]{:S(2)}) collective-permute-start(bf16[3,32,1024]{2,1,0:T(8,128)(2,1)S(1)} %collective-permute-done.13.refs_1_), channel_id=1, source_target_pairs={{8,0},{16,8},{24,16},{0,24},{9,1},{17,9},{25,17},{1,25},{10,2},{18... | collective-permute-start | bytes 589832 | tf_op jit(solution)/shard_map/ppermute | solution.py:37
  121.9 10.4 %collective-permute-start.18 = (bf16[3,32,1024]{2,1,0:T(8,128)(2,1)S(1)}, bf16[3,32,1024]{2,1,0:T(8,128)(2,1)S(1)}, u32[]{:S(2)}, u32[]{:S(2)}) collective-permute-start(bf16[3,32,1024]{2,1,0:T(8,128)(2,1)S(1)} %collective-permute-done.17.refs_7_), channel_id=1, source_target_pairs={{24,0},{0,8},{8,16},{16,24},{25,1},{1,9},{9,17},{17,25},{26,2},{2,... | collective-permute-start | bytes 589832 | tf_op jit(solution)/shard_map/ppermute | solution.py:37
  133.6 18.9 %collective-permute-start.20 = (bf16[3,128,1024]{2,1,0:T(8,128)(2,1)S(1)}, bf16[3,128,1024]{2,1,0:T(8,128)(2,1)S(1)}, u32[]{:S(2)}, u32[]{:S(2)}) collective-permute-start(bf16[3,128,1024]{2,1,0:T(8,128)(2,1)S(1)} %get-tuple-element.43), channel_id=1, source_target_pairs={{96,0},{0,32},{32,64},{64,96},{97,1},{1,33},{33,65},{65,97},{98,2}... | collective-permute-start | bytes 2359304 | tf_op jit(solution)/shard_map/ppermute | solution.py:37
  133.7 18.9 %collective-permute-start.21 = (bf16[3,128,1024]{2,1,0:T(8,128)(2,1)S(1)}, bf16[3,128,1024]{2,1,0:T(8,128)(2,1)S(1)}, u32[]{:S(2)}, u32[]{:S(2)}) collective-permute-start(bf16[3,128,1024]{2,1,0:T(8,128)(2,1)S(1)} %get-tuple-element.44), channel_id=1, source_target_pairs={{32,0},{64,32},{96,64},{0,96},{33,1},{65,33},{97,65},{1,97},{34,2}... | collective-permute-start | bytes 2359304 | tf_op jit(solution)/shard_map/ppermute | solution.py:37
  136.9 18.6 %collective-permute-start.22 = (bf16[3,128,1024]{2,1,0:T(8,128)(2,1)S(1)}, bf16[3,128,1024]{2,1,0:T(8,128)(2,1)S(1)}, u32[]{:S(2)}, u32[]{:S(2)}) collective-permute-start(bf16[3,128,1024]{2,1,0:T(8,128)(2,1)S(1)} %get-tuple-element.45), channel_id=1, source_target_pairs={{4,0},{0,4},{5,1},{1,5},{6,2},{2,6},{7,3},{3,7},{12,8},{8,12},{13,... | collective-permute-start | bytes 2359304 | tf_op jit(solution)/shard_map/ppermute | solution.py:37
